TPU v7x, 256 devices: a whole 4x4x8 slice. The times are simulated.
256 devices in a mesh: dev: 64 (over z, y, core), rep: 4 (over x).
Axes of the slice: x: 4, y: 4, z: 8, core: 2. Of those that a mesh axis runs over, the one named last changes fastest.
Arguments:
- features: bfloat16 [262144, 256], P(('dev', 'rep')), may hold values from -6 to 6
- history: bfloat16 [262144, 256], P(('dev', 'rep')), may hold values from -6 to 6
- new_owner: int32 [256, 64], P(('dev', 'rep')), may hold values from 0 to 63, as said below
- pull_rows: int32 [262144], P(('dev', 'rep')), may hold values from 0 to 1023
- occupancy: int32 [2048, 16], P(('dev', 'rep')), may hold values from 0 to 1, as said below
- adj_local: bfloat16 [262144, 1024], P(('dev', 'rep')), may hold values from -0.125 to 0.125
- adj_boundary: bfloat16 [262144, 1024], P(('dev', 'rep')), may hold values from -0.125 to 0.125
- w_first: bfloat16 [256, 256], replicated, may hold values from -0.375 to 0.375
- bias_first: float32 [256], replicated, may hold values from -3 to 3
- w_second: bfloat16 [256, 256], replicated, may hold values from -0.375 to 0.375
- cotangent: bfloat16 [262144, 256], P(('dev', 'rep')), may hold values from -24 to 24
Outputs:
- hidden: bfloat16 [262144, 256], P(('dev', 'rep'))
- output: bfloat16 [262144, 256], P(('dev', 'rep'))
- w_second_grad: float32 [256, 256], replicated
Inputs may be any that keep to these rules, and one draw needn't show every extreme that they name: Each row of new_owner is a permutation of 0 to 63. `occupancy`: tile flags of 0 or 1.
All inputs are finite; a program needn't handle non-finite values.
Results may differ from a plain program's by a relative error of at most 0.0061.
Values may be sent and summed in bfloat16 or wider, within the bound.
No kernel may reach another device: no remote copies, remote signals or barrier semaphores. Data moves between devices by JAX's collectives and lax.ppermute only.
A program may use at most 64 MiB of HBM per device.

v0:
```python
import jax
import jax.numpy as jnp
from jax import lax
from jax.sharding import Mesh
from jax.sharding import PartitionSpec as P

DEV = ("dev_0", "dev_1", "dev_2")
DEV_REP = ("dev_0", "dev_1", "dev_2", "rep")


def in_one_piece(arrays, axis, split_dim, concat_dim, along):
    ends, at = ([], 0)
    for a in arrays[:-1]:
        at += a.shape[along]
        ends.append(at)
    both = jnp.concatenate(arrays, axis=along)
    return tuple(
        jnp.split(
            lax.all_to_all(both, axis, split_axis=split_dim, concat_axis=concat_dim, tiled=True),
            ends,
            axis=along,
        )
    )


def padded_to(lines, count):
    spare = -len(lines) % count
    return jnp.pad(lines, [(0, spare)] + [(0, 0)] * (lines.ndim - 1))


def copy_for_each(array, axis):
    copies = jnp.broadcast_to(array, (lax.axis_size(axis), *array.shape))
    return lax.all_to_all(copies, axis, split_axis=0, concat_axis=0, tiled=True)


def in_order(tiles, dim):
    dims = list(tiles.shape[1:])
    dims[dim] *= tiles.shape[0]
    return jnp.moveaxis(tiles, 0, dim).reshape(dims)


def whole_of(array, axes, dim):
    far, near = axes
    leading = copy_for_each(array, far)
    tiles = jnp.swapaxes(copy_for_each(leading, near), 0, 1)
    return in_order(tiles.reshape(-1, *array.shape), dim)


def split_up(array, dim, count):
    dims = array.shape
    tiles = array.reshape(*dims[:dim], count, dims[dim] // count, *dims[dim + 1 :])
    return jnp.moveaxis(tiles, dim, 0)


def summed_on_arrival(array, axis, dim):
    tiles = split_up(array, dim, lax.axis_size(axis))
    arrived = lax.all_to_all(tiles, axis, split_axis=0, concat_axis=0, tiled=True)
    return arrived.sum(axis=0)


def summed_rows(array, axes, dim):
    far, near = axes
    own = summed_on_arrival(split_up(array, dim, lax.axis_size(far)), near, dim + 1)
    return jnp.sum(lax.all_to_all(own, far, 0, 0, tiled=True), axis=0)


def nested_sum(array, axes):
    lines = array.reshape(-1, array.shape[-1])
    padded = padded_to(lines, lax.axis_size(axes[0]) * lax.axis_size(axes[1]))
    whole = whole_of(summed_rows(padded, axes, 0), axes, 0)
    return lax.slice_in_dim(whole, 0, len(lines)).reshape(array.shape)


def expand(occupied):
    return jnp.repeat(jnp.repeat(occupied, 128, axis=0), 128, axis=1).astype(jnp.bfloat16)


def dense_terms(owned, remote, adj_local, adj_boundary, occupancy):
    height = owned.shape[0]
    full_mask = expand(occupancy)
    local_tile = adj_local * full_mask[:, :height]
    edge_tile = adj_boundary * full_mask[:, height:]
    summed = jnp.dot(local_tile, owned, preferred_element_type=jnp.float32)
    summed = summed + jnp.dot(edge_tile, remote, preferred_element_type=jnp.float32)
    partial_value = lax.dot_general(
        edge_tile, owned, (((0,), (0,)), ((), ())), preferred_element_type=jnp.float32
    )
    return (summed, partial_value)


def body(
    features,
    history,
    new_owner,
    pull_rows,
    occupancy,
    adj_local,
    adj_boundary,
    w_first,
    bias_first,
    w_second,
    cotangent,
):
    peer_count = lax.axis_size(DEV)
    height, breadth = features.shape
    cluster = height // peer_count
    pulled = pull_rows.shape[0]
    per_peer = pulled // peer_count
    indices = jnp.arange(peer_count, dtype=jnp.int32)
    matches = (new_owner[0][:, None] == indices[None, :]).astype(jnp.int32)
    inverse = jnp.sum(matches * indices[:, None], axis=0)

    def arrange(values):
        return values.reshape(peer_count, cluster, breadth)[inverse]

    requests = lax.all_to_all(
        pull_rows.reshape(peer_count, per_peer), DEV, split_axis=0, concat_axis=0, tiled=True
    ).reshape(pulled)

    def fetch_rows(values):
        return values[requests].reshape(peer_count, per_peer, breadth)

    selector = (requests[None, :] == jnp.arange(height, dtype=jnp.int32)[:, None]).astype(
        jnp.bfloat16
    )

    def collect(received):
        return jnp.dot(
            selector, received.reshape(pulled, breadth), preferred_element_type=jnp.float32
        )

    def layer_terms(owned, remote):
        return dense_terms(owned, remote, adj_local, adj_boundary, occupancy)

    moved_x, moved_h = in_one_piece((arrange(features), arrange(history)), DEV, 0, 0, 1)
    own_x = moved_x.reshape(height, breadth)
    own_h = moved_h.reshape(height, breadth)
    far_x, far_h = in_one_piece((fetch_rows(own_x), fetch_rows(own_h)), DEV, 0, 0, 1)
    summed_one, partial_one = layer_terms(own_x, far_x.reshape(pulled, breadth))
    pushed_one = lax.all_to_all(
        partial_one.astype(jnp.bfloat16).reshape(peer_count, per_peer, breadth),
        DEV,
        split_axis=0,
        concat_axis=0,
        tiled=True,
    )
    far_h = far_h.reshape(pulled, breadth)
    aggregate_one = (summed_one + collect(pushed_one)).astype(jnp.bfloat16)
    hidden = jnp.maximum(
        jnp.dot(aggregate_one, w_first, preferred_element_type=jnp.float32) + bias_first, 0.0
    ).astype(jnp.bfloat16)
    summed_two, partial_two = layer_terms(hidden, far_h)
    pushed_two = lax.all_to_all(
        partial_two.astype(jnp.bfloat16).reshape(peer_count, per_peer, breadth),
        DEV,
        split_axis=0,
        concat_axis=0,
        tiled=True,
    )
    aggregate_two = (summed_two + collect(pushed_two)).astype(jnp.bfloat16)
    output = jnp.dot(aggregate_two, w_second, preferred_element_type=jnp.float32).astype(
        jnp.bfloat16
    )
    local_grad = lax.dot_general(
        aggregate_two, cotangent, (((0,), (0,)), ((), ())), preferred_element_type=jnp.float32
    )
    gradient = nested_sum(local_grad, (("dev_0", "dev_1"), ("dev_2", "rep")))
    return (hidden, output, gradient)


def solution(mesh):
    finer = Mesh(
        mesh.devices.reshape(8, 4, 2, mesh.shape["rep"]), ("dev_0", "dev_1", "dev_2", "rep")
    )
    return jax.shard_map(
        body,
        mesh=finer,
        in_specs=(
            P(DEV_REP, None),
            P(DEV_REP, None),
            P(DEV_REP, None),
            P(DEV_REP),
            P(DEV_REP, None),
            P(DEV_REP, None),
            P(DEV_REP, None),
            P(),
            P(),
            P(),
            P(DEV_REP, None),
        ),
        out_specs=(P(DEV_REP, None), P(DEV_REP, None), P()),
        check_vma=False,
    )
```

profile of v0, /device:TPU:1, one launch (start us, length us, event | category | flops | bytes accessed | tf_op | source)
XLA Modules:
  0.0 208.1 jit_solution(64594992855767647)
XLA Ops:
  0.6 0.0 copy-start
  0.6 1.4 all_to_all.33
  2.1 13.1 %all-to-all-start.1 = ((s32[64,1,16]{2,1,0:T(1,128)}), s32[64,1,16]{2,1,0:T(1,128)S(1)}, u32[]{:S(2)}, u32[]{:S(2)}) async-start(s32[64,1,16]{2,1,0:T(1,128)} %bitcast.7), calls=%async_computation.1 | async-start | bytes 65536 | tf_op jit(solution)/shard_map/all_to_all | solution.py:116
  15.2 0.7 select_reduce_fusion
  16.0 0.0 copy-done
  16.0 0.6 gather_fusion.1
  16.6 1.6 gather_fusion
  18.3 1.1 pad_maximum_fusion
  19.4 5.2 %all-to-all-done.1 = s32[64,1,16]{2,1,0:T(1,128)S(1)} async-done(((s32[64,1,16]{2,1,0:T(1,128)}), s32[64,1,16]{2,1,0:T(1,128)S(1)}, u32[]{:S(2)}, u32[]{:S(2)}) %all-to-all-start.1) | async-done | bytes 4128 | tf_op jit(solution)/shard_map/all_to_all | solution.py:116
  24.6 5.1 %all-to-all-start = ((bf16[64,32,256]{2,1,0:T(8,128)(2,1)}), bf16[64,32,256]{2,1,0:T(8,128)(2,1)S(1)}, u32[]{:S(2)}, u32[]{:S(2)}) async-start(bf16[64,32,256]{2,1,0:T(8,128)(2,1)} %pad_maximum_fusion), calls=%async_computation | async-start | bytes 2097152 | tf_op jit(solution)/shard_map/all_to_all | solution.py:19
  29.7 0.5 broadcast.76
  30.2 0.7 reduce.7
  30.9 0.1 reshape.109
  31.1 26.8 %all-to-all-done = bf16[64,32,256]{2,1,0:T(8,128)(2,1)S(1)} async-done(((bf16[64,32,256]{2,1,0:T(8,128)(2,1)}), bf16[64,32,256]{2,1,0:T(8,128)(2,1)S(1)}, u32[]{:S(2)}, u32[]{:S(2)}) %all-to-all-start) | async-done | bytes 1048608 | tf_op jit(solution)/shard_map/all_to_all | solution.py:19
  57.9 0.1 fusion.14
  57.9 3.9 %gather_fusion.3 = bf16[1024,256]{1,0:T(8,128)(2,1)S(1)} fusion(bf16[1024,256]{1,0:T(8,128)(2,1)S(1)} %bitcast.59, s32[1024]{0:T(1024)S(1)} %broadcast_clamp_fusion), kind=kCustom, calls=%fused_computation.3 | custom fusion | bytes 1052672 | tf_op jit(solution)/shard_map/gather | solution.py:121
  61.9 3.9 %gather_fusion.2 = bf16[1024,256]{1,0:T(8,128)(2,1)S(1)} fusion(bf16[1024,256]{1,0:T(8,128)(2,1)S(1)} %bitcast.56, s32[1024]{0:T(1024)S(1)} %broadcast_clamp_fusion), kind=kCustom, calls=%fused_computation.2 | custom fusion | bytes 1052672 | tf_op jit(solution)/shard_map/gather | solution.py:121
  65.8 0.0 copy-start.5
  65.9 1.2 pad_maximum_fusion.1
  67.0 6.5 %all-to-all-start.2 = ((bf16[64,32,256]{2,1,0:T(8,128)(2,1)}), bf16[64,32,256]{2,1,0:T(8,128)(2,1)}, u32[]{:S(2)}, u32[]{:S(2)}) async-start(bf16[64,32,256]{2,1,0:T(8,128)(2,1)} %pad_maximum_fusion.1), calls=%async_computation.2 | async-start | bytes 2097152 | tf_op jit(solution)/shard_map/all_to_all | solution.py:19
  73.5 0.0 copy-done.5
  73.6 4.5 %broadcast_in_dim.9 = bf16[1024,16,128]{2,1,0:T(8,128)(2,1)S(1)} broadcast(bf16[1024,16]{1,0:T(8,128)(2,1)S(1)} %bitcast.68), dimensions={0,1} | broadcast | bytes 4227072 | tf_op jit(solution)/shard_map/broadcast_in_dim | solution.py:75
  78.0 0.0 copy-start.2
  78.0 2.2 %copy.28 = bf16[128,8,16,128]{3,1,2,0:T(8,128)(2,1)S(1)} copy(bf16[128,8,16,128]{3,2,1,0:T(8,128)(2,1)S(1)} %bitcast.60) | data formatting | bytes 8388608
  80.2 0.0 copy-start.1
  80.2 0.0 copy-done.2
  80.2 0.2 slice_multiply_fusion
  80.4 1.7 copy-done.1
  82.1 1.6 convolution_convert_fusion.2
  83.7 17.9 %all-to-all-done.2 = bf16[64,32,256]{2,1,0:T(8,128)(2,1)} async-done(((bf16[64,32,256]{2,1,0:T(8,128)(2,1)}), bf16[64,32,256]{2,1,0:T(8,128)(2,1)}, u32[]{:S(2)}, u32[]{:S(2)}) %all-to-all-start.2) | async-done | bytes 1048608 | tf_op jit(solution)/shard_map/all_to_all | solution.py:19
  101.6 6.5 %all-to-all-start.3 = ((bf16[64,16,256]{2,1,0:T(8,128)(2,1)}), bf16[64,16,256]{2,1,0:T(8,128)(2,1)}, u32[]{:S(2)}, u32[]{:S(2)}) async-start(bf16[64,16,256]{2,1,0:T(8,128)(2,1)} %bitcast.70), calls=%async_computation.3 | async-start | bytes 1048576 | tf_op jit(solution)/shard_map/all_to_all | solution.py:140
  108.0 0.1 eq.34
  108.1 2.9 %fusion.11 = f32[1024,256]{1,0:T(8,128)S(1)} fusion(bf16[1024,256]{1,0:T(8,128)(2,1)S(1)} %bitcast.58, bf16[1024,1024]{1,0:T(8,128)(2,1)} %param.16, bf16[1024,2048]{1,0:T(8,128)(2,1)} %bitcast.62), kind=kOutput, calls=%fused_computation.28 | convolution fusion | flops 537919488 | bytes 5767168 | tf_op jit(solution)/shard_map/dot_general | solution.py:83
  111.1 1.3 fusion.13
  112.3 0.0 copy-start.6
  112.4 0.0 copy-start.7
  112.4 1.7 convolution_add_fusion.2
  114.1 11.6 %all-to-all-done.3 = bf16[64,16,256]{2,1,0:T(8,128)(2,1)} async-done(((bf16[64,16,256]{2,1,0:T(8,128)(2,1)}), bf16[64,16,256]{2,1,0:T(8,128)(2,1)}, u32[]{:S(2)}, u32[]{:S(2)}) %all-to-all-start.3) | async-done | bytes 524320 | tf_op jit(solution)/shard_map/all_to_all | solution.py:140
  125.6 0.0 copy-done.6
  125.6 0.0 copy-done.7
  125.6 3.2 %fusion.7 = bf16[1024,256]{1,0:T(8,128)(2,1)} fusion(bf16[256,256]{1,0:T(8,128)(2,1)S(1)} %copy-done.6, f32[1024,256]{1,0:T(8,128)} %convolution_add_fusion.2, bf16[1024,256]{1,0:T(8,128)(2,1)} %bitcast.14, s32[1024]{0:T(1024)S(1)} %eq.34, f32[256]{0:T(256)S(1)} %copy-done.7), kind=kOutput, calls=%fused_computation.18 | convolution fusion | flops 673447936 | bytes 2233344 | tf_op jit(solution)/shard_map/dot_general | solution.py:150
  128.9 2.6 %convolution_convert_fusion.1 = bf16[1024,256]{1,0:T(8,128)(2,1)} fusion(bf16[1024,1024]{1,0:T(8,128)(2,1)S(1)} %slice_multiply_fusion, bf16[1024,256]{1,0:T(8,128)(2,1)} %fusion.7), kind=kOutput, calls=%fused_computation.22 | convolution fusion | flops 537133056 | bytes 3145728 | tf_op jit(solution)/shard_map/dot_general | solution.py:85
  131.5 5.9 %all-to-all-start.4 = ((bf16[64,16,256]{2,1,0:T(8,128)(2,1)}), bf16[64,16,256]{2,1,0:T(8,128)(2,1)}, u32[]{:S(2)}, u32[]{:S(2)}) async-start(bf16[64,16,256]{2,1,0:T(8,128)(2,1)} %bitcast.71), calls=%async_computation.4 | async-start | bytes 1048576 | tf_op jit(solution)/shard_map/all_to_all | solution.py:153
  137.3 3.0 %fusion.10 = f32[1024,256]{1,0:T(8,128)S(1)} fusion(bf16[1024,256]{1,0:T(8,128)(2,1)} %fusion.7, bf16[1024,1024]{1,0:T(8,128)(2,1)} %param.16, bf16[1024,2048]{1,0:T(8,128)(2,1)} %bitcast.63), kind=kOutput, calls=%fused_computation.27 | convolution fusion | flops 537919488 | bytes 5767168 | tf_op jit(solution)/shard_map/dot_general | solution.py:83
  140.4 1.7 convolution_add_fusion.1
  142.1 0.0 copy-start.3
  142.1 12.9 %all-to-all-done.4 = bf16[64,16,256]{2,1,0:T(8,128)(2,1)} async-done(((bf16[64,16,256]{2,1,0:T(8,128)(2,1)}), bf16[64,16,256]{2,1,0:T(8,128)(2,1)}, u32[]{:S(2)}, u32[]{:S(2)}) %all-to-all-start.4) | async-done | bytes 524320 | tf_op jit(solution)/shard_map/all_to_all | solution.py:153
  154.9 2.2 %fusion.8 = bf16[1024,256]{1,0:T(8,128)(2,1)S(1)} fusion(f32[1024,256]{1,0:T(8,128)} %convolution_add_fusion.1, bf16[1024,256]{1,0:T(8,128)(2,1)} %bitcast.17, s32[1024]{0:T(1024)S(1)} %eq.34), kind=kOutput, calls=%fused_computation.20 | convolution fusion | flops 538443776 | bytes 2101248 | tf_op jit(solution)/shard_map/dot_general | solution.py:128
  157.2 0.0 copy-done.3
  157.2 0.0 copy-start.4
  157.2 0.3 convolution_bitcast_fusion
  157.5 0.1 copy.30
  157.6 11.0 %all_to_all.52 = f32[8,32,1,256]{3,1,2,0:T(8,128)S(1)} all-to-all(f32[8,32,1,256]{3,1,2,0:T(8,128)S(1)} %bitcast.69), channel_id=1, replica_groups=mesh['dev_0'=8,'dev_1'=4,'dev_2'=2,'rep'=4] {'dev_2','rep'}, dimensions={0} | all-to-all | bytes 524288 | tf_op jit(solution)/shard_map/all_to_all | solution.py:57
  168.7 13.4 %all_to_all.53 = f32[32,1,256]{2,1,0:T(1,128)S(1)} all-to-all(f32[32,1,256]{2,1,0:T(1,128)S(1)} %reduce_sum.34), channel_id=1, replica_groups=mesh['dev_0'=8,'dev_1'=4,'dev_2'=2,'rep'=4] {'dev_0','dev_1'}, dimensions={0} | all-to-all | bytes 65536 | tf_op jit(solution)/shard_map/all_to_all | solution.py:64
  182.0 0.1 reduce_sum.35
  182.1 11.6 %all_to_all.54 = f32[32,1,256]{2,1,0:T(1,128)S(1)} all-to-all(f32[32,1,256]{2,1,0:T(1,128)S(1)} %broadcast_in_dim.10), channel_id=1, replica_groups=mesh['dev_0'=8,'dev_1'=4,'dev_2'=2,'rep'=4] {'dev_0','dev_1'}, dimensions={0} | all-to-all | bytes 65536 | tf_op jit(solution)/shard_map/all_to_all | solution.py:33
  193.7 0.7 broadcast_in_dim.11
  194.5 6.2 %all-to-all-start.8 = ((f32[8,32,1,256]{3,1,2,0:T(8,128)}), f32[8,32,1,256]{3,1,2,0:T(8,128)S(1)}, u32[]{:S(2)}, u32[]{:S(2)}) async-start(f32[8,32,1,256]{3,1,2,0:T(8,128)} %broadcast_in_dim.11), calls=%async_computation.8 | async-start | bytes 524288 | tf_op jit(solution)/shard_map/all_to_all | solution.py:33
  200.7 0.0 copy-done.4
  200.7 1.1 convolution_convert_fusion
  201.7 5.5 %all-to-all-done.8 = f32[8,32,1,256]{3,1,2,0:T(8,128)S(1)} async-done(((f32[8,32,1,256]{3,1,2,0:T(8,128)}), f32[8,32,1,256]{3,1,2,0:T(8,128)S(1)}, u32[]{:S(2)}, u32[]{:S(2)}) %all-to-all-start.8) | async-done | bytes 262176 | tf_op jit(solution)/shard_map/all_to_all | solution.py:33
  207.2 0.9 copy.29
  (10 shorter events, 0.1 us)
Async XLA Ops:
  0.6 15.4 %copy-start = (bf16[1024,256]{1,0:T(8,128)(2,1)S(1)}, bf16[1024,256]{1,0:T(8,128)(2,1)}, u32[]{:S(2)}) copy-start(bf16[1024,256]{1,0:T(8,128)(2,1)} %param.12) | copy-start | bytes 1572868
  2.1 22.5 %all-to-all-start.1 = ((s32[64,1,16]{2,1,0:T(1,128)}), s32[64,1,16]{2,1,0:T(1,128)S(1)}, u32[]{:S(2)}, u32[]{:S(2)}) async-start(s32[64,1,16]{2,1,0:T(1,128)} %bitcast.7), calls=%async_computation.1 | async-start | bytes 65536 | tf_op jit(solution)/shard_map/all_to_all | solution.py:116
  24.6 33.3 %all-to-all-start = ((bf16[64,32,256]{2,1,0:T(8,128)(2,1)}), bf16[64,32,256]{2,1,0:T(8,128)(2,1)S(1)}, u32[]{:S(2)}, u32[]{:S(2)}) async-start(bf16[64,32,256]{2,1,0:T(8,128)(2,1)} %pad_maximum_fusion), calls=%async_computation | async-start | bytes 2097152 | tf_op jit(solution)/shard_map/all_to_all | solution.py:19
  65.8 7.6 %copy-start.5 = (s32[8,16]{1,0:T(8,128)S(1)}, s32[8,16]{1,0:T(8,128)}, u32[]{:S(2)}) copy-start(s32[8,16]{1,0:T(8,128)} %param.15) | copy-start | bytes 1540
  67.0 34.6 %all-to-all-start.2 = ((bf16[64,32,256]{2,1,0:T(8,128)(2,1)}), bf16[64,32,256]{2,1,0:T(8,128)(2,1)}, u32[]{:S(2)}, u32[]{:S(2)}) async-start(bf16[64,32,256]{2,1,0:T(8,128)(2,1)} %pad_maximum_fusion.1), calls=%async_computation.2 | async-start | bytes 2097152 | tf_op jit(solution)/shard_map/all_to_all | solution.py:19
  78.0 2.2 %copy-start.2 = (bf16[1024,1024]{1,0:T(8,128)(2,1)S(1)}, bf16[1024,1024]{1,0:T(8,128)(2,1)}, u32[]{:S(2)}) copy-start(bf16[1024,1024]{1,0:T(8,128)(2,1)} %param.17) | copy-start | bytes 6291460
  80.2 1.9 copy-start.1
  101.6 24.1 %all-to-all-start.3 = ((bf16[64,16,256]{2,1,0:T(8,128)(2,1)}), bf16[64,16,256]{2,1,0:T(8,128)(2,1)}, u32[]{:S(2)}, u32[]{:S(2)}) async-start(bf16[64,16,256]{2,1,0:T(8,128)(2,1)} %bitcast.70), calls=%async_computation.3 | async-start | bytes 1048576 | tf_op jit(solution)/shard_map/all_to_all | solution.py:140
  112.3 13.3 %copy-start.6 = (bf16[256,256]{1,0:T(8,128)(2,1)S(1)}, bf16[256,256]{1,0:T(8,128)(2,1)}, u32[]{:S(2)}) copy-start(bf16[256,256]{1,0:T(8,128)(2,1)} %param.18) | copy-start | bytes 393220
  112.4 13.3 %copy-start.7 = (f32[256]{0:T(256)S(1)}, f32[256]{0:T(256)}, u32[]{:S(2)}) copy-start(f32[256]{0:T(256)} %param.19) | copy-start | bytes 3076
  131.5 23.5 %all-to-all-start.4 = ((bf16[64,16,256]{2,1,0:T(8,128)(2,1)}), bf16[64,16,256]{2,1,0:T(8,128)(2,1)}, u32[]{:S(2)}, u32[]{:S(2)}) async-start(bf16[64,16,256]{2,1,0:T(8,128)(2,1)} %bitcast.71), calls=%async_computation.4 | async-start | bytes 1048576 | tf_op jit(solution)/shard_map/all_to_all | solution.py:153
  142.1 15.1 %copy-start.3 = (bf16[1024,256]{1,0:T(8,128)(2,1)S(1)}, bf16[1024,256]{1,0:T(8,128)(2,1)}, u32[]{:S(2)}) copy-start(bf16[1024,256]{1,0:T(8,128)(2,1)} %param.21) | copy-start | bytes 1572868
  157.2 43.5 %copy-start.4 = (bf16[256,256]{1,0:T(8,128)(2,1)S(1)}, bf16[256,256]{1,0:T(8,128)(2,1)}, u32[]{:S(2)}) copy-start(bf16[256,256]{1,0:T(8,128)(2,1)} %param.20) | copy-start | bytes 393220
  194.5 12.8 %all-to-all-start.8 = ((f32[8,32,1,256]{3,1,2,0:T(8,128)}), f32[8,32,1,256]{3,1,2,0:T(8,128)S(1)}, u32[]{:S(2)}, u32[]{:S(2)}) async-start(f32[8,32,1,256]{3,1,2,0:T(8,128)} %broadcast_in_dim.11), calls=%async_computation.8 | async-start | bytes 524288 | tf_op jit(solution)/shard_map/all_to_all | solution.py:33
where the time goes:
time: 209 us; the launch traced here: 208 us
  waiting for transfers between devices  79.8 us (38%)
  starting transfers between devices  43.3 us (21%)
  blocking collectives  36 us (17%)
  local copies, waits for them, and re-layouts  23.7 us (11%)
  matrix products  20.3 us (10%)
  other arithmetic  4.08 us (2%)
    all_to_all x2, waiting for transfers between devices, in_one_piece(): lax.all_to_all(both, axis, split_axis=split_dim, concat_axis=concat_dim,...  44.7 us
    all_to_all x1, blocking collectives, summed_rows(): return jnp.sum(lax.all_to_all(own, far, 0, 0, tiled=True), axis=0)  13.4 us
    all_to_all x1, starting transfers between devices, body(): lax.all_to_all(pull_rows.reshape(peer_count, per_peer), DEV, split_axis=0...  13.1 us
    all_to_all x1, waiting for transfers between devices, body(): lax.all_to_all(partial_two.astype(jnp.bfloat16).reshape(peer_count, per_p...  12.9 us
    all_to_all x1, blocking collectives, copy_for_each(): return lax.all_to_all(copies, axis, split_axis=0, concat_axis=0, tiled=True)  11.6 us
    all_to_all x2, starting transfers between devices, in_one_piece(): lax.all_to_all(both, axis, split_axis=split_dim, concat_axis=concat_dim,...  11.6 us
    all_to_all x1, waiting for transfers between devices, body(): lax.all_to_all(partial_one.astype(jnp.bfloat16).reshape(peer_count, per_p...  11.6 us
    all_to_all x1, blocking collectives, summed_on_arrival(): lax.all_to_all(tiles, axis, split_axis=0, concat_axis=0, tiled=True)  11 us
  transfers between devices with their start and end apart: 6, of which 6 were waited for; matrix products, arithmetic and copies ran while one was open for 12% of the time, Pallas kernels for 0%

commit v1 on v0

v1 whole, which is shorter than its diff:
```python
import jax
import jax.numpy as jnp
from jax import lax
from jax.experimental import pallas as pl
from jax.experimental.pallas import tpu as pltpu
from jax.sharding import Mesh
from jax.sharding import PartitionSpec as P

CHIPS = ("dev_0", "dev_1")
DEV = ("dev_0", "dev_1", "dev_2")
DEV_REP = ("dev_0", "dev_1", "dev_2", "rep")
PEERS, SLOT, HALF, ROWS, F = 64, 16, 128, 1024, 256
STEP = 256

F32, BF16 = jnp.float32, jnp.bfloat16


def dot(a, b):
    return jnp.dot(a, b, preferred_element_type=F32)


def call(body, outs, operands, *, smem=0, scratch=(), flops=0, mib=24, name=None):
    specs = [
        pl.BlockSpec(memory_space=pltpu.SMEM if i < smem else pltpu.VMEM)
        for i in range(len(operands))
    ]
    moved = sum(a.size * a.dtype.itemsize for a in (*operands, *outs))
    return pl.pallas_call(
        body,
        out_shape=outs,
        in_specs=specs,
        out_specs=tuple(pl.BlockSpec(memory_space=pltpu.VMEM) for _ in outs),
        scratch_shapes=scratch,
        compiler_params=pltpu.CompilerParams(vmem_limit_bytes=mib << 20),
        cost_estimate=pl.CostEstimate(flops=flops, bytes_accessed=moved, transcendentals=0),
        name=name,
    )(*operands)


def shaped(*dims, dtype=BF16):
    return jax.ShapeDtypeStruct(dims, dtype)


def put(message, at, peers, value):
    count = value.shape[0] // SLOT
    message[peers, at : at + SLOT, :] = value[:, :HALF].reshape(count, SLOT, HALF)
    message[peers, at + SLOT : at + 2 * SLOT, :] = value[:, HALF:].reshape(count, SLOT, HALF)


def take(message, at, into):
    into[:, :HALF] = message[:, at : at + SLOT, :].reshape(ROWS, HALF)
    into[:, HALF:] = message[:, at + SLOT : at + 2 * SLOT, :].reshape(ROWS, HALF)


def send_clusters(owner, x, h, pulled, message):
    for j in range(PEERS):
        e = owner[0, j]
        rows = slice(j * SLOT, (j + 1) * SLOT)
        message[e, 0:16, :] = x[rows, :HALF]
        message[e, 16:32, :] = x[rows, HALF:]
        message[e, 32:48, :] = h[rows, :HALF]
        message[e, 48:64, :] = h[rows, HALF:]
    which = lax.broadcasted_iota(jnp.int32, (8, HALF), 0)
    for a in range(8):
        numbers = pulled[a : a + 1, :]
        high = (numbers // 32).astype(F32)
        low = (numbers % 32).astype(F32)
        tile = jnp.where(which == 0, high, jnp.where(which == 1, low, 0.0)).astype(BF16)
        for b in range(8):
            message[a * 8 + b, 64:72, :] = tile


def requested(me, message):
    tile = message[:, 64:72, :].astype(F32)
    numbers = 32.0 * tile[:, 0:1, :] + tile[:, 1:2, :]
    lane = lax.broadcasted_iota(jnp.int32, (PEERS, SLOT, HALF), 2)
    place = lax.broadcasted_iota(jnp.int32, (PEERS, SLOT, HALF), 1)
    mine = lane == (me % 8) * SLOT + place
    return jnp.sum(jnp.where(mine, numbers, 0.0), axis=2, keepdims=True).reshape(ROWS, 1)


def mask_tiles(occupied, local, edge, local_out, edge_out, flipped_out):
    for i in range(8):
        rows = slice(i * 128, (i + 1) * 128)
        for j in range(8):
            cols = slice(j * 128, (j + 1) * 128)
            part = local[rows, cols]
            local_out[rows, cols] = jnp.where(occupied[i, j] != 0, part, jnp.zeros_like(part))
            part = edge[rows, cols]
            part = jnp.where(occupied[i, 8 + j] != 0, part, jnp.zeros_like(part))
            edge_out[rows, cols] = part
            flipped_out[cols, rows] = part.T


def serve(me, message, flipped, own_x, reply, own_h):
    take(message, 0, own_x)
    take(message, 32, own_h)
    wanted = requested(me[0], message).astype(jnp.int32)
    for at in range(0, ROWS, STEP):
        rows, peers = slice(at, at + STEP), slice(at // SLOT, (at + STEP) // SLOT)
        column = lax.broadcasted_iota(jnp.int32, (STEP, ROWS), 1)
        select = (column == wanted[rows]).astype(BF16)
        put(reply, 0, peers, dot(select, own_x[...]).astype(BF16))
        put(reply, 64, peers, dot(select, own_h[...]).astype(BF16))
        put(reply, 32, peers, dot(flipped[rows, :], own_x[...]).astype(BF16))


def prepare(me, message, local, own_x, partial, gather):
    wanted = jnp.broadcast_to(requested(me[0], message), (ROWS, HALF))
    row = lax.broadcasted_iota(jnp.int32, (ROWS, HALF), 0).astype(F32)
    for a in range(8):
        cols = slice(a * HALF, (a + 1) * HALF)
        gather[:, cols] = (row == wanted[cols].T[0:1, :]).astype(BF16)
    for at in range(0, ROWS, STEP):
        rows = slice(at, at + STEP)
        partial[rows, :] = dot(local[rows, :], own_x[...])


def first_layer(message, partial, edge, gather, flipped, w, bias, hidden, push, far, pushed):
    take(message, 0, far)
    take(message, 32, pushed)
    for at in range(0, ROWS, STEP):
        rows = slice(at, at + STEP)
        total = partial[rows, :] + dot(edge[rows, :], far[...]) + dot(gather[rows, :], pushed[...])
        value = dot(total.astype(BF16), w[...]) + bias[...]
        hidden[rows, :] = jnp.maximum(value, 0.0).astype(BF16)
    for at in range(0, ROWS, STEP):
        rows, peers = slice(at, at + STEP), slice(at // SLOT, (at + STEP) // SLOT)
        put(push, 0, peers, dot(flipped[rows, :], hidden[...]).astype(BF16))


def second_terms(message, local, edge, hidden, partial, far):
    take(message, 64, far)
    for at in range(0, ROWS, STEP):
        rows = slice(at, at + STEP)
        partial[rows, :] = dot(local[rows, :], hidden[...]) + dot(edge[rows, :], far[...])


def second_layer(message, partial, gather, cotangent, aggregate, gradient, pushed):
    take(message, 0, pushed)
    for at in range(0, ROWS, STEP):
        rows = slice(at, at + STEP)
        total = partial[rows, :] + dot(gather[rows, :], pushed[...])
        aggregate[rows, :] = total.astype(BF16)
    gradient[...] = lax.dot_general(
        aggregate[...], cotangent[...], (((0,), (0,)), ((), ())), preferred_element_type=F32
    )


def exchange(message):
    return lax.all_to_all(message, DEV, split_axis=0, concat_axis=0, tiled=True)


def swapped(array, axis, mask):
    return lax.ppermute(array, axis, [(i, i ^ mask) for i in range(lax.axis_size(axis))])


def summed_everywhere(term):
    core = lax.axis_index("dev_2")
    halves = term.reshape(2, ROWS // 8, F)
    kept = lax.dynamic_index_in_dim(halves, core, 0, keepdims=False)
    sent = lax.dynamic_index_in_dim(halves, 1 - core, 0, keepdims=False)
    half = kept + swapped(sent, "dev_2", 1)
    tiles = lax.all_to_all(half.reshape(32, 4, F), CHIPS, split_axis=0, concat_axis=0, tiled=True)
    own = jnp.sum(tiles, axis=0)
    own = (own + swapped(own, "rep", 1)) + (swapped(own, "rep", 2) + swapped(own, "rep", 3))
    copies = jnp.broadcast_to(own[None], (32, 4, F))
    mine = lax.all_to_all(copies, CHIPS, split_axis=0, concat_axis=0, tiled=True).reshape(128, F)
    other = swapped(mine, "dev_2", 1)
    first = jnp.where(core == 0, mine, other)
    second = jnp.where(core == 0, other, mine)
    return jnp.concatenate([first, second], axis=0)


def body(
    features,
    history,
    new_owner,
    pull_rows,
    occupancy,
    adj_local,
    adj_boundary,
    w_first,
    bias_first,
    w_second,
    cotangent,
):
    me = lax.axis_index(DEV).astype(jnp.int32).reshape(1)
    wide = 2 * ROWS * ROWS * F
    nodes = pltpu.VMEM((ROWS, F), BF16)

    (message,) = call(
        send_clusters,
        (shaped(PEERS, 72, HALF),),
        (new_owner, features, history, pull_rows.reshape(8, 128)),
        smem=1,
        flops=ROWS * F,
        name="send_clusters",
    )
    local, edge, flipped = call(
        mask_tiles,
        (shaped(ROWS, ROWS),) * 3,
        (occupancy, adj_local, adj_boundary),
        smem=1,
        flops=wide,
        name="mask_tiles",
    )
    arrived = exchange(message)
    own_x, reply = call(
        serve,
        (shaped(ROWS, F), shaped(PEERS, 96, HALF)),
        (me, arrived, flipped),
        smem=1,
        scratch=(nodes,),
        flops=3 * wide,
        name="serve",
    )
    partial_one, gather = call(
        prepare,
        (shaped(ROWS, F, dtype=F32), shaped(ROWS, ROWS)),
        (me, arrived, local, own_x),
        smem=1,
        flops=wide,
        name="prepare",
    )
    answers = exchange(reply)
    hidden, push = call(
        first_layer,
        (shaped(ROWS, F), shaped(PEERS, 32, HALF)),
        (answers, partial_one, edge, gather, flipped, w_first, bias_first.reshape(1, F)),
        scratch=(nodes, nodes),
        flops=3 * wide,
        name="first_layer",
    )
    (partial_two,) = call(
        second_terms,
        (shaped(ROWS, F, dtype=F32),),
        (answers, local, edge, hidden),
        scratch=(nodes,),
        flops=2 * wide,
        name="second_terms",
    )
    pushed = exchange(push)
    aggregate, term = call(
        second_layer,
        (shaped(ROWS, F), shaped(F, F, dtype=F32)),
        (pushed, partial_two, gather, cotangent),
        scratch=(nodes,),
        flops=2 * wide,
        name="second_layer",
    )
    output = jnp.dot(aggregate, w_second, preferred_element_type=F32).astype(BF16)
    return (hidden, output, summed_everywhere(term))


def solution(mesh):
    finer = Mesh(
        mesh.devices.reshape(8, 4, 2, mesh.shape["rep"]), ("dev_0", "dev_1", "dev_2", "rep")
    )
    rows = P(DEV_REP, None)
    return jax.shard_map(
        body,
        mesh=finer,
        in_specs=(rows, rows, rows, P(DEV_REP), rows, rows, rows, P(), P(), P(), rows),
        out_specs=(rows, rows, P()),
        check_vma=False,
    )
```

time: 209 us -> 182 us (0.87)
  blocking collectives: 36 us -> 14 us
  matrix products: 20.3 us -> 1.09 us
  Pallas kernels: 0 us -> 13.9 us
  local copies, waits for them, and re-layouts: 23.7 us -> 31.1 us
  starting transfers between devices: 43.3 us -> 38.9 us
  other arithmetic: 4.08 us -> 0.81 us
    unnamed x18 -> x54, local copies, waits for them, and re-layouts: 3.92 us -> 30.3 us
    all_to_all x3 -> x1, blocking collectives: 36 us -> 14 us  [summed_everywhere(): lax.all_to_all(half.reshape(32, 4, F), CHIPS, split_axis=0, concat_axis=0...]
    dot_general x10 -> x1, matrix products: 20.3 us -> 1.09 us  [body(): jnp.dot(aggregate, w_second, preferred_element_type=F32).astype(BF16)]
    pallas_call x0 -> x7, Pallas kernels: none -> 13.9 us  [call(): pl.pallas_call(body, out_shape=outs, in_specs=specs, out_specs=tuple((pl....]
    all_to_all x6 -> x4, starting transfers between devices: 43.3 us -> 30.1 us  [the longest x3 26.3 us: exchange(): return lax.all_to_all(message, DEV, split_axis=0, concat_axis=0, tiled=True)]
    gather x4 -> x0, local copies, waits for them, and re-layouts: 10.1 us -> none  [the longest x2 7.88 us: fetch_rows(): return values[requests].reshape(peer_count, per_peer, breadth)]
    ppermute x0 -> x5, starting transfers between devices: none -> 8.8 us  [swapped(): lax.ppermute(array, axis, [(i, i ^ mask) for i in range(lax.axis_size(axi...]
    broadcast_in_dim x4 -> x1, local copies, waits for them, and re-layouts: 5.25 us -> 0.68 us  [summed_everywhere(): copies = jnp.broadcast_to(own[None], (32, 4, F))]
  transfers between devices with their start and end apart: 6 -> 9, of which waited for: 6 -> 7; matrix products, arithmetic and copies ran while one was open for 12% -> 1% of each run, Pallas kernels for 0% -> 3%
where the time goes in v1:
time: 182 us; the launch traced here: 181 us
  waiting for transfers between devices  80.4 us (44%)
  starting transfers between devices  38.9 us (21%)
  local copies, waits for them, and re-layouts  31.1 us (17%)
  blocking collectives  14 us (8%)
  Pallas kernels  13.9 us (8%)
    all_to_all x3, waiting for transfers between devices, exchange(): return lax.all_to_all(message, DEV, split_axis=0, concat_axis=0, tiled=True)  67 us
    unnamed x54, local copies, waits for them, and re-layouts  30.3 us
    all_to_all x3, starting transfers between devices, exchange(): return lax.all_to_all(message, DEV, split_axis=0, concat_axis=0, tiled=True)  26.3 us
    all_to_all x1, blocking collectives, summed_everywhere(): lax.all_to_all(half.reshape(32, 4, F), CHIPS, split_axis=0, concat_axis=0...  14 us
    pallas_call x7, Pallas kernels, call(): pl.pallas_call(body, out_shape=outs, in_specs=specs, out_specs=tuple((pl....  13.9 us
    all_to_all x1, waiting for transfers between devices, summed_everywhere(): lax.all_to_all(copies, CHIPS, split_axis=0, concat_axis=0, tiled=True)  9.4 us
    ppermute x5, starting transfers between devices, swapped(): lax.ppermute(array, axis, [(i, i ^ mask) for i in range(lax.axis_size(axi...  8.8 us
    ppermute x5, waiting for transfers between devices, swapped(): lax.ppermute(array, axis, [(i, i ^ mask) for i in range(lax.axis_size(axi...  4.09 us
  transfers between devices with their start and end apart: 9, of which 7 were waited for; matrix products, arithmetic and copies ran while one was open for 1% of the time, Pallas kernels for 3%

profile of v1, /device:TPU:1, one launch (start us, length us, event | category | flops | bytes accessed | tf_op | source)
XLA Modules:
  0.0 181.1 jit_solution(12867733437622018973)
XLA Ops:
  0.6 0.0 copy-start
  0.6 0.0 copy-start.19
  0.7 1.1 copy-done.19
  1.7 1.0 copy-done.20
  2.8 0.7 copy-done.23
  3.5 0.7 copy-done.26
  4.1 1.8 %send_clusters.1 = bf16[64,72,128]{2,1,0:T(8,128)(2,1)} custom-call(s32[1,64]{1,0:T(1,128)S(1)} %copy-done.26, bf16[1024,256]{1,0:T(8,128)(2,1)S(1)} %copy-done.19, bf16[1024,256]{1,0:T(8,128)(2,1)S(1)} %copy-done.20, s32[8,128]{1,0:T(8,128)S(1)} %bitcast.12), custom_call_target="tpu_custom_call" | custom-call | flops 262144 | bytes 2232576 | tf_op jit(solution)/shard_map/send_clusters/pallas_call | solution.py:28
  6.0 13.1 %all-to-all-start = ((bf16[64,72,128]{2,1,0:T(8,128)(2,1)}), bf16[64,72,128]{2,1,0:T(8,128)(2,1)S(1)}, u32[]{:S(2)}, u32[]{:S(2)}) async-start(bf16[64,72,128]{2,1,0:T(8,128)(2,1)} %send_clusters.1), calls=%async_computation | async-start | bytes 2359296 | tf_op jit(solution)/shard_map/all_to_all | solution.py:151
  19.1 0.0 copy-done.24
  19.1 0.0 copy-start.13
  19.1 1.6 copy-done.13
  20.7 1.6 copy-done.14
  22.3 2.1 %mask_tiles.1 = (bf16[1024,1024]{1,0:T(8,128)(2,1)S(1)}, bf16[1024,1024]{1,0:T(8,128)(2,1)S(1)}, bf16[1024,1024]{1,0:T(8,128)(2,1)S(1)}) custom-call(s32[8,16]{1,0:T(8,128)S(1)} %copy-done.24, bf16[1024,1024]{1,0:T(8,128)(2,1)S(1)} %copy-done.13, bf16[1024,1024]{1,0:T(8,128)(2,1)S(1)} %copy-done.14), custom_call_target="tpu_custom_call" | custom-call | flops 536870912 | bytes 10486272 | tf_op jit(solution)/shard_map/mask_tiles/pallas_call | solution.py:28
  24.4 0.0 copy-start.1
  24.4 1.3 copy-done.1
  25.7 1.4 copy-done.4
  27.1 1.4 copy-done.10
  28.5 21.2 %all-to-all-done.message = bf16[64,72,128]{2,1,0:T(8,128)(2,1)S(1)} async-done(((bf16[64,72,128]{2,1,0:T(8,128)(2,1)}), bf16[64,72,128]{2,1,0:T(8,128)(2,1)S(1)}, u32[]{:S(2)}, u32[]{:S(2)}) %all-to-all-start) | async-done | bytes 1179680 | tf_op jit(solution)/shard_map/all_to_all | solution.py:151
  49.7 1.6 copy-done.11
  51.3 1.9 %serve.1 = (bf16[1024,256]{1,0:T(8,128)(2,1)S(1)}, bf16[64,96,128]{2,1,0:T(8,128)(2,1)S(1)}) custom-call(s32[1]{0:T(128)} %bitcast.me, bf16[64,72,128]{2,1,0:T(8,128)(2,1)S(1)} %all-to-all-done.message, bf16[1024,1024]{1,0:T(8,128)(2,1)S(1)} %copy-done.11), custom_call_target="tpu_custom_call" | custom-call | flops 1610612736 | bytes 5373956 | tf_op jit(solution)/shard_map/serve/pallas_call | solution.py:28
  53.2 0.0 copy-start.15
  53.2 1.1 copy-done.15
  54.4 6.7 %all-to-all-start.1 = ((bf16[64,96,128]{2,1,0:T(8,128)(2,1)}), bf16[64,96,128]{2,1,0:T(8,128)(2,1)S(1)}, u32[]{:S(2)}, u32[]{:S(2)}) async-start(bf16[64,96,128]{2,1,0:T(8,128)(2,1)} %copy-done.15), calls=%async_computation.1 | async-start | bytes 3145728 | tf_op jit(solution)/shard_map/all_to_all | solution.py:151
  61.1 0.0 copy-start.25
  61.1 0.0 copy-start.5
  61.1 1.6 copy-done.5
  62.7 1.5 prepare.1
  64.3 0.0 copy-start.7
  64.3 1.4 copy-done.7
  65.6 1.0 copy-done.16
  66.6 33.5 %all-to-all-done.1.message = bf16[64,96,128]{2,1,0:T(8,128)(2,1)S(1)} async-done(((bf16[64,96,128]{2,1,0:T(8,128)(2,1)}), bf16[64,96,128]{2,1,0:T(8,128)(2,1)S(1)}, u32[]{:S(2)}, u32[]{:S(2)}) %all-to-all-start.1) | async-done | bytes 1572896 | tf_op jit(solution)/shard_map/all_to_all | solution.py:151
  100.2 0.0 copy-done.22
  100.2 0.0 copy-done.25
  100.2 1.6 copy-done.2
  101.8 1.6 copy-done.8
  103.4 1.6 copy-done.12
  104.9 1.2 copy-done.17
  106.2 4.2 %first_layer.1 = (bf16[1024,256]{1,0:T(8,128)(2,1)}, bf16[64,32,128]{2,1,0:T(8,128)(2,1)}) custom-call(bf16[64,96,128]{2,1,0:T(8,128)(2,1)S(1)} %all-to-all-done.1.message, f32[1024,256]{1,0:T(8,128)S(1)} %copy-done.17, bf16[1024,1024]{1,0:T(8,128)(2,1)S(1)} %copy-done.2, bf16[1024,1024]{1,0:T(8,128)(2,1)S(1)} %copy-done.8, ...), custom_call_target="tpu_custom_call" | custom-call | flops 1610612736 | bytes 10093568 | tf_op jit(solution)/shard_map/first_layer/pallas_call | solution.py:28
  110.4 6.4 %all-to-all-start.2 = ((bf16[64,32,128]{2,1,0:T(8,128)(2,1)}), bf16[64,32,128]{2,1,0:T(8,128)(2,1)S(1)}, u32[]{:S(2)}, u32[]{:S(2)}) async-start(bf16[64,32,128]{2,1,0:T(8,128)(2,1)} %get-tuple-element.22), calls=%async_computation.2 | async-start | bytes 1048576 | tf_op jit(solution)/shard_map/all_to_all | solution.py:151
  116.7 0.0 copy-start.3
  116.8 1.6 copy-done.3
  118.3 1.6 copy-done.6
  119.9 1.0 copy-done.18
  121.0 1.3 second_terms.1.partial
  122.2 12.2 %all-to-all-done.2.message = bf16[64,32,128]{2,1,0:T(8,128)(2,1)S(1)} async-done(((bf16[64,32,128]{2,1,0:T(8,128)(2,1)}), bf16[64,32,128]{2,1,0:T(8,128)(2,1)S(1)}, u32[]{:S(2)}, u32[]{:S(2)}) %all-to-all-start.2) | async-done | bytes 524320 | tf_op jit(solution)/shard_map/all_to_all | solution.py:151
  134.4 1.6 copy-done.9
  136.0 1.0 copy-done.21
  137.1 1.1 second_layer.1
  138.2 0.7 collective-permute-start
  138.8 1.0 collective-permute-done
  139.9 14.0 %all_to_all.25 = f32[32,4,256]{2,1,0:T(4,128)S(1)} all-to-all(f32[32,4,256]{2,1,0:T(4,128)S(1)} %reshape.29), channel_id=1, replica_groups=mesh['dev_0'=8,'dev_1'=4,'dev_2'=2,'rep'=4] {'dev_0','dev_1'}, dimensions={0} | all-to-all | bytes 262144 | tf_op jit(solution)/shard_map/all_to_all | solution.py:164
  153.9 2.8 %collective-permute-start.2 = (f32[4,256]{1,0:T(4,128)S(1)}, f32[4,256]{1,0:T(4,128)S(1)}, u32[]{:S(2)}, u32[]{:S(2)}) collective-permute-start(f32[4,256]{1,0:T(4,128)S(1)} %reduce_sum.9), channel_id=1, source_target_pairs={{0,2},{1,3},{2,0},{3,1},{4,6},{5,7},{6,4},{7,5},{8,10},{9,11},{10,... | collective-permute-start | bytes 12296 | tf_op jit(solution)/shard_map/ppermute | solution.py:155
  156.8 0.9 collective-permute-start.3
  157.6 0.0 collective-permute-start.1
  157.6 0.4 collective-permute-done.2
  158.0 2.7 %collective-permute-done.3 = f32[4,256]{1,0:T(4,128)S(1)} collective-permute-done((f32[4,256]{1,0:T(4,128)S(1)}, f32[4,256]{1,0:T(4,128)S(1)}, u32[]{:S(2)}, u32[]{:S(2)}) %collective-permute-start.3) | collective-permute-done | bytes 4128 | tf_op jit(solution)/shard_map/ppermute | solution.py:155
  160.7 0.0 collective-permute-done.1
  160.7 0.7 broadcast_in_dim.2
  161.4 3.9 %all-to-all-start.4 = ((f32[32,4,256]{2,1,0:T(4,128)}), f32[32,4,256]{2,1,0:T(4,128)S(1)}, u32[]{:S(2)}, u32[]{:S(2)}) async-start(f32[32,4,256]{2,1,0:T(4,128)} %broadcast_in_dim.2), calls=%async_computation.4 | async-start | bytes 262144 | tf_op jit(solution)/shard_map/all_to_all | solution.py:168
  165.3 9.4 %all-to-all-done.4 = f32[32,4,256]{2,1,0:T(4,128)S(1)} async-done(((f32[32,4,256]{2,1,0:T(4,128)}), f32[32,4,256]{2,1,0:T(4,128)S(1)}, u32[]{:S(2)}, u32[]{:S(2)}) %all-to-all-start.4) | async-done | bytes 131104 | tf_op jit(solution)/shard_map/all_to_all | solution.py:168
  174.7 4.5 %collective-permute-start.4 = (f32[128,256]{1,0:T(8,128)S(1)}, f32[128,256]{1,0:T(8,128)S(1)}, u32[]{:S(2)}, u32[]{:S(2)}) collective-permute-start(f32[128,256]{1,0:T(8,128)S(1)} %reshape.30), channel_id=1, source_target_pairs={{0,4},{4,0},{1,5},{5,1},{2,6},{6,2},{3,7},{7,3},{8,12},{12,8},{9,1... | collective-permute-start | bytes 393224 | tf_op jit(solution)/shard_map/ppermute | solution.py:155
  179.2 1.1 convolution_convert_fusion
  180.3 0.0 collective-permute-done.4
  180.3 0.7 pad_maximum_fusion
  (26 shorter events, 0.2 us)
Async XLA Ops:
  0.6 178.6 %copy-start = (bf16[256,256]{1,0:T(8,128)(2,1)S(1)}, bf16[256,256]{1,0:T(8,128)(2,1)}, u32[]{:S(2)}) copy-start(bf16[256,256]{1,0:T(8,128)(2,1)} %param.20) | copy-start | bytes 393220
  0.6 1.1 copy-start.19
  1.7 1.0 copy-start.20
  2.8 0.7 copy-start.23
  3.5 0.7 copy-start.26
  4.1 15.0 %copy-start.24 = (s32[8,16]{1,0:T(8,128)S(1)}, s32[8,16]{1,0:T(8,128)}, u32[]{:S(2)}) copy-start(s32[8,16]{1,0:T(8,128)} %occupied.1) | copy-start | bytes 1540
  6.0 43.8 %all-to-all-start = ((bf16[64,72,128]{2,1,0:T(8,128)(2,1)}), bf16[64,72,128]{2,1,0:T(8,128)(2,1)S(1)}, u32[]{:S(2)}, u32[]{:S(2)}) async-start(bf16[64,72,128]{2,1,0:T(8,128)(2,1)} %send_clusters.1), calls=%async_computation | async-start | bytes 2359296 | tf_op jit(solution)/shard_map/all_to_all | solution.py:151
  19.1 1.6 copy-start.13
  20.7 1.6 copy-start.14
  24.4 1.3 copy-start.1
  25.7 1.4 copy-start.4
  27.1 1.4 copy-start.10
  49.7 1.6 copy-start.11
  53.2 1.2 copy-start.15
  54.4 45.8 %copy-start.22 = (bf16[256,256]{1,0:T(8,128)(2,1)S(1)}, bf16[256,256]{1,0:T(8,128)(2,1)}, u32[]{:S(2)}) copy-start(bf16[256,256]{1,0:T(8,128)(2,1)} %w.1) | copy-start | bytes 393220
  54.4 45.8 %all-to-all-start.1 = ((bf16[64,96,128]{2,1,0:T(8,128)(2,1)}), bf16[64,96,128]{2,1,0:T(8,128)(2,1)S(1)}, u32[]{:S(2)}, u32[]{:S(2)}) async-start(bf16[64,96,128]{2,1,0:T(8,128)(2,1)} %copy-done.15), calls=%async_computation.1 | async-start | bytes 3145728 | tf_op jit(solution)/shard_map/all_to_all | solution.py:151
  61.1 39.1 %copy-start.25 = (f32[256]{0:T(256)S(1)}, f32[256]{0:T(256)}, u32[]{:S(2)}) copy-start(f32[256]{0:T(256)} %param.19) | copy-start | bytes 3076
  61.1 1.6 copy-start.5
  64.3 1.4 copy-start.7
  65.6 1.0 copy-start.16
  100.2 1.6 copy-start.2
  101.8 1.6 copy-start.8
  103.4 1.6 copy-start.12
  104.9 1.2 copy-start.17
  110.4 24.1 %all-to-all-start.2 = ((bf16[64,32,128]{2,1,0:T(8,128)(2,1)}), bf16[64,32,128]{2,1,0:T(8,128)(2,1)S(1)}, u32[]{:S(2)}, u32[]{:S(2)}) async-start(bf16[64,32,128]{2,1,0:T(8,128)(2,1)} %get-tuple-element.22), calls=%async_computation.2 | async-start | bytes 1048576 | tf_op jit(solution)/shard_map/all_to_all | solution.py:151
  116.7 1.6 copy-start.3
  118.3 1.6 copy-start.6
  119.9 1.0 copy-start.18
  134.4 1.6 copy-start.9
  136.0 1.0 copy-start.21
  138.2 1.6 collective-permute-start
  153.9 4.0 %collective-permute-start.2 = (f32[4,256]{1,0:T(4,128)S(1)}, f32[4,256]{1,0:T(4,128)S(1)}, u32[]{:S(2)}, u32[]{:S(2)}) collective-permute-start(f32[4,256]{1,0:T(4,128)S(1)} %reduce_sum.9), channel_id=1, source_target_pairs={{0,2},{1,3},{2,0},{3,1},{4,6},{5,7},{6,4},{7,5},{8,10},{9,11},{10,... | collective-permute-start | bytes 12296 | tf_op jit(solution)/shard_map/ppermute | solution.py:155
  156.8 4.0 %collective-permute-start.3 = (f32[4,256]{1,0:T(4,128)S(1)}, f32[4,256]{1,0:T(4,128)S(1)}, u32[]{:S(2)}, u32[]{:S(2)}) collective-permute-start(f32[4,256]{1,0:T(4,128)S(1)} %reduce_sum.9), channel_id=1, source_target_pairs={{0,3},{1,2},{2,1},{3,0},{4,7},{5,6},{6,5},{7,4},{8,11},{9,10},{10,... | collective-permute-start | bytes 12296 | tf_op jit(solution)/shard_map/ppermute | solution.py:155
  157.6 3.1 %collective-permute-start.1 = (f32[4,256]{1,0:T(4,128)S(1)}, f32[4,256]{1,0:T(4,128)S(1)}, u32[]{:S(2)}, u32[]{:S(2)}) collective-permute-start(f32[4,256]{1,0:T(4,128)S(1)} %reduce_sum.9), channel_id=1, source_target_pairs={{0,1},{1,0},{2,3},{3,2},{4,5},{5,4},{6,7},{7,6},{8,9},{9,8},{10,11... | collective-permute-start | bytes 12296 | tf_op jit(solution)/shard_map/ppermute | solution.py:155
  161.4 13.3 %all-to-all-start.4 = ((f32[32,4,256]{2,1,0:T(4,128)}), f32[32,4,256]{2,1,0:T(4,128)S(1)}, u32[]{:S(2)}, u32[]{:S(2)}) async-start(f32[32,4,256]{2,1,0:T(4,128)} %broadcast_in_dim.2), calls=%async_computation.4 | async-start | bytes 262144 | tf_op jit(solution)/shard_map/all_to_all | solution.py:168
  174.7 5.6 %collective-permute-start.4 = (f32[128,256]{1,0:T(8,128)S(1)}, f32[128,256]{1,0:T(8,128)S(1)}, u32[]{:S(2)}, u32[]{:S(2)}) collective-permute-start(f32[128,256]{1,0:T(8,128)S(1)} %reshape.30), channel_id=1, source_target_pairs={{0,4},{4,0},{1,5},{5,1},{2,6},{6,2},{3,7},{7,3},{8,12},{12,8},{9,1... | collective-permute-start | bytes 393224 | tf_op jit(solution)/shard_map/ppermute | solution.py:155

commit v2 on v1

v2 whole, which is shorter than its diff:
```python
import jax
import jax.numpy as jnp
from jax import lax
from jax.experimental import pallas as pl
from jax.experimental.pallas import tpu as pltpu
from jax.sharding import Mesh
from jax.sharding import PartitionSpec as P

DEV = ("dev_0", "dev_1", "dev_2")
DEV_REP = ("dev_0", "dev_1", "dev_2", "rep")
PEERS, SLOT, HALF, ROWS, F = 64, 16, 128, 1024, 256
STEP = 512
VMEM = 67043328

F32, BF16 = jnp.float32, jnp.bfloat16


def dot(a, b):
    return jnp.dot(a, b, preferred_element_type=F32)


def call(body, kinds, outs, operands, *, own=(), copies=0, flops=0, room=0, name=None):
    spaces = {"s": pltpu.SMEM, "v": pltpu.VMEM, "h": pltpu.HBM}
    moved = sum(a.size * a.dtype.itemsize for a in (*operands, *outs))
    arrivals = (pltpu.SemaphoreType.DMA((copies,)),) if copies else ()
    specs = [pl.BlockSpec(memory_space=spaces[k]) for k in kinds]
    return pl.pallas_call(
        body,
        out_shape=outs,
        in_specs=specs[: len(operands)],
        out_specs=tuple(specs[len(operands) :]),
        scratch_shapes=(*own, *arrivals),
        compiler_params=pltpu.CompilerParams(vmem_limit_bytes=VMEM - room),
        cost_estimate=pl.CostEstimate(flops=flops, bytes_accessed=moved, transcendentals=0),
        name=name,
    )(*operands)


class Copies:
    def __init__(self, semaphores):
        self.semaphores, self.used = semaphores, 0

    def start(self, source, target):
        copy = pltpu.make_async_copy(source, target, self.semaphores.at[self.used])
        self.used += 1
        copy.start()
        return copy

    def unpack(self, message, at, into, peers=slice(None)):
        left = self.start(message.at[peers, at : at + SLOT, :], into.at[peers, :, 0:HALF])
        right = self.start(message.at[peers, at + SLOT : at + 2 * SLOT, :], into.at[peers, :, HALF:])
        return (left, right)


def wait(*copies):
    for copy in copies:
        copy.wait()


def shaped(*dims, dtype=BF16):
    return jax.ShapeDtypeStruct(dims, dtype)


def put(message, at, peers, value):
    count = value.shape[0] // SLOT
    message[peers, at : at + SLOT, :] = value[:, :HALF].reshape(count, SLOT, HALF)
    message[peers, at + SLOT : at + 2 * SLOT, :] = value[:, HALF:].reshape(count, SLOT, HALF)


def steps():
    for at in range(0, ROWS, STEP):
        yield slice(at, at + STEP), slice(at // SLOT, (at + STEP) // SLOT)


def flat(ref):
    return ref[...].reshape(ROWS, F)


def send_clusters(owner, x, h, pulled, message, owners, xs, hs, numbers, packed, sem):
    copies = Copies(sem)
    order = copies.start(owner, owners)
    first = copies.start(x, xs)
    rows_in = copies.start(pulled, numbers)
    second = copies.start(h, hs)
    which = lax.broadcasted_iota(jnp.int32, (8, HALF), 0)
    rows_in.wait()
    for a in range(8):
        line = numbers[a : a + 1, :]
        high = (line // 32).astype(F32)
        low = (line % 32).astype(F32)
        tile = jnp.where(which == 0, high, jnp.where(which == 1, low, 0.0)).astype(BF16)
        for b in range(8):
            packed[a * 8 + b, 64:72, :] = tile
    wait(order, first)
    for j in range(PEERS):
        e = owners[0, j]
        rows = slice(j * SLOT, (j + 1) * SLOT)
        packed[e, 0:16, :] = xs[rows, :HALF]
        packed[e, 16:32, :] = xs[rows, HALF:]
    out_x = copies.start(packed.at[:, 0:32, :], message.at[:, 0:32, :])
    second.wait()
    for j in range(PEERS):
        e = owners[0, j]
        rows = slice(j * SLOT, (j + 1) * SLOT)
        packed[e, 32:48, :] = hs[rows, :HALF]
        packed[e, 48:64, :] = hs[rows, HALF:]
    out_h = copies.start(packed.at[:, 32:72, :], message.at[:, 32:72, :])
    wait(out_x, out_h)


def requested(me, digits):
    tile = digits[...].astype(F32)
    numbers = 32.0 * tile[:, 0:1, :] + tile[:, 1:2, :]
    lane = lax.broadcasted_iota(jnp.int32, (PEERS, SLOT, HALF), 2)
    place = lax.broadcasted_iota(jnp.int32, (PEERS, SLOT, HALF), 1)
    mine = lane == (me % 8) * SLOT + place
    return jnp.sum(jnp.where(mine, numbers, 0.0), axis=2, keepdims=True).reshape(ROWS, 1)


def mask_tiles(occupied, local, edge, local_out, edge_out, flipped_out):
    for i in range(8):
        rows = slice(i * 128, (i + 1) * 128)
        for j in range(8):
            cols = slice(j * 128, (j + 1) * 128)
            part = local[rows, cols]
            local_out[rows, cols] = jnp.where(occupied[i, j] != 0, part, jnp.zeros_like(part))
            part = edge[rows, cols]
            part = jnp.where(occupied[i, 8 + j] != 0, part, jnp.zeros_like(part))
            edge_out[rows, cols] = part
            flipped_out[cols, rows] = part.T


def serve(
    me, message, flipped_far, own_far, reply_far, digits, own_x, own_h, flipped, reply, sem
):
    copies = Copies(sem)
    numbers = copies.start(message.at[:, 64:72, :], digits)
    first = copies.unpack(message, 0, own_x)
    second = copies.unpack(message, 32, own_h)
    third = copies.start(flipped_far, flipped)
    numbers.wait()
    wanted = requested(me[0], digits).astype(jnp.int32)
    wait(*first)
    out = [copies.start(own_x, own_far)]
    wait(*second)
    for rows, peers in steps():
        column = lax.broadcasted_iota(jnp.int32, (STEP, ROWS), 1)
        select = (column == wanted[rows]).astype(BF16)
        put(reply, 0, peers, dot(select, flat(own_x)).astype(BF16))
        put(reply, 64, peers, dot(select, flat(own_h)).astype(BF16))
    third.wait()
    for rows, peers in steps():
        put(reply, 32, peers, dot(flipped[rows, :], flat(own_x)).astype(BF16))
        out.append(copies.start(reply.at[peers], reply_far.at[peers]))
    wait(*out)


def prepare(me, message, local_far, own_far, partial, gather, digits, local, own_x, sem):
    copies = Copies(sem)
    numbers = copies.start(message.at[:, 64:72, :], digits)
    rest = (copies.start(own_far, own_x), copies.start(local_far, local))
    numbers.wait()
    wanted = jnp.broadcast_to(requested(me[0], digits), (ROWS, HALF))
    row = lax.broadcasted_iota(jnp.int32, (ROWS, HALF), 0).astype(F32)
    for a in range(8):
        cols = slice(a * HALF, (a + 1) * HALF)
        gather[:, cols] = (row == wanted[cols].T[0:1, :]).astype(BF16)
    wait(*rest)
    for rows, peers in steps():
        partial[rows, :] = dot(local[rows, :], flat(own_x))


def first_layer(
    message, partial_far, edge_far, gather_far, flipped_far, w_far, bias_far,
    hidden_far, push_far,
    far, pushed, partial, edge, gather, flipped, w, bias, hidden, push, sem,
):
    copies = Copies(sem)
    needed = (*copies.unpack(message, 0, far), *copies.unpack(message, 32, pushed))
    arriving = []
    for rows, peers in steps():
        arriving.append(
            [
                copies.start(whole.at[rows], part.at[rows])
                for whole, part in ((edge_far, edge), (gather_far, gather), (partial_far, partial))
            ]
        )
    small = (copies.start(w_far, w), copies.start(bias_far, bias))
    last = copies.start(flipped_far, flipped)
    wait(*needed)
    for (rows, peers), parts in zip(steps(), arriving):
        wait(*parts)
        total = partial[rows, :] + dot(edge[rows, :], flat(far)) + dot(gather[rows, :], flat(pushed))
        if rows.start == 0:
            wait(*small)
        value = dot(total.astype(BF16), w[...]) + bias[...]
        hidden[rows, :] = jnp.maximum(value, 0.0).astype(BF16)
    last.wait()
    out = [copies.start(hidden, hidden_far)]
    for rows, peers in steps():
        put(push, 0, peers, dot(flipped[rows, :], hidden[...]).astype(BF16))
        out.append(copies.start(push.at[peers], push_far.at[peers]))
    wait(*out)


def second_terms(
    message, local_far, edge_far, hidden_far, partial, far, local, edge, hidden, sem
):
    copies = Copies(sem)
    parts = [
        *copies.unpack(message, 64, far),
        copies.start(local_far, local),
        copies.start(edge_far, edge),
        copies.start(hidden_far, hidden),
    ]
    wait(*parts)
    for rows, peers in steps():
        partial[rows, :] = dot(local[rows, :], hidden[...]) + dot(edge[rows, :], flat(far))


def second_layer(
    message, partial_far, gather_far, cotangent_far,
    aggregate_far, gradient,
    pushed, partial, gather, cotangent, aggregate, sem,
):
    copies = Copies(sem)
    needed = copies.unpack(message, 0, pushed)
    arriving = []
    for rows, peers in steps():
        arriving.append(
            (
                copies.start(gather_far.at[rows], gather.at[rows]),
                copies.start(partial_far.at[rows], partial.at[rows]),
            )
        )
    last = copies.start(cotangent_far, cotangent)
    wait(*needed)
    for (rows, peers), parts in zip(steps(), arriving):
        wait(*parts)
        total = partial[rows, :] + dot(gather[rows, :], flat(pushed))
        aggregate[rows, :] = total.astype(BF16)
    out = copies.start(aggregate, aggregate_far)
    last.wait()
    gradient[...] = lax.dot_general(
        aggregate[...], cotangent[...], (((0,), (0,)), ((), ())), preferred_element_type=F32
    )
    out.wait()


def exchange(message):
    return lax.all_to_all(message, DEV, split_axis=0, concat_axis=0, tiled=True)


def swapped(array, axis, mask):
    return lax.ppermute(array, axis, [(i, i ^ mask) for i in range(lax.axis_size(axis))])


def summed_everywhere(term):
    group = ("dev_0", "dev_1", "rep")
    core = lax.axis_index("dev_2")
    halves = term.reshape(2, F // 2, F)
    kept = lax.dynamic_index_in_dim(halves, core, 0, keepdims=False)
    sent = lax.dynamic_index_in_dim(halves, 1 - core, 0, keepdims=False)
    half = kept + swapped(sent, "dev_2", 1)
    tiles = lax.all_to_all(half[:, None, :], group, split_axis=0, concat_axis=0, tiled=True)
    own = jnp.sum(tiles, axis=0, keepdims=True)
    copies = jnp.broadcast_to(own, (F // 2, 1, F))
    mine = lax.all_to_all(copies, group, split_axis=0, concat_axis=0, tiled=True)[:, 0, :]
    other = swapped(mine, "dev_2", 1)
    first = jnp.where(core == 0, mine, other)
    second = jnp.where(core == 0, other, mine)
    return jnp.concatenate([first, second], axis=0)


def body(
    features,
    history,
    new_owner,
    pull_rows,
    occupancy,
    adj_local,
    adj_boundary,
    w_first,
    bias_first,
    w_second,
    cotangent,
):
    me = lax.axis_index(DEV).astype(jnp.int32).reshape(1)
    wide = 2 * ROWS * ROWS * F
    nodes, square = pltpu.VMEM((ROWS, F), BF16), pltpu.VMEM((ROWS, ROWS), BF16)
    sums, peers = pltpu.VMEM((ROWS, F), F32), pltpu.VMEM((PEERS, SLOT, F), BF16)
    digits = pltpu.VMEM((PEERS, 8, HALF), BF16)
    count = ROWS // STEP

    def letters(rows):
        return pltpu.VMEM((PEERS, rows, HALF), BF16)

    (message,) = call(
        send_clusters,
        "hhhhh",
        (shaped(PEERS, 72, HALF),),
        (new_owner, features, history, pull_rows.reshape(8, 128)),
        own=(
            pltpu.SMEM((1, PEERS), jnp.int32),
            nodes,
            nodes,
            pltpu.VMEM((8, 128), jnp.int32),
            letters(72),
        ),
        copies=6,
        flops=ROWS * F,
        name="send_clusters",
    )
    local, edge, flipped = call(
        mask_tiles,
        "svvvvv",
        (shaped(ROWS, ROWS),) * 3,
        (occupancy, adj_local, adj_boundary),
        flops=wide,
        room=40 << 20,
        name="mask_tiles",
    )
    arrived = exchange(message)
    own_x, reply = call(
        serve,
        "shhhh",
        (shaped(PEERS, SLOT, F), shaped(PEERS, 96, HALF)),
        (me, arrived, flipped),
        own=(digits, peers, peers, square, letters(96)),
        copies=7 + count,
        flops=3 * wide,
        name="serve",
    )
    partial_one, gather = call(
        prepare,
        "shhhvv",
        (shaped(ROWS, F, dtype=F32), shaped(ROWS, ROWS)),
        (me, arrived, local, own_x),
        own=(digits, square, peers),
        copies=3,
        flops=wide,
        name="prepare",
    )
    answers = exchange(reply)
    hidden, push = call(
        first_layer,
        "hhhhhhhhh",
        (shaped(ROWS, F), shaped(PEERS, 32, HALF)),
        (answers, partial_one, edge, gather, flipped, w_first, bias_first.reshape(1, F)),
        own=(
            peers,
            peers,
            sums,
            square,
            square,
            square,
            pltpu.VMEM((F, F), BF16),
            pltpu.VMEM((1, F), F32),
            nodes,
            letters(32),
        ),
        copies=4 * count + 8,
        flops=3 * wide,
        name="first_layer",
    )
    (partial_two,) = call(
        second_terms,
        "hhhhv",
        (shaped(ROWS, F, dtype=F32),),
        (answers, local, edge, hidden),
        own=(peers, square, square, nodes),
        copies=5,
        flops=2 * wide,
        name="second_terms",
    )
    pushed = exchange(push)
    aggregate, term = call(
        second_layer,
        "hhhhhv",
        (shaped(ROWS, F), shaped(F, F, dtype=F32)),
        (pushed, partial_two, gather, cotangent),
        own=(peers, sums, square, nodes, nodes),
        copies=2 * count + 4,
        flops=2 * wide,
        name="second_layer",
    )
    output = jnp.dot(aggregate, w_second, preferred_element_type=F32).astype(BF16)
    return (hidden, output, summed_everywhere(term))


def solution(mesh):
    finer = Mesh(
        mesh.devices.reshape(8, 4, 2, mesh.shape["rep"]), ("dev_0", "dev_1", "dev_2", "rep")
    )
    rows = P(DEV_REP, None)
    return jax.shard_map(
        body,
        mesh=finer,
        in_specs=(rows, rows, rows, P(DEV_REP), rows, rows, rows, P(), P(), P(), rows),
        out_specs=(rows, rows, P()),
        check_vma=False,
    )
```

time: 182 us -> 181 us (level)
  local copies, waits for them, and re-layouts: 31.1 us -> 7.4 us
  Pallas kernels: 13.9 us -> 28.2 us
  blocking collectives: 14 us -> 20.2 us
  waiting for transfers between devices: 80.4 us -> 83.1 us
  starting transfers between devices: 38.9 us -> 36.9 us
    unnamed x54 -> x15, local copies, waits for them, and re-layouts: 30.3 us -> 5.61 us
    pallas_call x7, Pallas kernels: 13.9 us -> 28.2 us  [call(): pl.pallas_call(body, out_shape=outs, in_specs=specs[:len(operands)], out_...]
    all_to_all x1, blocking collectives: 14 us -> 20.2 us  [summed_everywhere(): lax.all_to_all(half[:, None, :], group, split_axis=0, concat_axis=0, tile...]
    ppermute x5 -> x2, starting transfers between devices: 8.8 us -> 3.92 us  [swapped(): lax.ppermute(array, axis, [(i, i ^ mask) for i in range(lax.axis_size(axi...]
    all_to_all x3, waiting for transfers between devices: 67 us -> 70.9 us  [exchange(): return lax.all_to_all(message, DEV, split_axis=0, concat_axis=0, tiled=True)]
    ppermute x5 -> x2, waiting for transfers between devices: 4.09 us -> 0.99 us  [swapped(): lax.ppermute(array, axis, [(i, i ^ mask) for i in range(lax.axis_size(axi...]
    all_to_all x1, starting transfers between devices: 3.86 us -> 6.17 us  [summed_everywhere(): lax.all_to_all(copies, group, split_axis=0, concat_axis=0, tiled=True)]
    all_to_all x1, waiting for transfers between devices: 9.4 us -> 11.2 us  [summed_everywhere(): lax.all_to_all(copies, group, split_axis=0, concat_axis=0, tiled=True)]
  transfers between devices with their start and end apart: 9 -> 6, of which waited for: 7 -> 5; matrix products, arithmetic and copies ran while one was open for 1% -> 1% of each run, Pallas kernels for 3% -> 6%
where the time goes in v2:
time: 181 us
  waiting for transfers between devices  83.1 us (46%)
  starting transfers between devices  36.9 us (20%)
  Pallas kernels  28.2 us (16%)
  blocking collectives  20.2 us (11%)
  local copies, waits for them, and re-layouts  7.4 us (4%)
  matrix products  1.99 us (1%)
  other arithmetic  1.82 us (1%)
    all_to_all x3, waiting for transfers between devices, exchange(): return lax.all_to_all(message, DEV, split_axis=0, concat_axis=0, tiled=True)  70.9 us
    pallas_call x7, Pallas kernels, call(): pl.pallas_call(body, out_shape=outs, in_specs=specs[:len(operands)], out_...  28.2 us
    all_to_all x3, starting transfers between devices, exchange(): return lax.all_to_all(message, DEV, split_axis=0, concat_axis=0, tiled=True)  26.8 us
    all_to_all x1, blocking collectives, summed_everywhere(): lax.all_to_all(half[:, None, :], group, split_axis=0, concat_axis=0, tile...  20.2 us
    all_to_all x1, waiting for transfers between devices, summed_everywhere(): lax.all_to_all(copies, group, split_axis=0, concat_axis=0, tiled=True)  11.2 us
    all_to_all x1, starting transfers between devices, summed_everywhere(): lax.all_to_all(copies, group, split_axis=0, concat_axis=0, tiled=True)  6.17 us
    unnamed x15, local copies, waits for them, and re-layouts  5.61 us
    ppermute x2, starting transfers between devices, swapped(): lax.ppermute(array, axis, [(i, i ^ mask) for i in range(lax.axis_size(axi...  3.92 us
  transfers between devices with their start and end apart: 6, of which 5 were waited for; matrix products, arithmetic and copies ran while one was open for 1% of the time, Pallas kernels for 6%

profile of v2, /device:TPU:1, one launch (start us, length us, event | category | flops | bytes accessed | tf_op | source)
XLA Modules:
  0.0 180.5 jit_solution(6956945654832717914)
XLA Ops:
  0.6 2.3 %send_clusters.1 = bf16[64,72,128]{2,1,0:T(8,128)(2,1)} custom-call(s32[1,64]{1,0:T(1,128)} %owner.1, bf16[1024,256]{1,0:T(8,128)(2,1)} %x.1, bf16[1024,256]{1,0:T(8,128)(2,1)} %h.1, s32[8,128]{1,0:T(8,128)} %bitcast.20), custom_call_target="tpu_custom_call" | custom-call | flops 262144 | bytes 2232576 | tf_op jit(solution)/shard_map/send_clusters/pallas_call | solution.py:27
  2.9 0.0 copy-start.3
  2.9 0.0 copy-start.5
  2.9 13.5 %all-to-all-start = ((bf16[64,72,128]{2,1,0:T(8,128)(2,1)}), bf16[64,72,128]{2,1,0:T(8,128)(2,1)}, u32[]{:S(2)}, u32[]{:S(2)}) async-start(bf16[64,72,128]{2,1,0:T(8,128)(2,1)} %send_clusters.1), calls=%async_computation | async-start | bytes 2359296 | tf_op jit(solution)/shard_map/all_to_all | solution.py:251
  16.4 0.0 copy-done.3
  16.4 0.0 copy-done.5
  16.4 0.0 copy-start.4
  16.4 1.6 copy-done.4
  18.0 2.1 %mask_tiles.1 = (bf16[1024,1024]{1,0:T(8,128)(2,1)S(1)}, bf16[1024,1024]{1,0:T(8,128)(2,1)S(1)}, bf16[1024,1024]{1,0:T(8,128)(2,1)S(1)}) custom-call(s32[8,16]{1,0:T(8,128)S(1)} %copy-done.5, bf16[1024,1024]{1,0:T(8,128)(2,1)S(1)} %copy-done.3, bf16[1024,1024]{1,0:T(8,128)(2,1)S(1)} %copy-done.4), custom_call_target="tpu_custom_call" | custom-call | flops 536870912 | bytes 10486272 | tf_op jit(solution)/shard_map/mask_tiles/pallas_call | solution.py:27
  20.1 0.0 copy-start
  20.1 1.3 copy-done
  21.4 0.0 copy-start.1
  21.4 1.3 copy-done.1
  22.7 0.0 copy-start.2
  22.8 1.4 copy-done.2
  24.1 22.8 %all-to-all-done.message = bf16[64,72,128]{2,1,0:T(8,128)(2,1)} async-done(((bf16[64,72,128]{2,1,0:T(8,128)(2,1)}), bf16[64,72,128]{2,1,0:T(8,128)(2,1)}, u32[]{:S(2)}, u32[]{:S(2)}) %all-to-all-start) | async-done | bytes 1179680 | tf_op jit(solution)/shard_map/all_to_all | solution.py:251
  46.9 4.5 %serve.1 = (bf16[64,16,256]{2,1,0:T(8,128)(2,1)}, bf16[64,96,128]{2,1,0:T(8,128)(2,1)}) custom-call(s32[1]{0:T(128)} %bitcast.me, bf16[64,72,128]{2,1,0:T(8,128)(2,1)} %all-to-all-done.message, bf16[1024,1024]{1,0:T(8,128)(2,1)} %copy-done.2), custom_call_target="tpu_custom_call" | custom-call | flops 1610612736 | bytes 5373956 | tf_op jit(solution)/shard_map/serve/pallas_call | solution.py:27
  51.4 6.8 %all-to-all-start.1 = ((bf16[64,96,128]{2,1,0:T(8,128)(2,1)}), bf16[64,96,128]{2,1,0:T(8,128)(2,1)}, u32[]{:S(2)}, u32[]{:S(2)}) async-start(bf16[64,96,128]{2,1,0:T(8,128)(2,1)} %get-tuple-element.15), calls=%async_computation.1 | async-start | bytes 3145728 | tf_op jit(solution)/shard_map/all_to_all | solution.py:251
  58.2 3.8 %prepare.1 = (f32[1024,256]{1,0:T(8,128)}, bf16[1024,1024]{1,0:T(8,128)(2,1)}) custom-call(s32[1]{0:T(128)} %bitcast.me, bf16[64,72,128]{2,1,0:T(8,128)(2,1)} %all-to-all-done.message, bf16[1024,1024]{1,0:T(8,128)(2,1)} %copy-done.1, bf16[64,16,256]{2,1,0:T(8,128)(2,1)} %get-tuple-element.17.own_far), custom_call_target="tpu_custom_call" | custom-call | flops 536870912 | bytes 6946820 | tf_op jit(solution)/shard_map/prepare/pallas_call | solution.py:27
  62.0 35.2 %all-to-all-done.1.message = bf16[64,96,128]{2,1,0:T(8,128)(2,1)} async-done(((bf16[64,96,128]{2,1,0:T(8,128)(2,1)}), bf16[64,96,128]{2,1,0:T(8,128)(2,1)}, u32[]{:S(2)}, u32[]{:S(2)}) %all-to-all-start.1) | async-done | bytes 1572896 | tf_op jit(solution)/shard_map/all_to_all | solution.py:251
  97.2 6.5 %first_layer.1 = (bf16[1024,256]{1,0:T(8,128)(2,1)}, bf16[64,32,128]{2,1,0:T(8,128)(2,1)}) custom-call(bf16[64,96,128]{2,1,0:T(8,128)(2,1)} %all-to-all-done.1.message, f32[1024,256]{1,0:T(8,128)} %get-tuple-element.18.partial_far, bf16[1024,1024]{1,0:T(8,128)(2,1)} %copy-done, bf16[1024,1024]{1,0:T(8,128)(2,1)} %get-tuple-element.20.gather_far, ...), custom_call_target="tpu_custom_call" | custom-call | flops 1610612736 | bytes 10093568 | tf_op jit(solution)/shard_map/first_layer/pallas_call | solution.py:27
  103.7 6.6 %all-to-all-start.2 = ((bf16[64,32,128]{2,1,0:T(8,128)(2,1)}), bf16[64,32,128]{2,1,0:T(8,128)(2,1)}, u32[]{:S(2)}, u32[]{:S(2)}) async-start(bf16[64,32,128]{2,1,0:T(8,128)(2,1)} %get-tuple-element.22), calls=%async_computation.2 | async-start | bytes 1048576 | tf_op jit(solution)/shard_map/all_to_all | solution.py:251
  110.3 4.7 %second_terms.1.partial_far = f32[1024,256]{1,0:T(8,128)} custom-call(bf16[64,96,128]{2,1,0:T(8,128)(2,1)} %all-to-all-done.1.message, bf16[1024,1024]{1,0:T(8,128)(2,1)} %copy-done.1, bf16[1024,1024]{1,0:T(8,128)(2,1)} %copy-done, bf16[1024,256]{1,0:T(8,128)(2,1)} %get-tuple-element.11.hidden_far), custom_call_target="tpu_custom_call" | custom-call | flops 1073741824 | bytes 7340032 | tf_op jit(solution)/shard_map/second_terms/pallas_call | solution.py:27
  115.1 12.9 %all-to-all-done.2.message = bf16[64,32,128]{2,1,0:T(8,128)(2,1)} async-done(((bf16[64,32,128]{2,1,0:T(8,128)(2,1)}), bf16[64,32,128]{2,1,0:T(8,128)(2,1)}, u32[]{:S(2)}, u32[]{:S(2)}) %all-to-all-start.2) | async-done | bytes 524320 | tf_op jit(solution)/shard_map/all_to_all | solution.py:251
  127.9 4.3 %second_layer.1 = (bf16[1024,256]{1,0:T(8,128)(2,1)}, f32[256,256]{1,0:T(8,128)}) custom-call(bf16[64,32,128]{2,1,0:T(8,128)(2,1)} %all-to-all-done.2.message, f32[1024,256]{1,0:T(8,128)} %second_terms.1.partial_far, bf16[1024,1024]{1,0:T(8,128)(2,1)} %get-tuple-element.20.gather_far, bf16[1024,256]{1,0:T(8,128)(2,1)} %cotangent_far.1), custom_call_target="tpu_custom_call" | custom-call | flops 1073741824 | bytes 4980736 | tf_op jit(solution)/shard_map/second_layer/pallas_call | solution.py:27
  132.3 0.0 copy-start.6
  132.3 1.0 dynamic-slice_bitcast_fusion
  133.3 0.7 collective-permute-start
  133.9 1.0 collective-permute-done
  134.9 0.9 bitcast_add_fusion
  135.8 0.1 broadcast_in_dim.4
  135.9 20.2 %all_to_all.25 = f32[128,1,256]{2,1,0:T(1,128)S(1)} all-to-all(f32[128,1,256]{2,1,0:T(1,128)S(1)} %broadcast_in_dim.4), channel_id=1, replica_groups=mesh['dev_0'=8,'dev_1'=4,'dev_2'=2,'rep'=4] {'dev_0','dev_1','rep'}, dimensions={0} | all-to-all | bytes 262144 | tf_op jit(solution)/shard_map/all_to_all | solution.py:265
  156.2 0.2 reduce_sum.9
  156.3 0.7 broadcast_in_dim.10
  157.1 6.2 %all-to-all-start.4 = ((f32[128,1,256]{2,1,0:T(1,128)}), f32[128,1,256]{2,1,0:T(1,128)S(1)}, u32[]{:S(2)}, u32[]{:S(2)}) async-start(f32[128,1,256]{2,1,0:T(1,128)} %broadcast_in_dim.10), calls=%async_computation.4 | async-start | bytes 262144 | tf_op jit(solution)/shard_map/all_to_all | solution.py:268
  163.2 11.2 %all-to-all-done.4 = f32[128,1,256]{2,1,0:T(1,128)S(1)} async-done(((f32[128,1,256]{2,1,0:T(1,128)}), f32[128,1,256]{2,1,0:T(1,128)S(1)}, u32[]{:S(2)}, u32[]{:S(2)}) %all-to-all-start.4) | async-done | bytes 131104 | tf_op jit(solution)/shard_map/all_to_all | solution.py:268
  174.5 3.3 %collective-permute-start.1 = (f32[128,256]{1,0:T(8,128)S(1)}, f32[128,256]{1,0:T(8,128)S(1)}, u32[]{:S(2)}, u32[]{:S(2)}) collective-permute-start(f32[128,256]{1,0:T(8,128)S(1)} %bitcast.19), channel_id=1, source_target_pairs={{0,4},{4,0},{1,5},{5,1},{2,6},{6,2},{3,7},{7,3},{8,12},{12,8},{9,1... | collective-permute-start | bytes 393224 | tf_op jit(solution)/shard_map/ppermute | solution.py:255
  177.8 0.0 copy-done.6
  177.8 2.0 %convolution_convert_fusion = bf16[1024,256]{1,0:T(8,128)(2,1)} fusion(bf16[1024,256]{1,0:T(8,128)(2,1)S(1)} %copy-done.6, bf16[256,256]{1,0:T(8,128)(2,1)} %param.20), kind=kOutput, calls=%fused_computation | convolution fusion | flops 134479872 | bytes 1179648 | tf_op jit(solution)/shard_map/dot_general | solution.py:387
  179.8 0.0 collective-permute-done.1
  179.8 0.7 pad_maximum_fusion
  (2 shorter events, 0.0 us)
Async XLA Ops:
  2.9 13.5 %copy-start.3 = (bf16[1024,1024]{1,0:T(8,128)(2,1)S(1)}, bf16[1024,1024]{1,0:T(8,128)(2,1)}, u32[]{:S(2)}) copy-start(bf16[1024,1024]{1,0:T(8,128)(2,1)} %local.1) | copy-start | bytes 6291460
  2.9 13.5 %copy-start.5 = (s32[8,16]{1,0:T(8,128)S(1)}, s32[8,16]{1,0:T(8,128)}, u32[]{:S(2)}) copy-start(s32[8,16]{1,0:T(8,128)} %occupied.1) | copy-start | bytes 1540
  2.9 44.0 %all-to-all-start = ((bf16[64,72,128]{2,1,0:T(8,128)(2,1)}), bf16[64,72,128]{2,1,0:T(8,128)(2,1)}, u32[]{:S(2)}, u32[]{:S(2)}) async-start(bf16[64,72,128]{2,1,0:T(8,128)(2,1)} %send_clusters.1), calls=%async_computation | async-start | bytes 2359296 | tf_op jit(solution)/shard_map/all_to_all | solution.py:251
  16.4 1.6 copy-start.4
  20.1 1.3 copy-start
  21.4 1.3 copy-start.1
  22.7 1.4 copy-start.2
  51.4 45.8 %all-to-all-start.1 = ((bf16[64,96,128]{2,1,0:T(8,128)(2,1)}), bf16[64,96,128]{2,1,0:T(8,128)(2,1)}, u32[]{:S(2)}, u32[]{:S(2)}) async-start(bf16[64,96,128]{2,1,0:T(8,128)(2,1)} %get-tuple-element.15), calls=%async_computation.1 | async-start | bytes 3145728 | tf_op jit(solution)/shard_map/all_to_all | solution.py:251
  103.7 24.2 %all-to-all-start.2 = ((bf16[64,32,128]{2,1,0:T(8,128)(2,1)}), bf16[64,32,128]{2,1,0:T(8,128)(2,1)}, u32[]{:S(2)}, u32[]{:S(2)}) async-start(bf16[64,32,128]{2,1,0:T(8,128)(2,1)} %get-tuple-element.22), calls=%async_computation.2 | async-start | bytes 1048576 | tf_op jit(solution)/shard_map/all_to_all | solution.py:251
  132.3 45.5 %copy-start.6 = (bf16[1024,256]{1,0:T(8,128)(2,1)S(1)}, bf16[1024,256]{1,0:T(8,128)(2,1)}, u32[]{:S(2)}) copy-start(bf16[1024,256]{1,0:T(8,128)(2,1)} %get-tuple-element.23) | copy-start | bytes 1572868
  133.3 1.6 collective-permute-start
  157.1 17.4 %all-to-all-start.4 = ((f32[128,1,256]{2,1,0:T(1,128)}), f32[128,1,256]{2,1,0:T(1,128)S(1)}, u32[]{:S(2)}, u32[]{:S(2)}) async-start(f32[128,1,256]{2,1,0:T(1,128)} %broadcast_in_dim.10), calls=%async_computation.4 | async-start | bytes 262144 | tf_op jit(solution)/shard_map/all_to_all | solution.py:268
  174.5 5.3 %collective-permute-start.1 = (f32[128,256]{1,0:T(8,128)S(1)}, f32[128,256]{1,0:T(8,128)S(1)}, u32[]{:S(2)}, u32[]{:S(2)}) collective-permute-start(f32[128,256]{1,0:T(8,128)S(1)} %bitcast.19), channel_id=1, source_target_pairs={{0,4},{4,0},{1,5},{5,1},{2,6},{6,2},{3,7},{7,3},{8,12},{12,8},{9,1... | collective-permute-start | bytes 393224 | tf_op jit(solution)/shard_map/ppermute | solution.py:255

commit v3 on v2

v3 whole, which is shorter than its diff:
```python
import jax
import jax.numpy as jnp
from jax import lax
from jax.experimental import pallas as pl
from jax.experimental.pallas import tpu as pltpu
from jax.sharding import Mesh
from jax.sharding import PartitionSpec as P

CHIPS = ("dev_0", "dev_1")
DEV = ("dev_0", "dev_1", "dev_2")
DEV_REP = ("dev_0", "dev_1", "dev_2", "rep")
PEERS, SLOT, HALF, ROWS, F = 64, 16, 128, 1024, 256
STEP = 512
BANK = {
    "local": slice(0, 1024),
    "edge": slice(1024, 2048),
    "flipped": slice(2048, 3072),
    "gather": slice(3072, 4096),
    "high": slice(4096, 4352),
    "low": slice(4352, 4608),
    "cotangent": slice(4608, 4864),
}
VMEM = 67043328

F32, BF16 = jnp.float32, jnp.bfloat16


def dot(a, b):
    return jnp.dot(a, b, preferred_element_type=F32)


def call(body, kinds, outs, operands, *, own=(), copies=0, flops=0, room=16, alias=None, name=None):
    spaces = {"s": pltpu.SMEM, "v": pltpu.VMEM, "h": pltpu.HBM}
    moved = sum(a.size * a.dtype.itemsize for a in (*operands, *outs))
    arrivals = (pltpu.SemaphoreType.DMA((copies,)),) if copies else ()
    specs = [pl.BlockSpec(memory_space=spaces[k]) for k in kinds]
    return pl.pallas_call(
        body,
        out_shape=outs,
        in_specs=specs[: len(operands)],
        out_specs=tuple(specs[len(operands) :]),
        scratch_shapes=(*own, *arrivals),
        input_output_aliases=alias or {},
        compiler_params=pltpu.CompilerParams(vmem_limit_bytes=VMEM - (room << 20)),
        cost_estimate=pl.CostEstimate(flops=flops, bytes_accessed=moved, transcendentals=0),
        name=name,
    )(*operands)


class Copies:
    def __init__(self, semaphores):
        self.semaphores, self.used = semaphores, 0

    def start(self, source, target):
        copy = pltpu.make_async_copy(source, target, self.semaphores.at[self.used])
        self.used += 1
        copy.start()
        return copy

    def stored(self, source, bank, name):
        return self.start(source, bank.at[:, BANK[name]])


def wait(*copies):
    for copy in copies:
        copy.wait()


def shaped(*dims, dtype=BF16):
    return jax.ShapeDtypeStruct(dims, dtype)


def put(message, at, peers, value):
    count = value.shape[0] // SLOT
    message[peers, at : at + SLOT, :] = value[:, :HALF].reshape(count, SLOT, HALF)
    message[peers, at + SLOT : at + 2 * SLOT, :] = value[:, HALF:].reshape(count, SLOT, HALF)


def steps():
    for at in range(0, ROWS, STEP):
        yield slice(at, at + STEP), slice(at // SLOT, (at + STEP) // SLOT)


def send_clusters(owner, x, h, pulled, message, owners, xs, hs, numbers, packed, sem):
    copies = Copies(sem)
    order = copies.start(owner, owners)
    first = copies.start(x, xs)
    rows_in = copies.start(pulled, numbers)
    second = copies.start(h, hs)
    which = lax.broadcasted_iota(jnp.int32, (8, HALF), 0)
    rows_in.wait()
    for a in range(8):
        line = numbers[a : a + 1, :]
        high = (line // 32).astype(F32)
        low = (line % 32).astype(F32)
        tile = jnp.where(which == 0, high, jnp.where(which == 1, low, 0.0)).astype(BF16)
        for b in range(8):
            packed[a * 8 + b, 64:72, :] = tile
    wait(order, first)
    for j in range(PEERS):
        e = owners[0, j]
        rows = slice(j * SLOT, (j + 1) * SLOT)
        packed[e, 0:16, :] = xs[rows, :HALF]
        packed[e, 16:32, :] = xs[rows, HALF:]
    out_x = copies.start(packed.at[:, 0:32, :], message.at[:, 0:32, :])
    second.wait()
    for j in range(PEERS):
        e = owners[0, j]
        rows = slice(j * SLOT, (j + 1) * SLOT)
        packed[e, 32:48, :] = hs[rows, :HALF]
        packed[e, 48:64, :] = hs[rows, HALF:]
    out_h = copies.start(packed.at[:, 32:72, :], message.at[:, 32:72, :])
    wait(out_x, out_h)


def requested(me, tile):
    tile = tile.astype(F32)
    numbers = 32.0 * tile[:, 0:1, :] + tile[:, 1:2, :]
    lane = lax.broadcasted_iota(jnp.int32, (PEERS, SLOT, HALF), 2)
    place = lax.broadcasted_iota(jnp.int32, (PEERS, SLOT, HALF), 1)
    mine = lane == (me % 8) * SLOT + place
    return jnp.sum(jnp.where(mine, numbers, 0.0), axis=2, keepdims=True).reshape(ROWS, 1)


def take(message, at, into):
    into[:, :HALF] = message[:, at : at + SLOT, :].reshape(ROWS, HALF)
    into[:, HALF:] = message[:, at + SLOT : at + 2 * SLOT, :].reshape(ROWS, HALF)


def mask_tiles(occupied, local_in, edge_in, cotangent, bank, local, edge, flipped, sem):
    copies = Copies(sem)
    out = [copies.stored(cotangent, bank, "cotangent")]
    tiles = [slice(i * 128, (i + 1) * 128) for i in range(8)]
    for i, rows in enumerate(tiles):
        for j, cols in enumerate(tiles):
            part = local_in[rows, cols]
            local[rows, cols] = jnp.where(occupied[i, j] != 0, part, jnp.zeros_like(part))
    out.append(copies.stored(local, bank, "local"))
    for i, rows in enumerate(tiles):
        for j, cols in enumerate(tiles):
            part = edge_in[rows, cols]
            part = jnp.where(occupied[i, 8 + j] != 0, part, jnp.zeros_like(part))
            edge[rows, cols] = part
            flipped[cols, rows] = part.T
    out += [copies.stored(edge, bank, "edge"), copies.stored(flipped, bank, "flipped")]
    wait(*out)


def serve(me, message, bank, own_x, reply_far, own_h, flipped, reply, sem):
    copies = Copies(sem)
    last = copies.start(bank.at[:, BANK["flipped"]], flipped)
    take(message, 0, own_x)
    take(message, 32, own_h)
    wanted = requested(me[0], message[:, 64:72, :]).astype(jnp.int32)
    for rows, peers in steps():
        column = lax.broadcasted_iota(jnp.int32, (STEP, ROWS), 1)
        select = (column == wanted[rows]).astype(BF16)
        put(reply, 0, peers, dot(select, own_x[...]).astype(BF16))
        put(reply, 64, peers, dot(select, own_h[...]).astype(BF16))
    last.wait()
    out = []
    for rows, peers in steps():
        put(reply, 32, peers, dot(flipped[rows, :], own_x[...]).astype(BF16))
        out.append(copies.start(reply.at[peers], reply_far.at[peers]))
    wait(*out)


def prepare(me, message, own_x, bank, bank_out, local, gather, high, low, sem):
    copies = Copies(sem)
    first = copies.start(bank.at[:, BANK["local"]], local)
    wanted = jnp.broadcast_to(requested(me[0], message[:, 64:72, :]), (ROWS, HALF))
    row = lax.broadcasted_iota(jnp.int32, (ROWS, HALF), 0).astype(F32)
    for a in range(8):
        cols = slice(a * HALF, (a + 1) * HALF)
        gather[:, cols] = (row == wanted[cols].T[0:1, :]).astype(BF16)
    out = [copies.stored(gather, bank_out, "gather")]
    first.wait()
    for rows, peers in steps():
        total = dot(local[rows, :], own_x[...])
        high[rows, :] = total.astype(BF16)
        low[rows, :] = (total - high[rows, :].astype(F32)).astype(BF16)
    out += [copies.stored(high, bank_out, "high"), copies.stored(low, bank_out, "low")]
    wait(*out)


def first_layer(
    message, bank, w, bias, hidden_far, push_far,
    far, pushed, edge, gather, high, low, flipped, hidden, push, sem,
):
    copies = Copies(sem)
    into = {"edge": edge, "gather": gather, "high": high, "low": low}
    arriving = [
        [copies.start(bank.at[rows, BANK[name]], ref.at[rows]) for name, ref in into.items()]
        for rows, peers in steps()
    ]
    last = copies.start(bank.at[:, BANK["flipped"]], flipped)
    take(message, 0, far)
    take(message, 32, pushed)
    for (rows, peers), parts in zip(steps(), arriving):
        wait(*parts)
        total = high[rows, :].astype(F32) + low[rows, :].astype(F32)
        total = total + dot(edge[rows, :], far[...]) + dot(gather[rows, :], pushed[...])
        value = dot(total.astype(BF16), w[...]) + bias[...]
        hidden[rows, :] = jnp.maximum(value, 0.0).astype(BF16)
    out = [copies.start(hidden, hidden_far)]
    last.wait()
    for rows, peers in steps():
        put(push, 0, peers, dot(flipped[rows, :], hidden[...]).astype(BF16))
        out.append(copies.start(push.at[peers], push_far.at[peers]))
    wait(*out)


def second_terms(message, hidden, bank, partial, far, local, edge, sem):
    copies = Copies(sem)
    parts = [
        copies.start(bank.at[:, BANK["local"]], local),
        copies.start(bank.at[:, BANK["edge"]], edge),
    ]
    take(message, 64, far)
    wait(*parts)
    for rows, peers in steps():
        partial[rows, :] = dot(local[rows, :], hidden[...]) + dot(edge[rows, :], far[...])


def second_layer(message, partial, bank, aggregate, gradient, pushed, gather, cotangent, sem):
    copies = Copies(sem)
    arriving = [
        copies.start(bank.at[rows, BANK["gather"]], gather.at[rows]) for rows, peers in steps()
    ]
    last = copies.start(bank.at[:, BANK["cotangent"]], cotangent)
    take(message, 0, pushed)
    for (rows, peers), part in zip(steps(), arriving):
        part.wait()
        total = partial[rows, :] + dot(gather[rows, :], pushed[...])
        aggregate[rows, :] = total.astype(BF16)
    last.wait()
    gradient[...] = lax.dot_general(
        aggregate[...], cotangent[...], (((0,), (0,)), ((), ())), preferred_element_type=F32
    )


def exchange(message):
    return lax.all_to_all(message, DEV, split_axis=0, concat_axis=0, tiled=True)


def swapped(array, axis, mask):
    return lax.ppermute(array, axis, [(i, i ^ mask) for i in range(lax.axis_size(axis))])


def summed_everywhere(term):
    core = lax.axis_index("dev_2")
    halves = term.reshape(2, ROWS // 8, F)
    kept = lax.dynamic_index_in_dim(halves, core, 0, keepdims=False)
    sent = lax.dynamic_index_in_dim(halves, 1 - core, 0, keepdims=False)
    half = kept + swapped(sent, "dev_2", 1)
    tiles = lax.all_to_all(half.reshape(32, 4, F), CHIPS, split_axis=0, concat_axis=0, tiled=True)
    own = jnp.sum(tiles, axis=0)
    own = (own + swapped(own, "rep", 1)) + (swapped(own, "rep", 2) + swapped(own, "rep", 3))
    copies = jnp.broadcast_to(own[None], (32, 4, F))
    mine = lax.all_to_all(copies, CHIPS, split_axis=0, concat_axis=0, tiled=True).reshape(128, F)
    other = swapped(mine, "dev_2", 1)
    first = jnp.where(core == 0, mine, other)
    second = jnp.where(core == 0, other, mine)
    return jnp.concatenate([first, second], axis=0)


def body(
    features,
    history,
    new_owner,
    pull_rows,
    occupancy,
    adj_local,
    adj_boundary,
    w_first,
    bias_first,
    w_second,
    cotangent,
):
    me = lax.axis_index(DEV).astype(jnp.int32).reshape(1)
    wide = 2 * ROWS * ROWS * F
    nodes, square = pltpu.VMEM((ROWS, F), BF16), pltpu.VMEM((ROWS, ROWS), BF16)
    count = ROWS // STEP

    def letters(rows):
        return pltpu.VMEM((PEERS, rows, HALF), BF16)

    (message,) = call(
        send_clusters,
        "hhhhh",
        (shaped(PEERS, 72, HALF),),
        (new_owner, features, history, pull_rows.reshape(8, 128)),
        own=(
            pltpu.SMEM((1, PEERS), jnp.int32),
            nodes,
            nodes,
            pltpu.VMEM((8, 128), jnp.int32),
            letters(72),
        ),
        copies=6,
        flops=ROWS * F,
        room=0,
        name="send_clusters",
    )
    (bank,) = call(
        mask_tiles,
        "svvvh",
        (shaped(ROWS, 4864),),
        (occupancy, adj_local, adj_boundary, cotangent),
        own=(square, square, square),
        copies=4,
        flops=wide,
        name="mask_tiles",
    )
    arrived = exchange(message)
    own_x, reply = call(
        serve,
        "svhvh",
        (shaped(ROWS, F), shaped(PEERS, 96, HALF)),
        (me, arrived, bank),
        own=(nodes, square, letters(96)),
        copies=1 + count,
        flops=3 * wide,
        room=12,
        name="serve",
    )
    (bank,) = call(
        prepare,
        "svvhh",
        (shaped(ROWS, 4864),),
        (me, arrived, own_x, bank),
        own=(square, square, nodes, nodes),
        copies=4,
        flops=wide,
        alias={3: 0},
        name="prepare",
    )
    answers = exchange(reply)
    hidden, push = call(
        first_layer,
        "vhvvhh",
        (shaped(ROWS, F), shaped(PEERS, 32, HALF)),
        (answers, bank, w_first, bias_first.reshape(1, F)),
        own=(nodes, nodes, square, square, nodes, nodes, square, nodes, letters(32)),
        copies=5 * count + 2,
        flops=3 * wide,
        name="first_layer",
    )
    (partial_two,) = call(
        second_terms,
        "vvhv",
        (shaped(ROWS, F, dtype=F32),),
        (answers, hidden, bank),
        own=(nodes, square, square),
        copies=2,
        flops=2 * wide,
        name="second_terms",
    )
    pushed = exchange(push)
    aggregate, term = call(
        second_layer,
        "vvhvv",
        (shaped(ROWS, F), shaped(F, F, dtype=F32)),
        (pushed, partial_two, bank),
        own=(nodes, square, nodes),
        copies=count + 1,
        flops=2 * wide,
        name="second_layer",
    )
    output = jnp.dot(aggregate, w_second, preferred_element_type=F32).astype(BF16)
    return (hidden, output, summed_everywhere(term))


def solution(mesh):
    finer = Mesh(
        mesh.devices.reshape(8, 4, 2, mesh.shape["rep"]), ("dev_0", "dev_1", "dev_2", "rep")
    )
    rows = P(DEV_REP, None)
    return jax.shard_map(
        body,
        mesh=finer,
        in_specs=(rows, rows, rows, P(DEV_REP), rows, rows, rows, P(), P(), P(), rows),
        out_specs=(rows, rows, P()),
        check_vma=False,
    )
```

time: 181 us -> 173 us (0.956)
  blocking collectives: 20.2 us -> 14 us
  local copies, waits for them, and re-layouts: 7.4 us -> 5.02 us
  starting transfers between devices: 36.9 us -> 39 us
    all_to_all x1, blocking collectives: 20.2 us -> 14 us  [summed_everywhere(): lax.all_to_all(half.reshape(32, 4, F), CHIPS, split_axis=0, concat_axis=0...]
    ppermute x2 -> x5, starting transfers between devices: 3.92 us -> 8.8 us  [swapped(): lax.ppermute(array, axis, [(i, i ^ mask) for i in range(lax.axis_size(axi...]
    ppermute x2 -> x5, waiting for transfers between devices: 0.99 us -> 4.09 us  [swapped(): lax.ppermute(array, axis, [(i, i ^ mask) for i in range(lax.axis_size(axi...]
    all_to_all x1, starting transfers between devices: 6.17 us -> 3.86 us  [summed_everywhere(): lax.all_to_all(copies, CHIPS, split_axis=0, concat_axis=0, tiled=True)]
    all_to_all x1, waiting for transfers between devices: 11.2 us -> 9.4 us  [summed_everywhere(): lax.all_to_all(copies, CHIPS, split_axis=0, concat_axis=0, tiled=True)]
    unnamed x15 -> x16, local copies, waits for them, and re-layouts: 5.61 us -> 4.25 us
  transfers between devices with their start and end apart: 6 -> 9, of which waited for: 5 -> 7; matrix products, arithmetic and copies ran while one was open for 1% -> 1% of each run, Pallas kernels for 6% -> 7%
where the time goes in v3:
time: 173 us
  waiting for transfers between devices  84.8 us (49%)
  starting transfers between devices  39 us (23%)
  Pallas kernels  27.1 us (16%)
  blocking collectives  14 us (8%)
  local copies, waits for them, and re-layouts  5.02 us (3%)
    all_to_all x3, waiting for transfers between devices, exchange(): return lax.all_to_all(message, DEV, split_axis=0, concat_axis=0, tiled=True)  71.3 us
    pallas_call x7, Pallas kernels, call(): pl.pallas_call(body, out_shape=outs, in_specs=specs[:len(operands)], out_...  27.1 us
    all_to_all x3, starting transfers between devices, exchange(): return lax.all_to_all(message, DEV, split_axis=0, concat_axis=0, tiled=True)  26.3 us
    all_to_all x1, blocking collectives, summed_everywhere(): lax.all_to_all(half.reshape(32, 4, F), CHIPS, split_axis=0, concat_axis=0...  14 us
    all_to_all x1, waiting for transfers between devices, summed_everywhere(): lax.all_to_all(copies, CHIPS, split_axis=0, concat_axis=0, tiled=True)  9.4 us
    ppermute x5, starting transfers between devices, swapped(): lax.ppermute(array, axis, [(i, i ^ mask) for i in range(lax.axis_size(axi...  8.8 us
    unnamed x16, local copies, waits for them, and re-layouts  4.25 us
    ppermute x5, waiting for transfers between devices, swapped(): lax.ppermute(array, axis, [(i, i ^ mask) for i in range(lax.axis_size(axi...  4.09 us
  transfers between devices with their start and end apart: 9, of which 7 were waited for; matrix products, arithmetic and copies ran while one was open for 1% of the time, Pallas kernels for 7%

profile of v3, /device:TPU:1, one launch (start us, length us, event | category | flops | bytes accessed | tf_op | source)
XLA Modules:
  0.0 172.6 jit_solution(3402453756175526798)
XLA Ops:
  0.6 2.3 %send_clusters.1 = bf16[64,72,128]{2,1,0:T(8,128)(2,1)} custom-call(s32[1,64]{1,0:T(1,128)} %owner.1, bf16[1024,256]{1,0:T(8,128)(2,1)} %x.1, bf16[1024,256]{1,0:T(8,128)(2,1)} %h.1, s32[8,128]{1,0:T(8,128)} %bitcast.13), custom_call_target="tpu_custom_call" | custom-call | flops 262144 | bytes 2232576 | tf_op jit(solution)/shard_map/send_clusters/pallas_call | solution.py:37
  2.9 0.0 copy-start.2
  2.9 0.0 copy-start.5
  3.0 13.3 %all-to-all-start = ((bf16[64,72,128]{2,1,0:T(8,128)(2,1)}), bf16[64,72,128]{2,1,0:T(8,128)(2,1)S(1)}, u32[]{:S(2)}, u32[]{:S(2)}) async-start(bf16[64,72,128]{2,1,0:T(8,128)(2,1)} %send_clusters.1), calls=%async_computation | async-start | bytes 2359296 | tf_op jit(solution)/shard_map/all_to_all | solution.py:243
  16.3 0.0 copy-done.2
  16.3 0.0 copy-done.5
  16.3 0.0 copy-start
  16.3 1.6 copy-done
  17.9 0.0 copy-start.1
  17.9 1.6 copy-done.1
  19.5 4.8 %mask_tiles.1.bank = bf16[1024,4864]{1,0:T(8,128)(2,1)} custom-call(s32[8,16]{1,0:T(8,128)S(1)} %copy-done.5, bf16[1024,1024]{1,0:T(8,128)(2,1)S(1)} %copy-done, bf16[1024,1024]{1,0:T(8,128)(2,1)S(1)} %copy-done.1, bf16[1024,256]{1,0:T(8,128)(2,1)S(1)} %copy-done.2), custom_call_target="tpu_custom_call" | custom-call | flops 536870912 | bytes 14680576 | tf_op jit(solution)/shard_map/mask_tiles/pallas_call | solution.py:37
  24.2 22.6 %all-to-all-done.message = bf16[64,72,128]{2,1,0:T(8,128)(2,1)S(1)} async-done(((bf16[64,72,128]{2,1,0:T(8,128)(2,1)}), bf16[64,72,128]{2,1,0:T(8,128)(2,1)S(1)}, u32[]{:S(2)}, u32[]{:S(2)}) %all-to-all-start) | async-done | bytes 1179680 | tf_op jit(solution)/shard_map/all_to_all | solution.py:243
  46.9 4.1 %serve.1 = (bf16[1024,256]{1,0:T(8,128)(2,1)S(1)}, bf16[64,96,128]{2,1,0:T(8,128)(2,1)}) custom-call(s32[1]{0:T(128)} %bitcast.me, bf16[64,72,128]{2,1,0:T(8,128)(2,1)S(1)} %all-to-all-done.message, bf16[1024,4864]{1,0:T(8,128)(2,1)} %mask_tiles.1.bank), custom_call_target="tpu_custom_call" | custom-call | flops 1610612736 | bytes 13238276 | tf_op jit(solution)/shard_map/serve/pallas_call | solution.py:37
  51.0 6.6 %all-to-all-start.1 = ((bf16[64,96,128]{2,1,0:T(8,128)(2,1)}), bf16[64,96,128]{2,1,0:T(8,128)(2,1)S(1)}, u32[]{:S(2)}, u32[]{:S(2)}) async-start(bf16[64,96,128]{2,1,0:T(8,128)(2,1)} %get-tuple-element.9), calls=%async_computation.1 | async-start | bytes 3145728 | tf_op jit(solution)/shard_map/all_to_all | solution.py:243
  57.6 0.0 copy-start.4
  57.6 0.0 copy-start.6
  57.7 3.5 %prepare.1.bank = bf16[1024,4864]{1,0:T(8,128)(2,1)} custom-call(s32[1]{0:T(128)} %bitcast.me, bf16[64,72,128]{2,1,0:T(8,128)(2,1)S(1)} %all-to-all-done.message, bf16[1024,256]{1,0:T(8,128)(2,1)S(1)} %get-tuple-element.10.own_x, bf16[1024,4864]{1,0:T(8,128)(2,1)} %mask_tiles.1.bank), custom_call_target="tpu_custom_call", output_to_operand_aliasing={{}: (3, {})} | custom-call | flops 536870912 | bytes 21626884 | tf_op jit(solution)/shard_map/prepare/pallas_call | solution.py:37
  61.2 35.5 %all-to-all-done.1.message = bf16[64,96,128]{2,1,0:T(8,128)(2,1)S(1)} async-done(((bf16[64,96,128]{2,1,0:T(8,128)(2,1)}), bf16[64,96,128]{2,1,0:T(8,128)(2,1)S(1)}, u32[]{:S(2)}, u32[]{:S(2)}) %all-to-all-start.1) | async-done | bytes 1572896 | tf_op jit(solution)/shard_map/all_to_all | solution.py:243
  96.7 0.0 copy-done.4
  96.7 0.0 copy-done.6
  96.7 6.0 %first_layer.1 = (bf16[1024,256]{1,0:T(8,128)(2,1)}, bf16[64,32,128]{2,1,0:T(8,128)(2,1)}) custom-call(bf16[64,96,128]{2,1,0:T(8,128)(2,1)S(1)} %all-to-all-done.1.message, bf16[1024,4864]{1,0:T(8,128)(2,1)} %prepare.1.bank, bf16[256,256]{1,0:T(8,128)(2,1)S(1)} %copy-done.4, f32[1,256]{1,0:T(1,128)S(1)} %bitcast.12), custom_call_target="tpu_custom_call" | custom-call | flops 1610612736 | bytes 12715008 | tf_op jit(solution)/shard_map/first_layer/pallas_call | solution.py:37
  102.7 6.4 %all-to-all-start.2 = ((bf16[64,32,128]{2,1,0:T(8,128)(2,1)}), bf16[64,32,128]{2,1,0:T(8,128)(2,1)S(1)}, u32[]{:S(2)}, u32[]{:S(2)}) async-start(bf16[64,32,128]{2,1,0:T(8,128)(2,1)} %get-tuple-element.12), calls=%async_computation.2 | async-start | bytes 1048576 | tf_op jit(solution)/shard_map/all_to_all | solution.py:243
  109.1 0.0 copy-start.3
  109.1 1.0 copy-done.3
  110.2 3.5 %second_terms.1.partial = f32[1024,256]{1,0:T(8,128)S(1)} custom-call(bf16[64,96,128]{2,1,0:T(8,128)(2,1)S(1)} %all-to-all-done.1.message, bf16[1024,256]{1,0:T(8,128)(2,1)S(1)} %copy-done.3, bf16[1024,4864]{1,0:T(8,128)(2,1)} %prepare.1.bank), custom_call_target="tpu_custom_call" | custom-call | flops 1073741824 | bytes 13107200 | tf_op jit(solution)/shard_map/second_terms/pallas_call | solution.py:37
  113.7 13.1 %all-to-all-done.2.message = bf16[64,32,128]{2,1,0:T(8,128)(2,1)S(1)} async-done(((bf16[64,32,128]{2,1,0:T(8,128)(2,1)}), bf16[64,32,128]{2,1,0:T(8,128)(2,1)S(1)}, u32[]{:S(2)}, u32[]{:S(2)}) %all-to-all-start.2) | async-done | bytes 524320 | tf_op jit(solution)/shard_map/all_to_all | solution.py:243
  126.8 2.9 %second_layer.1 = (bf16[1024,256]{1,0:T(8,128)(2,1)S(1)}, f32[256,256]{1,0:T(8,128)S(1)}) custom-call(bf16[64,32,128]{2,1,0:T(8,128)(2,1)S(1)} %all-to-all-done.2.message, f32[1024,256]{1,0:T(8,128)S(1)} %second_terms.1.partial, bf16[1024,4864]{1,0:T(8,128)(2,1)} %prepare.1.bank), custom_call_target="tpu_custom_call" | custom-call | flops 1073741824 | bytes 12320768 | tf_op jit(solution)/shard_map/second_layer/pallas_call | solution.py:37
  129.8 0.0 copy-start.7
  129.8 0.7 collective-permute-start
  130.5 1.0 collective-permute-done
  131.5 14.0 %all_to_all.25 = f32[32,4,256]{2,1,0:T(4,128)S(1)} all-to-all(f32[32,4,256]{2,1,0:T(4,128)S(1)} %reshape.29), channel_id=1, replica_groups=mesh['dev_0'=8,'dev_1'=4,'dev_2'=2,'rep'=4] {'dev_0','dev_1'}, dimensions={0} | all-to-all | bytes 262144 | tf_op jit(solution)/shard_map/all_to_all | solution.py:256
  145.6 2.8 %collective-permute-start.2 = (f32[4,256]{1,0:T(4,128)S(1)}, f32[4,256]{1,0:T(4,128)S(1)}, u32[]{:S(2)}, u32[]{:S(2)}) collective-permute-start(f32[4,256]{1,0:T(4,128)S(1)} %reduce_sum.9), channel_id=1, source_target_pairs={{0,2},{1,3},{2,0},{3,1},{4,6},{5,7},{6,4},{7,5},{8,10},{9,11},{10,... | collective-permute-start | bytes 12296 | tf_op jit(solution)/shard_map/ppermute | solution.py:247
  148.4 0.9 collective-permute-start.3
  149.2 0.0 collective-permute-start.1
  149.2 0.4 collective-permute-done.2
  149.6 2.7 %collective-permute-done.3 = f32[4,256]{1,0:T(4,128)S(1)} collective-permute-done((f32[4,256]{1,0:T(4,128)S(1)}, f32[4,256]{1,0:T(4,128)S(1)}, u32[]{:S(2)}, u32[]{:S(2)}) %collective-permute-start.3) | collective-permute-done | bytes 4128 | tf_op jit(solution)/shard_map/ppermute | solution.py:247
  152.3 0.0 collective-permute-done.1
  152.4 0.7 broadcast_in_dim.2
  153.0 3.9 %all-to-all-start.4 = ((f32[32,4,256]{2,1,0:T(4,128)}), f32[32,4,256]{2,1,0:T(4,128)S(1)}, u32[]{:S(2)}, u32[]{:S(2)}) async-start(f32[32,4,256]{2,1,0:T(4,128)} %broadcast_in_dim.2), calls=%async_computation.4 | async-start | bytes 262144 | tf_op jit(solution)/shard_map/all_to_all | solution.py:260
  156.9 9.4 %all-to-all-done.4 = f32[32,4,256]{2,1,0:T(4,128)S(1)} async-done(((f32[32,4,256]{2,1,0:T(4,128)}), f32[32,4,256]{2,1,0:T(4,128)S(1)}, u32[]{:S(2)}, u32[]{:S(2)}) %all-to-all-start.4) | async-done | bytes 131104 | tf_op jit(solution)/shard_map/all_to_all | solution.py:260
  166.4 4.5 %collective-permute-start.4 = (f32[128,256]{1,0:T(8,128)S(1)}, f32[128,256]{1,0:T(8,128)S(1)}, u32[]{:S(2)}, u32[]{:S(2)}) collective-permute-start(f32[128,256]{1,0:T(8,128)S(1)} %reshape.30), channel_id=1, source_target_pairs={{0,4},{4,0},{1,5},{5,1},{2,6},{6,2},{3,7},{7,3},{8,12},{12,8},{9,1... | collective-permute-start | bytes 393224 | tf_op jit(solution)/shard_map/ppermute | solution.py:247
  170.8 0.0 copy-done.7
  170.8 1.1 convolution_convert_fusion
  171.9 0.0 collective-permute-done.4
  171.9 0.7 pad_maximum_fusion
  (7 shorter events, 0.2 us)
Async XLA Ops:
  2.9 13.3 %copy-start.2 = (bf16[1024,256]{1,0:T(8,128)(2,1)S(1)}, bf16[1024,256]{1,0:T(8,128)(2,1)}, u32[]{:S(2)}) copy-start(bf16[1024,256]{1,0:T(8,128)(2,1)} %cotangent.1) | copy-start | bytes 1572868
  2.9 13.3 %copy-start.5 = (s32[8,16]{1,0:T(8,128)S(1)}, s32[8,16]{1,0:T(8,128)}, u32[]{:S(2)}) copy-start(s32[8,16]{1,0:T(8,128)} %occupied.1) | copy-start | bytes 1540
  3.0 43.9 %all-to-all-start = ((bf16[64,72,128]{2,1,0:T(8,128)(2,1)}), bf16[64,72,128]{2,1,0:T(8,128)(2,1)S(1)}, u32[]{:S(2)}, u32[]{:S(2)}) async-start(bf16[64,72,128]{2,1,0:T(8,128)(2,1)} %send_clusters.1), calls=%async_computation | async-start | bytes 2359296 | tf_op jit(solution)/shard_map/all_to_all | solution.py:243
  16.3 1.6 copy-start
  17.9 1.6 copy-start.1
  51.0 45.7 %all-to-all-start.1 = ((bf16[64,96,128]{2,1,0:T(8,128)(2,1)}), bf16[64,96,128]{2,1,0:T(8,128)(2,1)S(1)}, u32[]{:S(2)}, u32[]{:S(2)}) async-start(bf16[64,96,128]{2,1,0:T(8,128)(2,1)} %get-tuple-element.9), calls=%async_computation.1 | async-start | bytes 3145728 | tf_op jit(solution)/shard_map/all_to_all | solution.py:243
  57.6 39.1 %copy-start.4 = (bf16[256,256]{1,0:T(8,128)(2,1)S(1)}, bf16[256,256]{1,0:T(8,128)(2,1)}, u32[]{:S(2)}) copy-start(bf16[256,256]{1,0:T(8,128)(2,1)} %w.1) | copy-start | bytes 393220
  57.6 39.1 %copy-start.6 = (f32[256]{0:T(256)S(1)}, f32[256]{0:T(256)}, u32[]{:S(2)}) copy-start(f32[256]{0:T(256)} %param.19) | copy-start | bytes 3076
  102.7 24.1 %all-to-all-start.2 = ((bf16[64,32,128]{2,1,0:T(8,128)(2,1)}), bf16[64,32,128]{2,1,0:T(8,128)(2,1)S(1)}, u32[]{:S(2)}, u32[]{:S(2)}) async-start(bf16[64,32,128]{2,1,0:T(8,128)(2,1)} %get-tuple-element.12), calls=%async_computation.2 | async-start | bytes 1048576 | tf_op jit(solution)/shard_map/all_to_all | solution.py:243
  109.1 1.0 copy-start.3
  129.8 41.1 %copy-start.7 = (bf16[256,256]{1,0:T(8,128)(2,1)S(1)}, bf16[256,256]{1,0:T(8,128)(2,1)}, u32[]{:S(2)}) copy-start(bf16[256,256]{1,0:T(8,128)(2,1)} %param.20) | copy-start | bytes 393220
  129.8 1.6 collective-permute-start
  145.6 4.0 %collective-permute-start.2 = (f32[4,256]{1,0:T(4,128)S(1)}, f32[4,256]{1,0:T(4,128)S(1)}, u32[]{:S(2)}, u32[]{:S(2)}) collective-permute-start(f32[4,256]{1,0:T(4,128)S(1)} %reduce_sum.9), channel_id=1, source_target_pairs={{0,2},{1,3},{2,0},{3,1},{4,6},{5,7},{6,4},{7,5},{8,10},{9,11},{10,... | collective-permute-start | bytes 12296 | tf_op jit(solution)/shard_map/ppermute | solution.py:247
  148.4 4.0 %collective-permute-start.3 = (f32[4,256]{1,0:T(4,128)S(1)}, f32[4,256]{1,0:T(4,128)S(1)}, u32[]{:S(2)}, u32[]{:S(2)}) collective-permute-start(f32[4,256]{1,0:T(4,128)S(1)} %reduce_sum.9), channel_id=1, source_target_pairs={{0,3},{1,2},{2,1},{3,0},{4,7},{5,6},{6,5},{7,4},{8,11},{9,10},{10,... | collective-permute-start | bytes 12296 | tf_op jit(solution)/shard_map/ppermute | solution.py:247
  149.2 3.1 %collective-permute-start.1 = (f32[4,256]{1,0:T(4,128)S(1)}, f32[4,256]{1,0:T(4,128)S(1)}, u32[]{:S(2)}, u32[]{:S(2)}) collective-permute-start(f32[4,256]{1,0:T(4,128)S(1)} %reduce_sum.9), channel_id=1, source_target_pairs={{0,1},{1,0},{2,3},{3,2},{4,5},{5,4},{6,7},{7,6},{8,9},{9,8},{10,11... | collective-permute-start | bytes 12296 | tf_op jit(solution)/shard_map/ppermute | solution.py:247
  153.0 13.3 %all-to-all-start.4 = ((f32[32,4,256]{2,1,0:T(4,128)}), f32[32,4,256]{2,1,0:T(4,128)S(1)}, u32[]{:S(2)}, u32[]{:S(2)}) async-start(f32[32,4,256]{2,1,0:T(4,128)} %broadcast_in_dim.2), calls=%async_computation.4 | async-start | bytes 262144 | tf_op jit(solution)/shard_map/all_to_all | solution.py:260
  166.4 5.5 %collective-permute-start.4 = (f32[128,256]{1,0:T(8,128)S(1)}, f32[128,256]{1,0:T(8,128)S(1)}, u32[]{:S(2)}, u32[]{:S(2)}) collective-permute-start(f32[128,256]{1,0:T(8,128)S(1)} %reshape.30), channel_id=1, source_target_pairs={{0,4},{4,0},{1,5},{5,1},{2,6},{6,2},{3,7},{7,3},{8,12},{12,8},{9,1... | collective-permute-start | bytes 393224 | tf_op jit(solution)/shard_map/ppermute | solution.py:247

commit v4 on v3

--- a/solution.py
+++ b/solution.py
@@ -8,6 +8,7 @@
 
 CHIPS = ("dev_0", "dev_1")
 DEV = ("dev_0", "dev_1", "dev_2")
+ORDER = ("dev_2", "dev_0", "dev_1")
 DEV_REP = ("dev_0", "dev_1", "dev_2", "rep")
 PEERS, SLOT, HALF, ROWS, F = 64, 16, 128, 1024, 256
 STEP = 512
@@ -15,11 +16,11 @@
     "local": slice(0, 1024),
     "edge": slice(1024, 2048),
     "flipped": slice(2048, 3072),
-    "gather": slice(3072, 4096),
-    "high": slice(4096, 4352),
-    "low": slice(4352, 4608),
-    "cotangent": slice(4608, 4864),
+    "high": slice(3072, 3328),
+    "low": slice(3328, 3584),
+    "cotangent": slice(3584, 3840),
 }
+WIDTH = 3840
 VMEM = 67043328
 
 F32, BF16 = jnp.float32, jnp.bfloat16
@@ -70,15 +71,31 @@
     return jax.ShapeDtypeStruct(dims, dtype)
 
 
+def place(e):
+    return (e & 1) * (PEERS // 2) + (e >> 1)
+
+
 def put(message, at, peers, value):
     count = value.shape[0] // SLOT
     message[peers, at : at + SLOT, :] = value[:, :HALF].reshape(count, SLOT, HALF)
     message[peers, at + SLOT : at + 2 * SLOT, :] = value[:, HALF:].reshape(count, SLOT, HALF)
 
 
-def steps():
-    for at in range(0, ROWS, STEP):
-        yield slice(at, at + STEP), slice(at // SLOT, (at + STEP) // SLOT)
+def put_by_owner(message, at, peers, value):
+    for i, e in enumerate(range(peers.start, peers.stop)):
+        block = value[i * SLOT : (i + 1) * SLOT]
+        message[place(e), at : at + SLOT, :] = block[:, :HALF]
+        message[place(e), at + SLOT : at + 2 * SLOT, :] = block[:, HALF:]
+
+
+def places(peers):
+    for core in range(2):
+        yield slice(place(peers.start + core), place(peers.stop - 2 + core) + 1)
+
+
+def steps(step=STEP):
+    for at in range(0, ROWS, step):
+        yield slice(at, at + step), slice(at // SLOT, (at + step) // SLOT)
 
 
 def send_clusters(owner, x, h, pulled, message, owners, xs, hs, numbers, packed, sem):
@@ -95,17 +112,17 @@
         low = (line % 32).astype(F32)
         tile = jnp.where(which == 0, high, jnp.where(which == 1, low, 0.0)).astype(BF16)
         for b in range(8):
-            packed[a * 8 + b, 64:72, :] = tile
+            packed[place(a * 8 + b), 64:72, :] = tile
     wait(order, first)
     for j in range(PEERS):
-        e = owners[0, j]
+        e = place(owners[0, j])
         rows = slice(j * SLOT, (j + 1) * SLOT)
         packed[e, 0:16, :] = xs[rows, :HALF]
         packed[e, 16:32, :] = xs[rows, HALF:]
     out_x = copies.start(packed.at[:, 0:32, :], message.at[:, 0:32, :])
     second.wait()
     for j in range(PEERS):
-        e = owners[0, j]
+        e = place(owners[0, j])
         rows = slice(j * SLOT, (j + 1) * SLOT)
         packed[e, 32:48, :] = hs[rows, :HALF]
         packed[e, 48:64, :] = hs[rows, HALF:]
@@ -125,6 +142,19 @@
 def take(message, at, into):
     into[:, :HALF] = message[:, at : at + SLOT, :].reshape(ROWS, HALF)
     into[:, HALF:] = message[:, at + SLOT : at + 2 * SLOT, :].reshape(ROWS, HALF)
+
+
+def take_by_owner(message, at, into):
+    for e in range(PEERS):
+        rows = slice(e * SLOT, (e + 1) * SLOT)
+        into[rows, :HALF] = message[place(e), at : at + SLOT, :]
+        into[rows, HALF:] = message[place(e), at + SLOT : at + 2 * SLOT, :]
+
+
+def collector(numbers, gather, rows):
+    row = lax.broadcasted_iota(jnp.int32, (STEP, HALF), 0).astype(F32) + float(rows.start)
+    for a in range(8):
+        gather[:, a * HALF : (a + 1) * HALF] = (row == numbers[a : a + 1, :]).astype(BF16)
 
 
 def mask_tiles(occupied, local_in, edge_in, cotangent, bank, local, edge, flipped, sem):
@@ -148,65 +178,71 @@
 
 def serve(me, message, bank, own_x, reply_far, own_h, flipped, reply, sem):
     copies = Copies(sem)
-    last = copies.start(bank.at[:, BANK["flipped"]], flipped)
-    take(message, 0, own_x)
-    take(message, 32, own_h)
+    arriving = [
+        copies.start(bank.at[rows, BANK["flipped"]], flipped.at[rows]) for rows, peers in steps()
+    ]
+    take_by_owner(message, 0, own_x)
+    take_by_owner(message, 32, own_h)
     wanted = requested(me[0], message[:, 64:72, :]).astype(jnp.int32)
+    out = []
     for rows, peers in steps():
         column = lax.broadcasted_iota(jnp.int32, (STEP, ROWS), 1)
         select = (column == wanted[rows]).astype(BF16)
         put(reply, 0, peers, dot(select, own_x[...]).astype(BF16))
-        put(reply, 64, peers, dot(select, own_h[...]).astype(BF16))
-    last.wait()
-    out = []
-    for rows, peers in steps():
-        put(reply, 32, peers, dot(flipped[rows, :], own_x[...]).astype(BF16))
-        out.append(copies.start(reply.at[peers], reply_far.at[peers]))
+        put(reply, 32, peers, dot(select, own_h[...]).astype(BF16))
+        out.append(copies.start(reply.at[peers, 0:64], reply_far.at[peers, 0:64]))
+    wait(*arriving)
+    for rows, peers in steps(STEP // 2):
+        put_by_owner(reply, 64, peers, dot(flipped[rows, :], own_x[...]).astype(BF16))
+        for part in places(peers):
+            out.append(copies.start(reply.at[part, 64:96], reply_far.at[part, 64:96]))
     wait(*out)
 
 
-def prepare(me, message, own_x, bank, bank_out, local, gather, high, low, sem):
+def prepare(me, message, own_x, bank, bank_out, numbers, local, high, low, sem):
     copies = Copies(sem)
     first = copies.start(bank.at[:, BANK["local"]], local)
     wanted = jnp.broadcast_to(requested(me[0], message[:, 64:72, :]), (ROWS, HALF))
-    row = lax.broadcasted_iota(jnp.int32, (ROWS, HALF), 0).astype(F32)
     for a in range(8):
-        cols = slice(a * HALF, (a + 1) * HALF)
-        gather[:, cols] = (row == wanted[cols].T[0:1, :]).astype(BF16)
-    out = [copies.stored(gather, bank_out, "gather")]
+        numbers[a : a + 1, :] = wanted[a * HALF : (a + 1) * HALF].T[0:1, :]
     first.wait()
     for rows, peers in steps():
         total = dot(local[rows, :], own_x[...])
         high[rows, :] = total.astype(BF16)
         low[rows, :] = (total - high[rows, :].astype(F32)).astype(BF16)
-    out += [copies.stored(high, bank_out, "high"), copies.stored(low, bank_out, "low")]
-    wait(*out)
+    wait(copies.stored(high, bank_out, "high"), copies.stored(low, bank_out, "low"))
 
 
 def first_layer(
-    message, bank, w, bias, hidden_far, push_far,
-    far, pushed, edge, gather, high, low, flipped, hidden, push, sem,
+    message, bank, numbers, w, bias, hidden_far, push_far,
+    far, pushed, edge, gather, high, low, sums, flipped, hidden, push, sem,
 ):
     copies = Copies(sem)
-    into = {"edge": edge, "gather": gather, "high": high, "low": low}
+    into = {"edge": edge, "high": high, "low": low}
     arriving = [
         [copies.start(bank.at[rows, BANK[name]], ref.at[rows]) for name, ref in into.items()]
         for rows, peers in steps()
     ]
-    last = copies.start(bank.at[:, BANK["flipped"]], flipped)
-    take(message, 0, far)
-    take(message, 32, pushed)
+    last = [
+        copies.start(bank.at[rows, BANK["flipped"]], flipped.at[rows]) for rows, peers in steps()
+    ]
+    take(message, 64, pushed)
+    for rows, peers in steps():
+        collector(numbers, gather, rows)
+        sums[rows, :] = dot(gather[...], pushed[...])
+    take_by_owner(message, 0, far)
     for (rows, peers), parts in zip(steps(), arriving):
         wait(*parts)
-        total = high[rows, :].astype(F32) + low[rows, :].astype(F32)
-        total = total + dot(edge[rows, :], far[...]) + dot(gather[rows, :], pushed[...])
+        total = sums[rows, :] + high[rows, :].astype(F32) + low[rows, :].astype(F32)
+        total = total + dot(edge[rows, :], far[...])
         value = dot(total.astype(BF16), w[...]) + bias[...]
         hidden[rows, :] = jnp.maximum(value, 0.0).astype(BF16)
     out = [copies.start(hidden, hidden_far)]
-    last.wait()
-    for rows, peers in steps():
-        put(push, 0, peers, dot(flipped[rows, :], hidden[...]).astype(BF16))
-        out.append(copies.start(push.at[peers], push_far.at[peers]))
+    wait(*last)
+    for rows, peers in steps(STEP // 2):
+        put_by_owner(push, 0, peers, dot(flipped[rows, :], hidden[...]).astype(BF16))
+        for part in places(peers):
+            out.append(copies.start(push.at[part], push_far.at[part]))
     wait(*out)
 
 
@@ -216,22 +252,19 @@
         copies.start(bank.at[:, BANK["local"]], local),
         copies.start(bank.at[:, BANK["edge"]], edge),
     ]
-    take(message, 64, far)
+    take_by_owner(message, 32, far)
     wait(*parts)
     for rows, peers in steps():
         partial[rows, :] = dot(local[rows, :], hidden[...]) + dot(edge[rows, :], far[...])
 
 
-def second_layer(message, partial, bank, aggregate, gradient, pushed, gather, cotangent, sem):
-    copies = Copies(sem)
-    arriving = [
-        copies.start(bank.at[rows, BANK["gather"]], gather.at[rows]) for rows, peers in steps()
-    ]
+def second_layer(message, partial, bank, numbers, aggregate, gradient, pushed, gather, cotangent, sem):
+    copies = Copies(sem)
     last = copies.start(bank.at[:, BANK["cotangent"]], cotangent)
     take(message, 0, pushed)
-    for (rows, peers), part in zip(steps(), arriving):
-        part.wait()
-        total = partial[rows, :] + dot(gather[rows, :], pushed[...])
+    for rows, peers in steps():
+        collector(numbers, gather, rows)
+        total = partial[rows, :] + dot(gather[...], pushed[...])
         aggregate[rows, :] = total.astype(BF16)
     last.wait()
     gradient[...] = lax.dot_general(
@@ -240,7 +273,7 @@
 
 
 def exchange(message):
-    return lax.all_to_all(message, DEV, split_axis=0, concat_axis=0, tiled=True)
+    return lax.all_to_all(message, ORDER, split_axis=0, concat_axis=0, tiled=True)
 
 
 def swapped(array, axis, mask):
@@ -305,7 +338,7 @@
     (bank,) = call(
         mask_tiles,
         "svvvh",
-        (shaped(ROWS, 4864),),
+        (shaped(ROWS, WIDTH),),
         (occupancy, adj_local, adj_boundary, cotangent),
         own=(square, square, square),
         copies=4,
@@ -313,24 +346,25 @@
         name="mask_tiles",
     )
     arrived = exchange(message)
+    half = pltpu.VMEM((STEP, ROWS), BF16)
     own_x, reply = call(
         serve,
         "svhvh",
         (shaped(ROWS, F), shaped(PEERS, 96, HALF)),
         (me, arrived, bank),
         own=(nodes, square, letters(96)),
-        copies=1 + count,
+        copies=6 * count,
         flops=3 * wide,
         room=12,
         name="serve",
     )
-    (bank,) = call(
+    bank, numbers = call(
         prepare,
-        "svvhh",
-        (shaped(ROWS, 4864),),
+        "svvhhv",
+        (shaped(ROWS, WIDTH), shaped(8, HALF, dtype=F32)),
         (me, arrived, own_x, bank),
-        own=(square, square, nodes, nodes),
-        copies=4,
+        own=(square, nodes, nodes),
+        copies=3,
         flops=wide,
         alias={3: 0},
         name="prepare",
@@ -338,11 +372,22 @@
     answers = exchange(reply)
     hidden, push = call(
         first_layer,
-        "vhvvhh",
+        "vhvvvhh",
         (shaped(ROWS, F), shaped(PEERS, 32, HALF)),
-        (answers, bank, w_first, bias_first.reshape(1, F)),
-        own=(nodes, nodes, square, square, nodes, nodes, square, nodes, letters(32)),
-        copies=5 * count + 2,
+        (answers, bank, numbers, w_first, bias_first.reshape(1, F)),
+        own=(
+            nodes,
+            nodes,
+            square,
+            half,
+            nodes,
+            nodes,
+            pltpu.VMEM((ROWS, F), F32),
+            square,
+            nodes,
+            letters(32),
+        ),
+        copies=8 * count + 1,
         flops=3 * wide,
         name="first_layer",
     )
@@ -359,11 +404,11 @@
     pushed = exchange(push)
     aggregate, term = call(
         second_layer,
-        "vvhvv",
+        "vvhvvv",
         (shaped(ROWS, F), shaped(F, F, dtype=F32)),
-        (pushed, partial_two, bank),
-        own=(nodes, square, nodes),
-        copies=count + 1,
+        (pushed, partial_two, bank, numbers),
+        own=(nodes, half, nodes),
+        copies=1,
         flops=2 * wide,
         name="second_layer",
     )

time: 173 us -> 170 us (0.983)
  Pallas kernels: 27.1 us -> 24.3 us
    pallas_call x7, Pallas kernels: 27.1 us -> 24.3 us  [call(): pl.pallas_call(body, out_shape=outs, in_specs=specs[:len(operands)], out_...]
where the time goes in v4:
time: 170 us
  waiting for transfers between devices  84.4 us (50%)
  starting transfers between devices  38.9 us (23%)
  Pallas kernels  24.3 us (14%)
  blocking collectives  14.3 us (8%)
  local copies, waits for them, and re-layouts  5.02 us (3%)
    all_to_all x3, waiting for transfers between devices, exchange(): lax.all_to_all(message, ORDER, split_axis=0, concat_axis=0, tiled=True)  70.6 us
    all_to_all x3, starting transfers between devices, exchange(): lax.all_to_all(message, ORDER, split_axis=0, concat_axis=0, tiled=True)  26.6 us
    pallas_call x7, Pallas kernels, call(): pl.pallas_call(body, out_shape=outs, in_specs=specs[:len(operands)], out_...  24.3 us
    all_to_all x1, blocking collectives, summed_everywhere(): lax.all_to_all(half.reshape(32, 4, F), CHIPS, split_axis=0, concat_axis=0...  14.3 us
    all_to_all x1, waiting for transfers between devices, summed_everywhere(): lax.all_to_all(copies, CHIPS, split_axis=0, concat_axis=0, tiled=True)  9.4 us
    ppermute x5, starting transfers between devices, swapped(): lax.ppermute(array, axis, [(i, i ^ mask) for i in range(lax.axis_size(axi...  8.42 us
    ppermute x5, waiting for transfers between devices, swapped(): lax.ppermute(array, axis, [(i, i ^ mask) for i in range(lax.axis_size(axi...  4.44 us
    unnamed x16, local copies, waits for them, and re-layouts  4.25 us
  transfers between devices with their start and end apart: 9, of which 7 were waited for; matrix products, arithmetic and copies ran while one was open for 1% of the time, Pallas kernels for 7%

profile of v4, /device:TPU:1, one launch (start us, length us, event | category | flops | bytes accessed | tf_op | source)
XLA Modules:
  0.0 169.7 jit_solution(8369892409602462762)
XLA Ops:
  0.6 2.3 %send_clusters.1 = bf16[64,72,128]{2,1,0:T(8,128)(2,1)} custom-call(s32[1,64]{1,0:T(1,128)} %owner.1, bf16[1024,256]{1,0:T(8,128)(2,1)} %x.1, bf16[1024,256]{1,0:T(8,128)(2,1)} %h.1, s32[8,128]{1,0:T(8,128)} %bitcast.13), custom_call_target="tpu_custom_call" | custom-call | flops 262144 | bytes 2232576 | tf_op jit(solution)/shard_map/send_clusters/pallas_call | solution.py:38
  3.0 0.0 copy-start.2
  3.0 0.0 copy-start.5
  3.0 13.4 %all-to-all-start = ((bf16[64,72,128]{2,1,0:T(8,128)(2,1)}), bf16[64,72,128]{2,1,0:T(8,128)(2,1)S(1)}, u32[]{:S(2)}, u32[]{:S(2)}) async-start(bf16[64,72,128]{2,1,0:T(8,128)(2,1)} %send_clusters.1), calls=%async_computation | async-start | bytes 2359296 | tf_op jit(solution)/shard_map/all_to_all | solution.py:276
  16.4 0.0 copy-done.2
  16.4 0.0 copy-done.5
  16.4 0.0 copy-start
  16.4 1.6 copy-done
  18.0 0.0 copy-start.1
  18.0 1.6 copy-done.1
  19.6 4.8 %mask_tiles.1.bank = bf16[1024,3840]{1,0:T(8,128)(2,1)} custom-call(s32[8,16]{1,0:T(8,128)S(1)} %copy-done.5, bf16[1024,1024]{1,0:T(8,128)(2,1)S(1)} %copy-done, bf16[1024,1024]{1,0:T(8,128)(2,1)S(1)} %copy-done.1, bf16[1024,256]{1,0:T(8,128)(2,1)S(1)} %copy-done.2), custom_call_target="tpu_custom_call" | custom-call | flops 536870912 | bytes 12583424 | tf_op jit(solution)/shard_map/mask_tiles/pallas_call | solution.py:38
  24.5 22.7 %all-to-all-done.message = bf16[64,72,128]{2,1,0:T(8,128)(2,1)S(1)} async-done(((bf16[64,72,128]{2,1,0:T(8,128)(2,1)}), bf16[64,72,128]{2,1,0:T(8,128)(2,1)S(1)}, u32[]{:S(2)}, u32[]{:S(2)}) %all-to-all-start) | async-done | bytes 1179680 | tf_op jit(solution)/shard_map/all_to_all | solution.py:276
  47.2 3.2 %serve.1 = (bf16[1024,256]{1,0:T(8,128)(2,1)S(1)}, bf16[64,96,128]{2,1,0:T(8,128)(2,1)}) custom-call(s32[1]{0:T(128)} %bitcast.me, bf16[64,72,128]{2,1,0:T(8,128)(2,1)S(1)} %all-to-all-done.message, bf16[1024,3840]{1,0:T(8,128)(2,1)} %mask_tiles.1.bank), custom_call_target="tpu_custom_call" | custom-call | flops 1610612736 | bytes 11141124 | tf_op jit(solution)/shard_map/serve/pallas_call | solution.py:38
  50.4 6.3 %all-to-all-start.1 = ((bf16[64,96,128]{2,1,0:T(8,128)(2,1)}), bf16[64,96,128]{2,1,0:T(8,128)(2,1)S(1)}, u32[]{:S(2)}, u32[]{:S(2)}) async-start(bf16[64,96,128]{2,1,0:T(8,128)(2,1)} %get-tuple-element.11), calls=%async_computation.1 | async-start | bytes 3145728 | tf_op jit(solution)/shard_map/all_to_all | solution.py:276
  56.7 0.0 copy-start.4
  56.7 0.0 copy-start.6
  56.7 3.4 %prepare.1 = (bf16[1024,3840]{1,0:T(8,128)(2,1)}, f32[8,128]{1,0:T(8,128)S(1)}) custom-call(s32[1]{0:T(128)} %bitcast.me, bf16[64,72,128]{2,1,0:T(8,128)(2,1)S(1)} %all-to-all-done.message, bf16[1024,256]{1,0:T(8,128)(2,1)S(1)} %get-tuple-element.12.own_x, bf16[1024,3840]{1,0:T(8,128)(2,1)} %mask_tiles.1.bank), custom_call_target="tpu_custom_call", output_to_operand_aliasing={{0}: (3, {})} | custom-call | flops 536870912 | bytes 17436676 | tf_op jit(solution)/shard_map/prepare/pallas_call | solution.py:38
  60.2 35.1 %all-to-all-done.1.message = bf16[64,96,128]{2,1,0:T(8,128)(2,1)S(1)} async-done(((bf16[64,96,128]{2,1,0:T(8,128)(2,1)}), bf16[64,96,128]{2,1,0:T(8,128)(2,1)S(1)}, u32[]{:S(2)}, u32[]{:S(2)}) %all-to-all-start.1) | async-done | bytes 1572896 | tf_op jit(solution)/shard_map/all_to_all | solution.py:276
  95.2 0.0 copy-done.4
  95.2 0.0 copy-done.6
  95.2 5.3 %first_layer.1 = (bf16[1024,256]{1,0:T(8,128)(2,1)}, bf16[64,32,128]{2,1,0:T(8,128)(2,1)}) custom-call(bf16[64,96,128]{2,1,0:T(8,128)(2,1)S(1)} %all-to-all-done.1.message, bf16[1024,3840]{1,0:T(8,128)(2,1)} %get-tuple-element.13.bank, f32[8,128]{1,0:T(8,128)S(1)} %get-tuple-element.14.numbers, bf16[256,256]{1,0:T(8,128)(2,1)S(1)} %copy-done.4, ...), custom_call_target="tpu_custom_call" | custom-call | flops 1610612736 | bytes 10621952 | tf_op jit(solution)/shard_map/first_layer/pallas_call | solution.py:38
  100.6 7.0 %all-to-all-start.2 = ((bf16[64,32,128]{2,1,0:T(8,128)(2,1)}), bf16[64,32,128]{2,1,0:T(8,128)(2,1)S(1)}, u32[]{:S(2)}, u32[]{:S(2)}) async-start(bf16[64,32,128]{2,1,0:T(8,128)(2,1)} %get-tuple-element.16), calls=%async_computation.2 | async-start | bytes 1048576 | tf_op jit(solution)/shard_map/all_to_all | solution.py:276
  107.6 0.0 copy-start.3
  107.6 1.0 copy-done.3
  108.6 3.5 %second_terms.1.partial = f32[1024,256]{1,0:T(8,128)S(1)} custom-call(bf16[64,96,128]{2,1,0:T(8,128)(2,1)S(1)} %all-to-all-done.1.message, bf16[1024,256]{1,0:T(8,128)(2,1)S(1)} %copy-done.3, bf16[1024,3840]{1,0:T(8,128)(2,1)} %get-tuple-element.13.bank), custom_call_target="tpu_custom_call" | custom-call | flops 1073741824 | bytes 11010048 | tf_op jit(solution)/shard_map/second_terms/pallas_call | solution.py:38
  112.1 12.8 %all-to-all-done.2.message = bf16[64,32,128]{2,1,0:T(8,128)(2,1)S(1)} async-done(((bf16[64,32,128]{2,1,0:T(8,128)(2,1)}), bf16[64,32,128]{2,1,0:T(8,128)(2,1)S(1)}, u32[]{:S(2)}, u32[]{:S(2)}) %all-to-all-start.2) | async-done | bytes 524320 | tf_op jit(solution)/shard_map/all_to_all | solution.py:276
  124.9 1.6 second_layer.1
  126.5 0.0 copy-start.7
  126.6 0.3 collective-permute-start
  126.9 1.3 collective-permute-done
  128.3 14.3 %all_to_all.25 = f32[32,4,256]{2,1,0:T(4,128)S(1)} all-to-all(f32[32,4,256]{2,1,0:T(4,128)S(1)} %reshape.29), channel_id=1, replica_groups=mesh['dev_0'=8,'dev_1'=4,'dev_2'=2,'rep'=4] {'dev_0','dev_1'}, dimensions={0} | all-to-all | bytes 262144 | tf_op jit(solution)/shard_map/all_to_all | solution.py:289
  142.6 2.8 %collective-permute-start.2 = (f32[4,256]{1,0:T(4,128)S(1)}, f32[4,256]{1,0:T(4,128)S(1)}, u32[]{:S(2)}, u32[]{:S(2)}) collective-permute-start(f32[4,256]{1,0:T(4,128)S(1)} %reduce_sum.9), channel_id=1, source_target_pairs={{0,2},{1,3},{2,0},{3,1},{4,6},{5,7},{6,4},{7,5},{8,10},{9,11},{10,... | collective-permute-start | bytes 12296 | tf_op jit(solution)/shard_map/ppermute | solution.py:280
  145.4 0.9 collective-permute-start.3
  146.3 0.0 collective-permute-start.1
  146.3 0.4 collective-permute-done.2
  146.6 2.7 %collective-permute-done.3 = f32[4,256]{1,0:T(4,128)S(1)} collective-permute-done((f32[4,256]{1,0:T(4,128)S(1)}, f32[4,256]{1,0:T(4,128)S(1)}, u32[]{:S(2)}, u32[]{:S(2)}) %collective-permute-start.3) | collective-permute-done | bytes 4128 | tf_op jit(solution)/shard_map/ppermute | solution.py:280
  149.4 0.0 collective-permute-done.1
  149.4 0.7 broadcast_in_dim.2
  150.1 3.9 %all-to-all-start.4 = ((f32[32,4,256]{2,1,0:T(4,128)}), f32[32,4,256]{2,1,0:T(4,128)S(1)}, u32[]{:S(2)}, u32[]{:S(2)}) async-start(f32[32,4,256]{2,1,0:T(4,128)} %broadcast_in_dim.2), calls=%async_computation.4 | async-start | bytes 262144 | tf_op jit(solution)/shard_map/all_to_all | solution.py:293
  153.9 9.4 %all-to-all-done.4 = f32[32,4,256]{2,1,0:T(4,128)S(1)} async-done(((f32[32,4,256]{2,1,0:T(4,128)}), f32[32,4,256]{2,1,0:T(4,128)S(1)}, u32[]{:S(2)}, u32[]{:S(2)}) %all-to-all-start.4) | async-done | bytes 131104 | tf_op jit(solution)/shard_map/all_to_all | solution.py:293
  163.4 4.5 %collective-permute-start.4 = (f32[128,256]{1,0:T(8,128)S(1)}, f32[128,256]{1,0:T(8,128)S(1)}, u32[]{:S(2)}, u32[]{:S(2)}) collective-permute-start(f32[128,256]{1,0:T(8,128)S(1)} %reshape.30), channel_id=1, source_target_pairs={{0,4},{4,0},{1,5},{5,1},{2,6},{6,2},{3,7},{7,3},{8,12},{12,8},{9,1... | collective-permute-start | bytes 393224 | tf_op jit(solution)/shard_map/ppermute | solution.py:280
  167.8 0.0 copy-done.7
  167.8 1.1 convolution_convert_fusion
  168.9 0.0 collective-permute-done.4
  169.0 0.7 pad_maximum_fusion
  (7 shorter events, 0.2 us)
Async XLA Ops:
  3.0 13.4 %copy-start.2 = (bf16[1024,256]{1,0:T(8,128)(2,1)S(1)}, bf16[1024,256]{1,0:T(8,128)(2,1)}, u32[]{:S(2)}) copy-start(bf16[1024,256]{1,0:T(8,128)(2,1)} %cotangent.1) | copy-start | bytes 1572868
  3.0 13.4 %copy-start.5 = (s32[8,16]{1,0:T(8,128)S(1)}, s32[8,16]{1,0:T(8,128)}, u32[]{:S(2)}) copy-start(s32[8,16]{1,0:T(8,128)} %occupied.1) | copy-start | bytes 1540
  3.0 44.2 %all-to-all-start = ((bf16[64,72,128]{2,1,0:T(8,128)(2,1)}), bf16[64,72,128]{2,1,0:T(8,128)(2,1)S(1)}, u32[]{:S(2)}, u32[]{:S(2)}) async-start(bf16[64,72,128]{2,1,0:T(8,128)(2,1)} %send_clusters.1), calls=%async_computation | async-start | bytes 2359296 | tf_op jit(solution)/shard_map/all_to_all | solution.py:276
  16.4 1.6 copy-start
  18.0 1.6 copy-start.1
  50.4 44.8 %all-to-all-start.1 = ((bf16[64,96,128]{2,1,0:T(8,128)(2,1)}), bf16[64,96,128]{2,1,0:T(8,128)(2,1)S(1)}, u32[]{:S(2)}, u32[]{:S(2)}) async-start(bf16[64,96,128]{2,1,0:T(8,128)(2,1)} %get-tuple-element.11), calls=%async_computation.1 | async-start | bytes 3145728 | tf_op jit(solution)/shard_map/all_to_all | solution.py:276
  56.7 38.5 %copy-start.4 = (bf16[256,256]{1,0:T(8,128)(2,1)S(1)}, bf16[256,256]{1,0:T(8,128)(2,1)}, u32[]{:S(2)}) copy-start(bf16[256,256]{1,0:T(8,128)(2,1)} %w.1) | copy-start | bytes 393220
  56.7 38.5 %copy-start.6 = (f32[256]{0:T(256)S(1)}, f32[256]{0:T(256)}, u32[]{:S(2)}) copy-start(f32[256]{0:T(256)} %param.19) | copy-start | bytes 3076
  100.6 24.3 %all-to-all-start.2 = ((bf16[64,32,128]{2,1,0:T(8,128)(2,1)}), bf16[64,32,128]{2,1,0:T(8,128)(2,1)S(1)}, u32[]{:S(2)}, u32[]{:S(2)}) async-start(bf16[64,32,128]{2,1,0:T(8,128)(2,1)} %get-tuple-element.16), calls=%async_computation.2 | async-start | bytes 1048576 | tf_op jit(solution)/shard_map/all_to_all | solution.py:276
  107.6 1.0 copy-start.3
  126.5 41.3 %copy-start.7 = (bf16[256,256]{1,0:T(8,128)(2,1)S(1)}, bf16[256,256]{1,0:T(8,128)(2,1)}, u32[]{:S(2)}) copy-start(bf16[256,256]{1,0:T(8,128)(2,1)} %param.20) | copy-start | bytes 393220
  126.6 1.6 collective-permute-start
  142.6 4.0 %collective-permute-start.2 = (f32[4,256]{1,0:T(4,128)S(1)}, f32[4,256]{1,0:T(4,128)S(1)}, u32[]{:S(2)}, u32[]{:S(2)}) collective-permute-start(f32[4,256]{1,0:T(4,128)S(1)} %reduce_sum.9), channel_id=1, source_target_pairs={{0,2},{1,3},{2,0},{3,1},{4,6},{5,7},{6,4},{7,5},{8,10},{9,11},{10,... | collective-permute-start | bytes 12296 | tf_op jit(solution)/shard_map/ppermute | solution.py:280
  145.4 4.0 %collective-permute-start.3 = (f32[4,256]{1,0:T(4,128)S(1)}, f32[4,256]{1,0:T(4,128)S(1)}, u32[]{:S(2)}, u32[]{:S(2)}) collective-permute-start(f32[4,256]{1,0:T(4,128)S(1)} %reduce_sum.9), channel_id=1, source_target_pairs={{0,3},{1,2},{2,1},{3,0},{4,7},{5,6},{6,5},{7,4},{8,11},{9,10},{10,... | collective-permute-start | bytes 12296 | tf_op jit(solution)/shard_map/ppermute | solution.py:280
  146.3 3.1 %collective-permute-start.1 = (f32[4,256]{1,0:T(4,128)S(1)}, f32[4,256]{1,0:T(4,128)S(1)}, u32[]{:S(2)}, u32[]{:S(2)}) collective-permute-start(f32[4,256]{1,0:T(4,128)S(1)} %reduce_sum.9), channel_id=1, source_target_pairs={{0,1},{1,0},{2,3},{3,2},{4,5},{5,4},{6,7},{7,6},{8,9},{9,8},{10,11... | collective-permute-start | bytes 12296 | tf_op jit(solution)/shard_map/ppermute | solution.py:280
  150.1 13.3 %all-to-all-start.4 = ((f32[32,4,256]{2,1,0:T(4,128)}), f32[32,4,256]{2,1,0:T(4,128)S(1)}, u32[]{:S(2)}, u32[]{:S(2)}) async-start(f32[32,4,256]{2,1,0:T(4,128)} %broadcast_in_dim.2), calls=%async_computation.4 | async-start | bytes 262144 | tf_op jit(solution)/shard_map/all_to_all | solution.py:293
  163.4 5.6 %collective-permute-start.4 = (f32[128,256]{1,0:T(8,128)S(1)}, f32[128,256]{1,0:T(8,128)S(1)}, u32[]{:S(2)}, u32[]{:S(2)}) collective-permute-start(f32[128,256]{1,0:T(8,128)S(1)} %reshape.30), channel_id=1, source_target_pairs={{0,4},{4,0},{1,5},{5,1},{2,6},{6,2},{3,7},{7,3},{8,12},{12,8},{9,1... | collective-permute-start | bytes 393224 | tf_op jit(solution)/shard_map/ppermute | solution.py:280

commit v5 on v4

--- a/solution.py
+++ b/solution.py
@@ -13,14 +13,14 @@
 PEERS, SLOT, HALF, ROWS, F = 64, 16, 128, 1024, 256
 STEP = 512
 BANK = {
-    "local": slice(0, 1024),
-    "edge": slice(1024, 2048),
-    "flipped": slice(2048, 3072),
-    "high": slice(3072, 3328),
-    "low": slice(3328, 3584),
-    "cotangent": slice(3584, 3840),
+    "local": (0, slice(0, 1024)),
+    "edge": (1024, slice(0, 1024)),
+    "flipped": (2048, slice(0, 1024)),
+    "high": (3072, slice(0, 256)),
+    "low": (3072, slice(256, 512)),
+    "cotangent": (3072, slice(512, 768)),
 }
-WIDTH = 3840
+DEPTH = 4096
 VMEM = 67043328
 
 F32, BF16 = jnp.float32, jnp.bfloat16
@@ -59,7 +59,12 @@
         return copy
 
     def stored(self, source, bank, name):
-        return self.start(source, bank.at[:, BANK[name]])
+        return self.start(source, kept(bank, name, slice(0, ROWS)))
+
+
+def kept(bank, name, rows):
+    first, columns = BANK[name]
+    return bank.at[first + rows.start : first + rows.stop, columns]
 
 
 def wait(*copies):
@@ -179,7 +184,7 @@
 def serve(me, message, bank, own_x, reply_far, own_h, flipped, reply, sem):
     copies = Copies(sem)
     arriving = [
-        copies.start(bank.at[rows, BANK["flipped"]], flipped.at[rows]) for rows, peers in steps()
+        copies.start(kept(bank, "flipped", rows), flipped.at[rows]) for rows, peers in steps()
     ]
     take_by_owner(message, 0, own_x)
     take_by_owner(message, 32, own_h)
@@ -201,7 +206,7 @@
 
 def prepare(me, message, own_x, bank, bank_out, numbers, local, high, low, sem):
     copies = Copies(sem)
-    first = copies.start(bank.at[:, BANK["local"]], local)
+    first = copies.start(kept(bank, "local", slice(0, ROWS)), local)
     wanted = jnp.broadcast_to(requested(me[0], message[:, 64:72, :]), (ROWS, HALF))
     for a in range(8):
         numbers[a : a + 1, :] = wanted[a * HALF : (a + 1) * HALF].T[0:1, :]
@@ -220,11 +225,11 @@
     copies = Copies(sem)
     into = {"edge": edge, "high": high, "low": low}
     arriving = [
-        [copies.start(bank.at[rows, BANK[name]], ref.at[rows]) for name, ref in into.items()]
+        [copies.start(kept(bank, name, rows), ref.at[rows]) for name, ref in into.items()]
         for rows, peers in steps()
     ]
     last = [
-        copies.start(bank.at[rows, BANK["flipped"]], flipped.at[rows]) for rows, peers in steps()
+        copies.start(kept(bank, "flipped", rows), flipped.at[rows]) for rows, peers in steps()
     ]
     take(message, 64, pushed)
     for rows, peers in steps():
@@ -249,8 +254,8 @@
 def second_terms(message, hidden, bank, partial, far, local, edge, sem):
     copies = Copies(sem)
     parts = [
-        copies.start(bank.at[:, BANK["local"]], local),
-        copies.start(bank.at[:, BANK["edge"]], edge),
+        copies.start(kept(bank, "local", slice(0, ROWS)), local),
+        copies.start(kept(bank, "edge", slice(0, ROWS)), edge),
     ]
     take_by_owner(message, 32, far)
     wait(*parts)
@@ -260,7 +265,7 @@
 
 def second_layer(message, partial, bank, numbers, aggregate, gradient, pushed, gather, cotangent, sem):
     copies = Copies(sem)
-    last = copies.start(bank.at[:, BANK["cotangent"]], cotangent)
+    last = copies.start(kept(bank, "cotangent", slice(0, ROWS)), cotangent)
     take(message, 0, pushed)
     for rows, peers in steps():
         collector(numbers, gather, rows)
@@ -283,18 +288,18 @@
 def summed_everywhere(term):
     core = lax.axis_index("dev_2")
     halves = term.reshape(2, ROWS // 8, F)
-    kept = lax.dynamic_index_in_dim(halves, core, 0, keepdims=False)
+    kept_half = lax.dynamic_index_in_dim(halves, core, 0, keepdims=False)
     sent = lax.dynamic_index_in_dim(halves, 1 - core, 0, keepdims=False)
-    half = kept + swapped(sent, "dev_2", 1)
+    half = (kept_half + swapped(sent, "dev_2", 1)).astype(BF16)
     tiles = lax.all_to_all(half.reshape(32, 4, F), CHIPS, split_axis=0, concat_axis=0, tiled=True)
-    own = jnp.sum(tiles, axis=0)
+    own = jnp.sum(tiles.astype(F32), axis=0)
     own = (own + swapped(own, "rep", 1)) + (swapped(own, "rep", 2) + swapped(own, "rep", 3))
-    copies = jnp.broadcast_to(own[None], (32, 4, F))
+    copies = jnp.broadcast_to(own.astype(BF16)[None], (32, 4, F))
     mine = lax.all_to_all(copies, CHIPS, split_axis=0, concat_axis=0, tiled=True).reshape(128, F)
     other = swapped(mine, "dev_2", 1)
     first = jnp.where(core == 0, mine, other)
     second = jnp.where(core == 0, other, mine)
-    return jnp.concatenate([first, second], axis=0)
+    return jnp.concatenate([first, second], axis=0).astype(F32)
 
 
 def body(
@@ -338,7 +343,7 @@
     (bank,) = call(
         mask_tiles,
         "svvvh",
-        (shaped(ROWS, WIDTH),),
+        (shaped(DEPTH, ROWS),),
         (occupancy, adj_local, adj_boundary, cotangent),
         own=(square, square, square),
         copies=4,
@@ -361,7 +366,7 @@
     bank, numbers = call(
         prepare,
         "svvhhv",
-        (shaped(ROWS, WIDTH), shaped(8, HALF, dtype=F32)),
+        (shaped(DEPTH, ROWS), shaped(8, HALF, dtype=F32)),
         (me, arrived, own_x, bank),
         own=(square, nodes, nodes),
         copies=3,

time: 170 us -> 169 us (level)
  no operation moved by 1% of the time
where the time goes in v5:
time: 169 us; the launch traced here: 168 us
  waiting for transfers between devices  83.8 us (50%)
  starting transfers between devices  38.8 us (23%)
  Pallas kernels  24.1 us (14%)
  blocking collectives  13.7 us (8%)
  local copies, waits for them, and re-layouts  4.96 us (3%)
    all_to_all x3, waiting for transfers between devices, exchange(): lax.all_to_all(message, ORDER, split_axis=0, concat_axis=0, tiled=True)  70.7 us
    all_to_all x3, starting transfers between devices, exchange(): lax.all_to_all(message, ORDER, split_axis=0, concat_axis=0, tiled=True)  26.6 us
    pallas_call x7, Pallas kernels, call(): pl.pallas_call(body, out_shape=outs, in_specs=specs[:len(operands)], out_...  24.1 us
    all_to_all x1, blocking collectives, summed_everywhere(): lax.all_to_all(half.reshape(32, 4, F), CHIPS, split_axis=0, concat_axis=0...  13.7 us
    all_to_all x1, waiting for transfers between devices, summed_everywhere(): lax.all_to_all(copies, CHIPS, split_axis=0, concat_axis=0, tiled=True)  8.87 us
    ppermute x5, starting transfers between devices, swapped(): lax.ppermute(array, axis, [(i, i ^ mask) for i in range(lax.axis_size(axi...  8.32 us
    unnamed x16, local copies, waits for them, and re-layouts  4.25 us
    ppermute x5, waiting for transfers between devices, swapped(): lax.ppermute(array, axis, [(i, i ^ mask) for i in range(lax.axis_size(axi...  4.24 us
  transfers between devices with their start and end apart: 9, of which 7 were waited for; matrix products, arithmetic and copies ran while one was open for 1% of the time, Pallas kernels for 7%

profile of v5, /device:TPU:1, one launch (start us, length us, event | category | flops | bytes accessed | tf_op | source)
XLA Modules:
  0.0 168.2 jit_solution(13403158765755032170)
XLA Ops:
  0.6 2.3 %send_clusters.1 = bf16[64,72,128]{2,1,0:T(8,128)(2,1)} custom-call(s32[1,64]{1,0:T(1,128)} %owner.1, bf16[1024,256]{1,0:T(8,128)(2,1)} %x.1, bf16[1024,256]{1,0:T(8,128)(2,1)} %h.1, s32[8,128]{1,0:T(8,128)} %bitcast.15), custom_call_target="tpu_custom_call" | custom-call | flops 262144 | bytes 2232576 | tf_op jit(solution)/shard_map/send_clusters/pallas_call | solution.py:38
  3.0 0.0 copy-start.2
  3.0 0.0 copy-start.5
  3.0 13.4 %all-to-all-start = ((bf16[64,72,128]{2,1,0:T(8,128)(2,1)}), bf16[64,72,128]{2,1,0:T(8,128)(2,1)S(1)}, u32[]{:S(2)}, u32[]{:S(2)}) async-start(bf16[64,72,128]{2,1,0:T(8,128)(2,1)} %send_clusters.1), calls=%async_computation | async-start | bytes 2359296 | tf_op jit(solution)/shard_map/all_to_all | solution.py:281
  16.4 0.0 copy-done.2
  16.4 0.0 copy-done.5
  16.4 0.0 copy-start
  16.4 1.6 copy-done
  18.0 0.0 copy-start.1
  18.0 1.6 copy-done.1
  19.6 4.8 %mask_tiles.1.bank = bf16[4096,1024]{1,0:T(8,128)(2,1)} custom-call(s32[8,16]{1,0:T(8,128)S(1)} %copy-done.5, bf16[1024,1024]{1,0:T(8,128)(2,1)S(1)} %copy-done, bf16[1024,1024]{1,0:T(8,128)(2,1)S(1)} %copy-done.1, bf16[1024,256]{1,0:T(8,128)(2,1)S(1)} %copy-done.2), custom_call_target="tpu_custom_call" | custom-call | flops 536870912 | bytes 13107712 | tf_op jit(solution)/shard_map/mask_tiles/pallas_call | solution.py:38
  24.4 22.8 %all-to-all-done.message = bf16[64,72,128]{2,1,0:T(8,128)(2,1)S(1)} async-done(((bf16[64,72,128]{2,1,0:T(8,128)(2,1)}), bf16[64,72,128]{2,1,0:T(8,128)(2,1)S(1)}, u32[]{:S(2)}, u32[]{:S(2)}) %all-to-all-start) | async-done | bytes 1179680 | tf_op jit(solution)/shard_map/all_to_all | solution.py:281
  47.2 3.2 %serve.1 = (bf16[1024,256]{1,0:T(8,128)(2,1)S(1)}, bf16[64,96,128]{2,1,0:T(8,128)(2,1)}) custom-call(s32[1]{0:T(128)} %bitcast.me, bf16[64,72,128]{2,1,0:T(8,128)(2,1)S(1)} %all-to-all-done.message, bf16[4096,1024]{1,0:T(8,128)(2,1)} %mask_tiles.1.bank), custom_call_target="tpu_custom_call" | custom-call | flops 1610612736 | bytes 11665412 | tf_op jit(solution)/shard_map/serve/pallas_call | solution.py:38
  50.4 6.3 %all-to-all-start.1 = ((bf16[64,96,128]{2,1,0:T(8,128)(2,1)}), bf16[64,96,128]{2,1,0:T(8,128)(2,1)S(1)}, u32[]{:S(2)}, u32[]{:S(2)}) async-start(bf16[64,96,128]{2,1,0:T(8,128)(2,1)} %get-tuple-element.11), calls=%async_computation.1 | async-start | bytes 3145728 | tf_op jit(solution)/shard_map/all_to_all | solution.py:281
  56.7 0.0 copy-start.4
  56.7 0.0 copy-start.6
  56.7 3.4 %prepare.1 = (bf16[4096,1024]{1,0:T(8,128)(2,1)}, f32[8,128]{1,0:T(8,128)S(1)}) custom-call(s32[1]{0:T(128)} %bitcast.me, bf16[64,72,128]{2,1,0:T(8,128)(2,1)S(1)} %all-to-all-done.message, bf16[1024,256]{1,0:T(8,128)(2,1)S(1)} %get-tuple-element.12.own_x, bf16[4096,1024]{1,0:T(8,128)(2,1)} %mask_tiles.1.bank), custom_call_target="tpu_custom_call", output_to_operand_aliasing={{0}: (3, {})} | custom-call | flops 536870912 | bytes 18485252 | tf_op jit(solution)/shard_map/prepare/pallas_call | solution.py:38
  60.1 35.1 %all-to-all-done.1.message = bf16[64,96,128]{2,1,0:T(8,128)(2,1)S(1)} async-done(((bf16[64,96,128]{2,1,0:T(8,128)(2,1)}), bf16[64,96,128]{2,1,0:T(8,128)(2,1)S(1)}, u32[]{:S(2)}, u32[]{:S(2)}) %all-to-all-start.1) | async-done | bytes 1572896 | tf_op jit(solution)/shard_map/all_to_all | solution.py:281
  95.2 0.0 copy-done.4
  95.2 0.0 copy-done.6
  95.2 5.3 %first_layer.1 = (bf16[1024,256]{1,0:T(8,128)(2,1)}, bf16[64,32,128]{2,1,0:T(8,128)(2,1)}) custom-call(bf16[64,96,128]{2,1,0:T(8,128)(2,1)S(1)} %all-to-all-done.1.message, bf16[4096,1024]{1,0:T(8,128)(2,1)} %get-tuple-element.13.bank, f32[8,128]{1,0:T(8,128)S(1)} %get-tuple-element.14.numbers, bf16[256,256]{1,0:T(8,128)(2,1)S(1)} %copy-done.4, ...), custom_call_target="tpu_custom_call" | custom-call | flops 1610612736 | bytes 11146240 | tf_op jit(solution)/shard_map/first_layer/pallas_call | solution.py:38
  100.5 7.0 %all-to-all-start.2 = ((bf16[64,32,128]{2,1,0:T(8,128)(2,1)}), bf16[64,32,128]{2,1,0:T(8,128)(2,1)S(1)}, u32[]{:S(2)}, u32[]{:S(2)}) async-start(bf16[64,32,128]{2,1,0:T(8,128)(2,1)} %get-tuple-element.16), calls=%async_computation.2 | async-start | bytes 1048576 | tf_op jit(solution)/shard_map/all_to_all | solution.py:281
  107.5 0.0 copy-start.3
  107.5 1.0 copy-done.3
  108.5 3.5 %second_terms.1.partial = f32[1024,256]{1,0:T(8,128)S(1)} custom-call(bf16[64,96,128]{2,1,0:T(8,128)(2,1)S(1)} %all-to-all-done.1.message, bf16[1024,256]{1,0:T(8,128)(2,1)S(1)} %copy-done.3, bf16[4096,1024]{1,0:T(8,128)(2,1)} %get-tuple-element.13.bank), custom_call_target="tpu_custom_call" | custom-call | flops 1073741824 | bytes 11534336 | tf_op jit(solution)/shard_map/second_terms/pallas_call | solution.py:38
  112.0 0.0 copy-start.7
  112.0 12.8 %all-to-all-done.2.message = bf16[64,32,128]{2,1,0:T(8,128)(2,1)S(1)} async-done(((bf16[64,32,128]{2,1,0:T(8,128)(2,1)}), bf16[64,32,128]{2,1,0:T(8,128)(2,1)S(1)}, u32[]{:S(2)}, u32[]{:S(2)}) %all-to-all-start.2) | async-done | bytes 524320 | tf_op jit(solution)/shard_map/all_to_all | solution.py:281
  124.8 1.7 second_layer.1
  126.5 0.3 collective-permute-start
  126.8 1.3 collective-permute-done
  128.2 13.7 %all_to_all.25 = bf16[32,4,256]{2,1,0:T(4,128)(2,1)S(1)} all-to-all(bf16[32,4,256]{2,1,0:T(4,128)(2,1)S(1)} %reshape.29), channel_id=1, replica_groups=mesh['dev_0'=8,'dev_1'=4,'dev_2'=2,'rep'=4] {'dev_0','dev_1'}, dimensions={0} | all-to-all | bytes 131072 | tf_op jit(solution)/shard_map/all_to_all | solution.py:294
  141.9 0.1 convert_reduce_fusion
  142.0 2.8 %collective-permute-start.2 = (f32[4,256]{1,0:T(4,128)S(1)}, f32[4,256]{1,0:T(4,128)S(1)}, u32[]{:S(2)}, u32[]{:S(2)}) collective-permute-start(f32[4,256]{1,0:T(4,128)S(1)} %convert_reduce_fusion), channel_id=1, source_target_pairs={{0,2},{1,3},{2,0},{3,1},{4,6},{5,7},{6,4},{7,5},{8,10},{9,11},{10,... | collective-permute-start | bytes 12296 | tf_op jit(solution)/shard_map/ppermute | solution.py:285
  144.8 0.9 collective-permute-start.3
  145.6 0.0 collective-permute-start.1
  145.7 0.3 collective-permute-done.2
  146.0 2.5 %collective-permute-done.3 = f32[4,256]{1,0:T(4,128)S(1)} collective-permute-done((f32[4,256]{1,0:T(4,128)S(1)}, f32[4,256]{1,0:T(4,128)S(1)}, u32[]{:S(2)}, u32[]{:S(2)}) %collective-permute-start.3) | collective-permute-done | bytes 4128 | tf_op jit(solution)/shard_map/ppermute | solution.py:285
  148.5 0.0 collective-permute-done.1
  148.6 0.7 broadcast_in_dim.2
  149.2 3.9 %all-to-all-start.4 = ((bf16[32,4,256]{2,1,0:T(4,128)(2,1)}), bf16[32,4,256]{2,1,0:T(4,128)(2,1)S(1)}, u32[]{:S(2)}, u32[]{:S(2)}) async-start(bf16[32,4,256]{2,1,0:T(4,128)(2,1)} %broadcast_in_dim.2), calls=%async_computation.4 | async-start | bytes 131072 | tf_op jit(solution)/shard_map/all_to_all | solution.py:298
  153.1 8.9 %all-to-all-done.4 = bf16[32,4,256]{2,1,0:T(4,128)(2,1)S(1)} async-done(((bf16[32,4,256]{2,1,0:T(4,128)(2,1)}), bf16[32,4,256]{2,1,0:T(4,128)(2,1)S(1)}, u32[]{:S(2)}, u32[]{:S(2)}) %all-to-all-start.4) | async-done | bytes 65568 | tf_op jit(solution)/shard_map/all_to_all | solution.py:298
  162.0 4.4 %collective-permute-start.4 = (bf16[128,256]{1,0:T(8,128)(2,1)S(1)}, bf16[128,256]{1,0:T(8,128)(2,1)S(1)}, u32[]{:S(2)}, u32[]{:S(2)}) collective-permute-start(bf16[128,256]{1,0:T(8,128)(2,1)S(1)} %reshape.30), channel_id=1, source_target_pairs={{0,4},{4,0},{1,5},{5,1},{2,6},{6,2},{3,7},{7,3},{8,12},{12,8},{9,1... | collective-permute-start | bytes 196616 | tf_op jit(solution)/shard_map/ppermute | solution.py:285
  166.3 0.0 copy-done.7
  166.3 1.1 convolution_convert_fusion
  167.4 0.0 collective-permute-done.4
  167.5 0.7 maximum_convert_fusion
  (6 shorter events, 0.1 us)
Async XLA Ops:
  3.0 13.4 %copy-start.2 = (bf16[1024,256]{1,0:T(8,128)(2,1)S(1)}, bf16[1024,256]{1,0:T(8,128)(2,1)}, u32[]{:S(2)}) copy-start(bf16[1024,256]{1,0:T(8,128)(2,1)} %cotangent.1) | copy-start | bytes 1572868
  3.0 13.4 %copy-start.5 = (s32[8,16]{1,0:T(8,128)S(1)}, s32[8,16]{1,0:T(8,128)}, u32[]{:S(2)}) copy-start(s32[8,16]{1,0:T(8,128)} %occupied.1) | copy-start | bytes 1540
  3.0 44.2 %all-to-all-start = ((bf16[64,72,128]{2,1,0:T(8,128)(2,1)}), bf16[64,72,128]{2,1,0:T(8,128)(2,1)S(1)}, u32[]{:S(2)}, u32[]{:S(2)}) async-start(bf16[64,72,128]{2,1,0:T(8,128)(2,1)} %send_clusters.1), calls=%async_computation | async-start | bytes 2359296 | tf_op jit(solution)/shard_map/all_to_all | solution.py:281
  16.4 1.6 copy-start
  18.0 1.6 copy-start.1
  50.4 44.8 %all-to-all-start.1 = ((bf16[64,96,128]{2,1,0:T(8,128)(2,1)}), bf16[64,96,128]{2,1,0:T(8,128)(2,1)S(1)}, u32[]{:S(2)}, u32[]{:S(2)}) async-start(bf16[64,96,128]{2,1,0:T(8,128)(2,1)} %get-tuple-element.11), calls=%async_computation.1 | async-start | bytes 3145728 | tf_op jit(solution)/shard_map/all_to_all | solution.py:281
  56.7 38.5 %copy-start.4 = (bf16[256,256]{1,0:T(8,128)(2,1)S(1)}, bf16[256,256]{1,0:T(8,128)(2,1)}, u32[]{:S(2)}) copy-start(bf16[256,256]{1,0:T(8,128)(2,1)} %w.1) | copy-start | bytes 393220
  56.7 38.5 %copy-start.6 = (f32[256]{0:T(256)S(1)}, f32[256]{0:T(256)}, u32[]{:S(2)}) copy-start(f32[256]{0:T(256)} %param.19) | copy-start | bytes 3076
  100.5 24.3 %all-to-all-start.2 = ((bf16[64,32,128]{2,1,0:T(8,128)(2,1)}), bf16[64,32,128]{2,1,0:T(8,128)(2,1)S(1)}, u32[]{:S(2)}, u32[]{:S(2)}) async-start(bf16[64,32,128]{2,1,0:T(8,128)(2,1)} %get-tuple-element.16), calls=%async_computation.2 | async-start | bytes 1048576 | tf_op jit(solution)/shard_map/all_to_all | solution.py:281
  107.5 1.0 copy-start.3
  112.0 54.3 %copy-start.7 = (bf16[256,256]{1,0:T(8,128)(2,1)S(1)}, bf16[256,256]{1,0:T(8,128)(2,1)}, u32[]{:S(2)}) copy-start(bf16[256,256]{1,0:T(8,128)(2,1)} %param.20) | copy-start | bytes 393220
  126.5 1.6 collective-permute-start
  142.0 4.0 %collective-permute-start.2 = (f32[4,256]{1,0:T(4,128)S(1)}, f32[4,256]{1,0:T(4,128)S(1)}, u32[]{:S(2)}, u32[]{:S(2)}) collective-permute-start(f32[4,256]{1,0:T(4,128)S(1)} %convert_reduce_fusion), channel_id=1, source_target_pairs={{0,2},{1,3},{2,0},{3,1},{4,6},{5,7},{6,4},{7,5},{8,10},{9,11},{10,... | collective-permute-start | bytes 12296 | tf_op jit(solution)/shard_map/ppermute | solution.py:285
  144.8 3.8 %collective-permute-start.3 = (f32[4,256]{1,0:T(4,128)S(1)}, f32[4,256]{1,0:T(4,128)S(1)}, u32[]{:S(2)}, u32[]{:S(2)}) collective-permute-start(f32[4,256]{1,0:T(4,128)S(1)} %convert_reduce_fusion), channel_id=1, source_target_pairs={{0,3},{1,2},{2,1},{3,0},{4,7},{5,6},{6,5},{7,4},{8,11},{9,10},{10,... | collective-permute-start | bytes 12296 | tf_op jit(solution)/shard_map/ppermute | solution.py:285
  145.6 2.9 %collective-permute-start.1 = (f32[4,256]{1,0:T(4,128)S(1)}, f32[4,256]{1,0:T(4,128)S(1)}, u32[]{:S(2)}, u32[]{:S(2)}) collective-permute-start(f32[4,256]{1,0:T(4,128)S(1)} %convert_reduce_fusion), channel_id=1, source_target_pairs={{0,1},{1,0},{2,3},{3,2},{4,5},{5,4},{6,7},{7,6},{8,9},{9,8},{10,11... | collective-permute-start | bytes 12296 | tf_op jit(solution)/shard_map/ppermute | solution.py:285
  149.2 12.7 %all-to-all-start.4 = ((bf16[32,4,256]{2,1,0:T(4,128)(2,1)}), bf16[32,4,256]{2,1,0:T(4,128)(2,1)S(1)}, u32[]{:S(2)}, u32[]{:S(2)}) async-start(bf16[32,4,256]{2,1,0:T(4,128)(2,1)} %broadcast_in_dim.2), calls=%async_computation.4 | async-start | bytes 131072 | tf_op jit(solution)/shard_map/all_to_all | solution.py:298
  162.0 5.5 %collective-permute-start.4 = (bf16[128,256]{1,0:T(8,128)(2,1)S(1)}, bf16[128,256]{1,0:T(8,128)(2,1)S(1)}, u32[]{:S(2)}, u32[]{:S(2)}) collective-permute-start(bf16[128,256]{1,0:T(8,128)(2,1)S(1)} %reshape.30), channel_id=1, source_target_pairs={{0,4},{4,0},{1,5},{5,1},{2,6},{6,2},{3,7},{7,3},{8,12},{12,8},{9,1... | collective-permute-start | bytes 196616 | tf_op jit(solution)/shard_map/ppermute | solution.py:285

commit v6 on v5

--- a/solution.py
+++ b/solution.py
@@ -70,6 +70,10 @@
 def wait(*copies):
     for copy in copies:
         copy.wait()
+
+
+def dot_flipped(a, b):
+    return lax.dot_general(a, b, (((0,), (0,)), ((), ())), preferred_element_type=F32)
 
 
 def shaped(*dims, dtype=BF16):
@@ -220,16 +224,13 @@
 
 def first_layer(
     message, bank, numbers, w, bias, hidden_far, push_far,
-    far, pushed, edge, gather, high, low, sums, flipped, hidden, push, sem,
+    far, pushed, edge, gather, high, low, sums, hidden, push, sem,
 ):
     copies = Copies(sem)
     into = {"edge": edge, "high": high, "low": low}
     arriving = [
         [copies.start(kept(bank, name, rows), ref.at[rows]) for name, ref in into.items()]
         for rows, peers in steps()
-    ]
-    last = [
-        copies.start(kept(bank, "flipped", rows), flipped.at[rows]) for rows, peers in steps()
     ]
     take(message, 64, pushed)
     for rows, peers in steps():
@@ -243,9 +244,8 @@
         value = dot(total.astype(BF16), w[...]) + bias[...]
         hidden[rows, :] = jnp.maximum(value, 0.0).astype(BF16)
     out = [copies.start(hidden, hidden_far)]
-    wait(*last)
     for rows, peers in steps(STEP // 2):
-        put_by_owner(push, 0, peers, dot(flipped[rows, :], hidden[...]).astype(BF16))
+        put_by_owner(push, 0, peers, dot_flipped(edge[:, rows], hidden[...]).astype(BF16))
         for part in places(peers):
             out.append(copies.start(push.at[part], push_far.at[part]))
     wait(*out)
@@ -388,11 +388,10 @@
             nodes,
             nodes,
             pltpu.VMEM((ROWS, F), F32),
-            square,
             nodes,
             letters(32),
         ),
-        copies=8 * count + 1,
+        copies=7 * count + 1,
         flops=3 * wide,
         name="first_layer",
     )

time: 169 us -> 168 us (level)
  no operation moved by 1% of the time
where the time goes in v6:
time: 168 us; the launch traced here: 167 us
  waiting for transfers between devices  83.8 us (50%)
  starting transfers between devices  38.8 us (23%)
  Pallas kernels  23.3 us (14%)
  blocking collectives  13.7 us (8%)
  local copies, waits for them, and re-layouts  4.96 us (3%)
    all_to_all x3, waiting for transfers between devices, exchange(): lax.all_to_all(message, ORDER, split_axis=0, concat_axis=0, tiled=True)  70.7 us
    all_to_all x3, starting transfers between devices, exchange(): lax.all_to_all(message, ORDER, split_axis=0, concat_axis=0, tiled=True)  26.6 us
    pallas_call x7, Pallas kernels, call(): pl.pallas_call(body, out_shape=outs, in_specs=specs[:len(operands)], out_...  23.3 us
    all_to_all x1, blocking collectives, summed_everywhere(): lax.all_to_all(half.reshape(32, 4, F), CHIPS, split_axis=0, concat_axis=0...  13.7 us
    all_to_all x1, waiting for transfers between devices, summed_everywhere(): lax.all_to_all(copies, CHIPS, split_axis=0, concat_axis=0, tiled=True)  8.87 us
    ppermute x5, starting transfers between devices, swapped(): lax.ppermute(array, axis, [(i, i ^ mask) for i in range(lax.axis_size(axi...  8.32 us
    unnamed x16, local copies, waits for them, and re-layouts  4.25 us
    ppermute x5, waiting for transfers between devices, swapped(): lax.ppermute(array, axis, [(i, i ^ mask) for i in range(lax.axis_size(axi...  4.24 us
  transfers between devices with their start and end apart: 9, of which 7 were waited for; matrix products, arithmetic and copies ran while one was open for 1% of the time, Pallas kernels for 7%

profile of v6, /device:TPU:1, one launch (start us, length us, event | category | flops | bytes accessed | tf_op | source)
XLA Modules:
  0.0 167.3 jit_solution(17168255482402896537)
XLA Ops:
  0.6 2.3 %send_clusters.1 = bf16[64,72,128]{2,1,0:T(8,128)(2,1)} custom-call(s32[1,64]{1,0:T(1,128)} %owner.1, bf16[1024,256]{1,0:T(8,128)(2,1)} %x.1, bf16[1024,256]{1,0:T(8,128)(2,1)} %h.1, s32[8,128]{1,0:T(8,128)} %bitcast.15), custom_call_target="tpu_custom_call" | custom-call | flops 262144 | bytes 2232576 | tf_op jit(solution)/shard_map/send_clusters/pallas_call | solution.py:38
  3.0 0.0 copy-start.2
  3.0 0.0 copy-start.5
  3.0 13.4 %all-to-all-start = ((bf16[64,72,128]{2,1,0:T(8,128)(2,1)}), bf16[64,72,128]{2,1,0:T(8,128)(2,1)S(1)}, u32[]{:S(2)}, u32[]{:S(2)}) async-start(bf16[64,72,128]{2,1,0:T(8,128)(2,1)} %send_clusters.1), calls=%async_computation | async-start | bytes 2359296 | tf_op jit(solution)/shard_map/all_to_all | solution.py:281
  16.4 0.0 copy-done.2
  16.4 0.0 copy-done.5
  16.4 0.0 copy-start
  16.4 1.6 copy-done
  18.0 0.0 copy-start.1
  18.0 1.6 copy-done.1
  19.6 4.8 %mask_tiles.1.bank = bf16[4096,1024]{1,0:T(8,128)(2,1)} custom-call(s32[8,16]{1,0:T(8,128)S(1)} %copy-done.5, bf16[1024,1024]{1,0:T(8,128)(2,1)S(1)} %copy-done, bf16[1024,1024]{1,0:T(8,128)(2,1)S(1)} %copy-done.1, bf16[1024,256]{1,0:T(8,128)(2,1)S(1)} %copy-done.2), custom_call_target="tpu_custom_call" | custom-call | flops 536870912 | bytes 13107712 | tf_op jit(solution)/shard_map/mask_tiles/pallas_call | solution.py:38
  24.4 22.8 %all-to-all-done.message = bf16[64,72,128]{2,1,0:T(8,128)(2,1)S(1)} async-done(((bf16[64,72,128]{2,1,0:T(8,128)(2,1)}), bf16[64,72,128]{2,1,0:T(8,128)(2,1)S(1)}, u32[]{:S(2)}, u32[]{:S(2)}) %all-to-all-start) | async-done | bytes 1179680 | tf_op jit(solution)/shard_map/all_to_all | solution.py:281
  47.2 3.2 %serve.1 = (bf16[1024,256]{1,0:T(8,128)(2,1)S(1)}, bf16[64,96,128]{2,1,0:T(8,128)(2,1)}) custom-call(s32[1]{0:T(128)} %bitcast.me, bf16[64,72,128]{2,1,0:T(8,128)(2,1)S(1)} %all-to-all-done.message, bf16[4096,1024]{1,0:T(8,128)(2,1)} %mask_tiles.1.bank), custom_call_target="tpu_custom_call" | custom-call | flops 1610612736 | bytes 11665412 | tf_op jit(solution)/shard_map/serve/pallas_call | solution.py:38
  50.4 6.3 %all-to-all-start.1 = ((bf16[64,96,128]{2,1,0:T(8,128)(2,1)}), bf16[64,96,128]{2,1,0:T(8,128)(2,1)S(1)}, u32[]{:S(2)}, u32[]{:S(2)}) async-start(bf16[64,96,128]{2,1,0:T(8,128)(2,1)} %get-tuple-element.11), calls=%async_computation.1 | async-start | bytes 3145728 | tf_op jit(solution)/shard_map/all_to_all | solution.py:281
  56.7 0.0 copy-start.4
  56.7 0.0 copy-start.6
  56.7 3.4 %prepare.1 = (bf16[4096,1024]{1,0:T(8,128)(2,1)}, f32[8,128]{1,0:T(8,128)S(1)}) custom-call(s32[1]{0:T(128)} %bitcast.me, bf16[64,72,128]{2,1,0:T(8,128)(2,1)S(1)} %all-to-all-done.message, bf16[1024,256]{1,0:T(8,128)(2,1)S(1)} %get-tuple-element.12.own_x, bf16[4096,1024]{1,0:T(8,128)(2,1)} %mask_tiles.1.bank), custom_call_target="tpu_custom_call", output_to_operand_aliasing={{0}: (3, {})} | custom-call | flops 536870912 | bytes 18485252 | tf_op jit(solution)/shard_map/prepare/pallas_call | solution.py:38
  60.1 35.1 %all-to-all-done.1.message = bf16[64,96,128]{2,1,0:T(8,128)(2,1)S(1)} async-done(((bf16[64,96,128]{2,1,0:T(8,128)(2,1)}), bf16[64,96,128]{2,1,0:T(8,128)(2,1)S(1)}, u32[]{:S(2)}, u32[]{:S(2)}) %all-to-all-start.1) | async-done | bytes 1572896 | tf_op jit(solution)/shard_map/all_to_all | solution.py:281
  95.2 0.0 copy-done.4
  95.2 0.0 copy-done.6
  95.2 4.5 %first_layer.1 = (bf16[1024,256]{1,0:T(8,128)(2,1)}, bf16[64,32,128]{2,1,0:T(8,128)(2,1)}) custom-call(bf16[64,96,128]{2,1,0:T(8,128)(2,1)S(1)} %all-to-all-done.1.message, bf16[4096,1024]{1,0:T(8,128)(2,1)} %get-tuple-element.13.bank, f32[8,128]{1,0:T(8,128)S(1)} %get-tuple-element.14.numbers, bf16[256,256]{1,0:T(8,128)(2,1)S(1)} %copy-done.4, ...), custom_call_target="tpu_custom_call" | custom-call | flops 1610612736 | bytes 11146240 | tf_op jit(solution)/shard_map/first_layer/pallas_call | solution.py:38
  99.7 7.0 %all-to-all-start.2 = ((bf16[64,32,128]{2,1,0:T(8,128)(2,1)}), bf16[64,32,128]{2,1,0:T(8,128)(2,1)S(1)}, u32[]{:S(2)}, u32[]{:S(2)}) async-start(bf16[64,32,128]{2,1,0:T(8,128)(2,1)} %get-tuple-element.16), calls=%async_computation.2 | async-start | bytes 1048576 | tf_op jit(solution)/shard_map/all_to_all | solution.py:281
  106.6 0.0 copy-start.3
  106.7 1.0 copy-done.3
  107.7 3.5 %second_terms.1.partial = f32[1024,256]{1,0:T(8,128)S(1)} custom-call(bf16[64,96,128]{2,1,0:T(8,128)(2,1)S(1)} %all-to-all-done.1.message, bf16[1024,256]{1,0:T(8,128)(2,1)S(1)} %copy-done.3, bf16[4096,1024]{1,0:T(8,128)(2,1)} %get-tuple-element.13.bank), custom_call_target="tpu_custom_call" | custom-call | flops 1073741824 | bytes 11534336 | tf_op jit(solution)/shard_map/second_terms/pallas_call | solution.py:38
  111.2 0.0 copy-start.7
  111.2 12.8 %all-to-all-done.2.message = bf16[64,32,128]{2,1,0:T(8,128)(2,1)S(1)} async-done(((bf16[64,32,128]{2,1,0:T(8,128)(2,1)}), bf16[64,32,128]{2,1,0:T(8,128)(2,1)S(1)}, u32[]{:S(2)}, u32[]{:S(2)}) %all-to-all-start.2) | async-done | bytes 524320 | tf_op jit(solution)/shard_map/all_to_all | solution.py:281
  124.0 1.6 second_layer.1
  125.7 0.3 collective-permute-start
  125.9 1.3 collective-permute-done
  127.3 13.7 %all_to_all.25 = bf16[32,4,256]{2,1,0:T(4,128)(2,1)S(1)} all-to-all(bf16[32,4,256]{2,1,0:T(4,128)(2,1)S(1)} %reshape.29), channel_id=1, replica_groups=mesh['dev_0'=8,'dev_1'=4,'dev_2'=2,'rep'=4] {'dev_0','dev_1'}, dimensions={0} | all-to-all | bytes 131072 | tf_op jit(solution)/shard_map/all_to_all | solution.py:294
  141.1 0.1 convert_reduce_fusion
  141.1 2.8 %collective-permute-start.2 = (f32[4,256]{1,0:T(4,128)S(1)}, f32[4,256]{1,0:T(4,128)S(1)}, u32[]{:S(2)}, u32[]{:S(2)}) collective-permute-start(f32[4,256]{1,0:T(4,128)S(1)} %convert_reduce_fusion), channel_id=1, source_target_pairs={{0,2},{1,3},{2,0},{3,1},{4,6},{5,7},{6,4},{7,5},{8,10},{9,11},{10,... | collective-permute-start | bytes 12296 | tf_op jit(solution)/shard_map/ppermute | solution.py:285
  143.9 0.9 collective-permute-start.3
  144.8 0.0 collective-permute-start.1
  144.8 0.4 collective-permute-done.2
  145.2 2.5 %collective-permute-done.3 = f32[4,256]{1,0:T(4,128)S(1)} collective-permute-done((f32[4,256]{1,0:T(4,128)S(1)}, f32[4,256]{1,0:T(4,128)S(1)}, u32[]{:S(2)}, u32[]{:S(2)}) %collective-permute-start.3) | collective-permute-done | bytes 4128 | tf_op jit(solution)/shard_map/ppermute | solution.py:285
  147.7 0.0 collective-permute-done.1
  147.7 0.7 broadcast_in_dim.2
  148.4 3.9 %all-to-all-start.4 = ((bf16[32,4,256]{2,1,0:T(4,128)(2,1)}), bf16[32,4,256]{2,1,0:T(4,128)(2,1)S(1)}, u32[]{:S(2)}, u32[]{:S(2)}) async-start(bf16[32,4,256]{2,1,0:T(4,128)(2,1)} %broadcast_in_dim.2), calls=%async_computation.4 | async-start | bytes 131072 | tf_op jit(solution)/shard_map/all_to_all | solution.py:298
  152.2 8.9 %all-to-all-done.4 = bf16[32,4,256]{2,1,0:T(4,128)(2,1)S(1)} async-done(((bf16[32,4,256]{2,1,0:T(4,128)(2,1)}), bf16[32,4,256]{2,1,0:T(4,128)(2,1)S(1)}, u32[]{:S(2)}, u32[]{:S(2)}) %all-to-all-start.4) | async-done | bytes 65568 | tf_op jit(solution)/shard_map/all_to_all | solution.py:298
  161.1 4.4 %collective-permute-start.4 = (bf16[128,256]{1,0:T(8,128)(2,1)S(1)}, bf16[128,256]{1,0:T(8,128)(2,1)S(1)}, u32[]{:S(2)}, u32[]{:S(2)}) collective-permute-start(bf16[128,256]{1,0:T(8,128)(2,1)S(1)} %reshape.30), channel_id=1, source_target_pairs={{0,4},{4,0},{1,5},{5,1},{2,6},{6,2},{3,7},{7,3},{8,12},{12,8},{9,1... | collective-permute-start | bytes 196616 | tf_op jit(solution)/shard_map/ppermute | solution.py:285
  165.5 0.0 copy-done.7
  165.5 1.1 convolution_convert_fusion
  166.6 0.0 collective-permute-done.4
  166.6 0.7 maximum_convert_fusion
  (6 shorter events, 0.1 us)
Async XLA Ops:
  3.0 13.4 %copy-start.2 = (bf16[1024,256]{1,0:T(8,128)(2,1)S(1)}, bf16[1024,256]{1,0:T(8,128)(2,1)}, u32[]{:S(2)}) copy-start(bf16[1024,256]{1,0:T(8,128)(2,1)} %cotangent.1) | copy-start | bytes 1572868
  3.0 13.4 %copy-start.5 = (s32[8,16]{1,0:T(8,128)S(1)}, s32[8,16]{1,0:T(8,128)}, u32[]{:S(2)}) copy-start(s32[8,16]{1,0:T(8,128)} %occupied.1) | copy-start | bytes 1540
  3.0 44.2 %all-to-all-start = ((bf16[64,72,128]{2,1,0:T(8,128)(2,1)}), bf16[64,72,128]{2,1,0:T(8,128)(2,1)S(1)}, u32[]{:S(2)}, u32[]{:S(2)}) async-start(bf16[64,72,128]{2,1,0:T(8,128)(2,1)} %send_clusters.1), calls=%async_computation | async-start | bytes 2359296 | tf_op jit(solution)/shard_map/all_to_all | solution.py:281
  16.4 1.6 copy-start
  18.0 1.6 copy-start.1
  50.4 44.8 %all-to-all-start.1 = ((bf16[64,96,128]{2,1,0:T(8,128)(2,1)}), bf16[64,96,128]{2,1,0:T(8,128)(2,1)S(1)}, u32[]{:S(2)}, u32[]{:S(2)}) async-start(bf16[64,96,128]{2,1,0:T(8,128)(2,1)} %get-tuple-element.11), calls=%async_computation.1 | async-start | bytes 3145728 | tf_op jit(solution)/shard_map/all_to_all | solution.py:281
  56.7 38.5 %copy-start.4 = (bf16[256,256]{1,0:T(8,128)(2,1)S(1)}, bf16[256,256]{1,0:T(8,128)(2,1)}, u32[]{:S(2)}) copy-start(bf16[256,256]{1,0:T(8,128)(2,1)} %w.1) | copy-start | bytes 393220
  56.7 38.5 %copy-start.6 = (f32[256]{0:T(256)S(1)}, f32[256]{0:T(256)}, u32[]{:S(2)}) copy-start(f32[256]{0:T(256)} %param.19) | copy-start | bytes 3076
  99.7 24.3 %all-to-all-start.2 = ((bf16[64,32,128]{2,1,0:T(8,128)(2,1)}), bf16[64,32,128]{2,1,0:T(8,128)(2,1)S(1)}, u32[]{:S(2)}, u32[]{:S(2)}) async-start(bf16[64,32,128]{2,1,0:T(8,128)(2,1)} %get-tuple-element.16), calls=%async_computation.2 | async-start | bytes 1048576 | tf_op jit(solution)/shard_map/all_to_all | solution.py:281
  106.6 1.0 copy-start.3
  111.2 54.3 %copy-start.7 = (bf16[256,256]{1,0:T(8,128)(2,1)S(1)}, bf16[256,256]{1,0:T(8,128)(2,1)}, u32[]{:S(2)}) copy-start(bf16[256,256]{1,0:T(8,128)(2,1)} %param.20) | copy-start | bytes 393220
  125.7 1.6 collective-permute-start
  141.1 4.0 %collective-permute-start.2 = (f32[4,256]{1,0:T(4,128)S(1)}, f32[4,256]{1,0:T(4,128)S(1)}, u32[]{:S(2)}, u32[]{:S(2)}) collective-permute-start(f32[4,256]{1,0:T(4,128)S(1)} %convert_reduce_fusion), channel_id=1, source_target_pairs={{0,2},{1,3},{2,0},{3,1},{4,6},{5,7},{6,4},{7,5},{8,10},{9,11},{10,... | collective-permute-start | bytes 12296 | tf_op jit(solution)/shard_map/ppermute | solution.py:285
  143.9 3.8 %collective-permute-start.3 = (f32[4,256]{1,0:T(4,128)S(1)}, f32[4,256]{1,0:T(4,128)S(1)}, u32[]{:S(2)}, u32[]{:S(2)}) collective-permute-start(f32[4,256]{1,0:T(4,128)S(1)} %convert_reduce_fusion), channel_id=1, source_target_pairs={{0,3},{1,2},{2,1},{3,0},{4,7},{5,6},{6,5},{7,4},{8,11},{9,10},{10,... | collective-permute-start | bytes 12296 | tf_op jit(solution)/shard_map/ppermute | solution.py:285
  144.8 2.9 %collective-permute-start.1 = (f32[4,256]{1,0:T(4,128)S(1)}, f32[4,256]{1,0:T(4,128)S(1)}, u32[]{:S(2)}, u32[]{:S(2)}) collective-permute-start(f32[4,256]{1,0:T(4,128)S(1)} %convert_reduce_fusion), channel_id=1, source_target_pairs={{0,1},{1,0},{2,3},{3,2},{4,5},{5,4},{6,7},{7,6},{8,9},{9,8},{10,11... | collective-permute-start | bytes 12296 | tf_op jit(solution)/shard_map/ppermute | solution.py:285
  148.4 12.7 %all-to-all-start.4 = ((bf16[32,4,256]{2,1,0:T(4,128)(2,1)}), bf16[32,4,256]{2,1,0:T(4,128)(2,1)S(1)}, u32[]{:S(2)}, u32[]{:S(2)}) async-start(bf16[32,4,256]{2,1,0:T(4,128)(2,1)} %broadcast_in_dim.2), calls=%async_computation.4 | async-start | bytes 131072 | tf_op jit(solution)/shard_map/all_to_all | solution.py:298
  161.1 5.5 %collective-permute-start.4 = (bf16[128,256]{1,0:T(8,128)(2,1)S(1)}, bf16[128,256]{1,0:T(8,128)(2,1)S(1)}, u32[]{:S(2)}, u32[]{:S(2)}) collective-permute-start(bf16[128,256]{1,0:T(8,128)(2,1)S(1)} %reshape.30), channel_id=1, source_target_pairs={{0,4},{4,0},{1,5},{5,1},{2,6},{6,2},{3,7},{7,3},{8,12},{12,8},{9,1... | collective-permute-start | bytes 196616 | tf_op jit(solution)/shard_map/ppermute | solution.py:285

commit v7 on v6

--- a/solution.py
+++ b/solution.py
@@ -292,14 +292,14 @@
     sent = lax.dynamic_index_in_dim(halves, 1 - core, 0, keepdims=False)
     half = (kept_half + swapped(sent, "dev_2", 1)).astype(BF16)
     tiles = lax.all_to_all(half.reshape(32, 4, F), CHIPS, split_axis=0, concat_axis=0, tiled=True)
-    own = jnp.sum(tiles.astype(F32), axis=0)
-    own = (own + swapped(own, "rep", 1)) + (swapped(own, "rep", 2) + swapped(own, "rep", 3))
-    copies = jnp.broadcast_to(own.astype(BF16)[None], (32, 4, F))
-    mine = lax.all_to_all(copies, CHIPS, split_axis=0, concat_axis=0, tiled=True).reshape(128, F)
+    own = lax.optimization_barrier(jnp.sum(tiles.astype(F32), axis=0)).astype(BF16)
+    copies = jnp.broadcast_to(own[None], (128, 4, F))
+    all_terms = lax.all_to_all(copies, (*CHIPS, "rep"), split_axis=0, concat_axis=0, tiled=True)
+    mine = jnp.sum(all_terms.reshape(32, 4, 4, F).astype(F32), axis=1).reshape(128, F)
     other = swapped(mine, "dev_2", 1)
     first = jnp.where(core == 0, mine, other)
     second = jnp.where(core == 0, other, mine)
-    return jnp.concatenate([first, second], axis=0).astype(F32)
+    return jnp.concatenate([first, second], axis=0)
 
 
 def body(

time: 168 us -> 168 us (level)
    ppermute x5 -> x2, starting transfers between devices: 8.32 us -> 4.06 us  [swapped(): lax.ppermute(array, axis, [(i, i ^ mask) for i in range(lax.axis_size(axi...]
    all_to_all x1, starting transfers between devices: 3.86 us -> 7.62 us  [summed_everywhere(): lax.all_to_all(copies, (*CHIPS, 'rep'), split_axis=0, concat_axis=0, tile...]
    all_to_all x1, waiting for transfers between devices: 8.87 us -> 12.4 us  [summed_everywhere(): lax.all_to_all(copies, (*CHIPS, 'rep'), split_axis=0, concat_axis=0, tile...]
    ppermute x5 -> x2, waiting for transfers between devices: 4.24 us -> 1.34 us  [swapped(): lax.ppermute(array, axis, [(i, i ^ mask) for i in range(lax.axis_size(axi...]
  transfers between devices with their start and end apart: 9 -> 6, of which waited for: 7 -> 5; matrix products, arithmetic and copies ran while one was open for 1% -> 1% of each run, Pallas kernels for 7% -> 7%
where the time goes in v7:
time: 168 us
  waiting for transfers between devices  84.4 us (50%)
  starting transfers between devices  38.3 us (23%)
  Pallas kernels  23.3 us (14%)
  blocking collectives  13.7 us (8%)
  local copies, waits for them, and re-layouts  5.11 us (3%)
    all_to_all x3, waiting for transfers between devices, exchange(): lax.all_to_all(message, ORDER, split_axis=0, concat_axis=0, tiled=True)  70.7 us
    all_to_all x3, starting transfers between devices, exchange(): lax.all_to_all(message, ORDER, split_axis=0, concat_axis=0, tiled=True)  26.6 us
    pallas_call x7, Pallas kernels, call(): pl.pallas_call(body, out_shape=outs, in_specs=specs[:len(operands)], out_...  23.3 us
    all_to_all x1, blocking collectives, summed_everywhere(): lax.all_to_all(half.reshape(32, 4, F), CHIPS, split_axis=0, concat_axis=0...  13.7 us
    all_to_all x1, waiting for transfers between devices, summed_everywhere(): lax.all_to_all(copies, (*CHIPS, 'rep'), split_axis=0, concat_axis=0, tile...  12.4 us
    all_to_all x1, starting transfers between devices, summed_everywhere(): lax.all_to_all(copies, (*CHIPS, 'rep'), split_axis=0, concat_axis=0, tile...  7.62 us
    unnamed x16, local copies, waits for them, and re-layouts  4.25 us
    ppermute x2, starting transfers between devices, swapped(): lax.ppermute(array, axis, [(i, i ^ mask) for i in range(lax.axis_size(axi...  4.06 us
  transfers between devices with their start and end apart: 6, of which 5 were waited for; matrix products, arithmetic and copies ran while one was open for 1% of the time, Pallas kernels for 7%

profile of v7, /device:TPU:1, one launch (start us, length us, event | category | flops | bytes accessed | tf_op | source)
XLA Modules:
  0.0 167.8 jit_solution(11556856933675564724)
XLA Ops:
  0.6 2.3 %send_clusters.1 = bf16[64,72,128]{2,1,0:T(8,128)(2,1)} custom-call(s32[1,64]{1,0:T(1,128)} %owner.1, bf16[1024,256]{1,0:T(8,128)(2,1)} %x.1, bf16[1024,256]{1,0:T(8,128)(2,1)} %h.1, s32[8,128]{1,0:T(8,128)} %bitcast.18), custom_call_target="tpu_custom_call" | custom-call | flops 262144 | bytes 2232576 | tf_op jit(solution)/shard_map/send_clusters/pallas_call | solution.py:38
  3.0 0.0 copy-start.2
  3.0 0.0 copy-start.5
  3.0 13.4 %all-to-all-start = ((bf16[64,72,128]{2,1,0:T(8,128)(2,1)}), bf16[64,72,128]{2,1,0:T(8,128)(2,1)S(1)}, u32[]{:S(2)}, u32[]{:S(2)}) async-start(bf16[64,72,128]{2,1,0:T(8,128)(2,1)} %send_clusters.1), calls=%async_computation | async-start | bytes 2359296 | tf_op jit(solution)/shard_map/all_to_all | solution.py:281
  16.4 0.0 copy-done.2
  16.4 0.0 copy-done.5
  16.4 0.0 copy-start
  16.4 1.6 copy-done
  18.0 0.0 copy-start.1
  18.0 1.6 copy-done.1
  19.6 4.8 %mask_tiles.1.bank = bf16[4096,1024]{1,0:T(8,128)(2,1)} custom-call(s32[8,16]{1,0:T(8,128)S(1)} %copy-done.5, bf16[1024,1024]{1,0:T(8,128)(2,1)S(1)} %copy-done, bf16[1024,1024]{1,0:T(8,128)(2,1)S(1)} %copy-done.1, bf16[1024,256]{1,0:T(8,128)(2,1)S(1)} %copy-done.2), custom_call_target="tpu_custom_call" | custom-call | flops 536870912 | bytes 13107712 | tf_op jit(solution)/shard_map/mask_tiles/pallas_call | solution.py:38
  24.4 22.8 %all-to-all-done.message = bf16[64,72,128]{2,1,0:T(8,128)(2,1)S(1)} async-done(((bf16[64,72,128]{2,1,0:T(8,128)(2,1)}), bf16[64,72,128]{2,1,0:T(8,128)(2,1)S(1)}, u32[]{:S(2)}, u32[]{:S(2)}) %all-to-all-start) | async-done | bytes 1179680 | tf_op jit(solution)/shard_map/all_to_all | solution.py:281
  47.2 3.2 %serve.1 = (bf16[1024,256]{1,0:T(8,128)(2,1)S(1)}, bf16[64,96,128]{2,1,0:T(8,128)(2,1)}) custom-call(s32[1]{0:T(128)} %bitcast.me, bf16[64,72,128]{2,1,0:T(8,128)(2,1)S(1)} %all-to-all-done.message, bf16[4096,1024]{1,0:T(8,128)(2,1)} %mask_tiles.1.bank), custom_call_target="tpu_custom_call" | custom-call | flops 1610612736 | bytes 11665412 | tf_op jit(solution)/shard_map/serve/pallas_call | solution.py:38
  50.4 6.3 %all-to-all-start.1 = ((bf16[64,96,128]{2,1,0:T(8,128)(2,1)}), bf16[64,96,128]{2,1,0:T(8,128)(2,1)S(1)}, u32[]{:S(2)}, u32[]{:S(2)}) async-start(bf16[64,96,128]{2,1,0:T(8,128)(2,1)} %get-tuple-element.11), calls=%async_computation.1 | async-start | bytes 3145728 | tf_op jit(solution)/shard_map/all_to_all | solution.py:281
  56.7 0.0 copy-start.4
  56.7 0.0 copy-start.6
  56.7 3.4 %prepare.1 = (bf16[4096,1024]{1,0:T(8,128)(2,1)}, f32[8,128]{1,0:T(8,128)S(1)}) custom-call(s32[1]{0:T(128)} %bitcast.me, bf16[64,72,128]{2,1,0:T(8,128)(2,1)S(1)} %all-to-all-done.message, bf16[1024,256]{1,0:T(8,128)(2,1)S(1)} %get-tuple-element.12.own_x, bf16[4096,1024]{1,0:T(8,128)(2,1)} %mask_tiles.1.bank), custom_call_target="tpu_custom_call", output_to_operand_aliasing={{0}: (3, {})} | custom-call | flops 536870912 | bytes 18485252 | tf_op jit(solution)/shard_map/prepare/pallas_call | solution.py:38
  60.1 35.1 %all-to-all-done.1.message = bf16[64,96,128]{2,1,0:T(8,128)(2,1)S(1)} async-done(((bf16[64,96,128]{2,1,0:T(8,128)(2,1)}), bf16[64,96,128]{2,1,0:T(8,128)(2,1)S(1)}, u32[]{:S(2)}, u32[]{:S(2)}) %all-to-all-start.1) | async-done | bytes 1572896 | tf_op jit(solution)/shard_map/all_to_all | solution.py:281
  95.2 0.0 copy-done.4
  95.2 0.0 copy-done.6
  95.2 4.5 %first_layer.1 = (bf16[1024,256]{1,0:T(8,128)(2,1)}, bf16[64,32,128]{2,1,0:T(8,128)(2,1)}) custom-call(bf16[64,96,128]{2,1,0:T(8,128)(2,1)S(1)} %all-to-all-done.1.message, bf16[4096,1024]{1,0:T(8,128)(2,1)} %get-tuple-element.13.bank, f32[8,128]{1,0:T(8,128)S(1)} %get-tuple-element.14.numbers, bf16[256,256]{1,0:T(8,128)(2,1)S(1)} %copy-done.4, ...), custom_call_target="tpu_custom_call" | custom-call | flops 1610612736 | bytes 11146240 | tf_op jit(solution)/shard_map/first_layer/pallas_call | solution.py:38
  99.7 7.0 %all-to-all-start.2 = ((bf16[64,32,128]{2,1,0:T(8,128)(2,1)}), bf16[64,32,128]{2,1,0:T(8,128)(2,1)S(1)}, u32[]{:S(2)}, u32[]{:S(2)}) async-start(bf16[64,32,128]{2,1,0:T(8,128)(2,1)} %get-tuple-element.16), calls=%async_computation.2 | async-start | bytes 1048576 | tf_op jit(solution)/shard_map/all_to_all | solution.py:281
  106.7 0.0 copy-start.3
  106.7 1.0 copy-done.3
  107.7 3.5 %second_terms.1.partial = f32[1024,256]{1,0:T(8,128)S(1)} custom-call(bf16[64,96,128]{2,1,0:T(8,128)(2,1)S(1)} %all-to-all-done.1.message, bf16[1024,256]{1,0:T(8,128)(2,1)S(1)} %copy-done.3, bf16[4096,1024]{1,0:T(8,128)(2,1)} %get-tuple-element.13.bank), custom_call_target="tpu_custom_call" | custom-call | flops 1073741824 | bytes 11534336 | tf_op jit(solution)/shard_map/second_terms/pallas_call | solution.py:38
  111.2 12.8 %all-to-all-done.2.message = bf16[64,32,128]{2,1,0:T(8,128)(2,1)S(1)} async-done(((bf16[64,32,128]{2,1,0:T(8,128)(2,1)}), bf16[64,32,128]{2,1,0:T(8,128)(2,1)S(1)}, u32[]{:S(2)}, u32[]{:S(2)}) %all-to-all-start.2) | async-done | bytes 524320 | tf_op jit(solution)/shard_map/all_to_all | solution.py:281
  124.0 1.7 second_layer.1
  125.7 0.0 copy-start.7
  125.7 0.3 collective-permute-start
  126.0 1.3 collective-permute-done
  127.4 13.7 %all_to_all.25 = bf16[32,4,256]{2,1,0:T(4,128)(2,1)S(1)} all-to-all(bf16[32,4,256]{2,1,0:T(4,128)(2,1)S(1)} %reshape.32), channel_id=1, replica_groups=mesh['dev_0'=8,'dev_1'=4,'dev_2'=2,'rep'=4] {'dev_0','dev_1'}, dimensions={0} | all-to-all | bytes 131072 | tf_op jit(solution)/shard_map/all_to_all | solution.py:294
  141.1 0.1 convert_reduce_fusion.1
  141.2 0.8 broadcast_in_dim.2
  141.9 7.6 %all-to-all-start.4 = ((bf16[128,4,256]{2,1,0:T(4,128)(2,1)}), bf16[128,4,256]{2,1,0:T(4,128)(2,1)S(1)}, u32[]{:S(2)}, u32[]{:S(2)}) async-start(bf16[128,4,256]{2,1,0:T(4,128)(2,1)} %broadcast_in_dim.2), calls=%async_computation.4 | async-start | bytes 524288 | tf_op jit(solution)/shard_map/all_to_all | solution.py:297
  149.6 12.4 %all-to-all-done.4 = bf16[128,4,256]{2,1,0:T(4,128)(2,1)S(1)} async-done(((bf16[128,4,256]{2,1,0:T(4,128)(2,1)}), bf16[128,4,256]{2,1,0:T(4,128)(2,1)S(1)}, u32[]{:S(2)}, u32[]{:S(2)}) %all-to-all-start.4) | async-done | bytes 262176 | tf_op jit(solution)/shard_map/all_to_all | solution.py:297
  162.0 0.1 convert_reduce_fusion
  162.2 3.8 %collective-permute-start.1 = (f32[128,256]{1,0:T(8,128)S(1)}, f32[128,256]{1,0:T(8,128)S(1)}, u32[]{:S(2)}, u32[]{:S(2)}) collective-permute-start(f32[128,256]{1,0:T(8,128)S(1)} %reshape.33), channel_id=1, source_target_pairs={{0,4},{4,0},{1,5},{5,1},{2,6},{6,2},{3,7},{7,3},{8,12},{12,8},{9,1... | collective-permute-start | bytes 393224 | tf_op jit(solution)/shard_map/ppermute | solution.py:285
  165.9 0.0 copy-done.7
  166.0 1.1 convolution_convert_fusion
  167.0 0.0 collective-permute-done.1
  167.1 0.7 pad_maximum_fusion
  (5 shorter events, 0.1 us)
Async XLA Ops:
  3.0 13.4 %copy-start.2 = (bf16[1024,256]{1,0:T(8,128)(2,1)S(1)}, bf16[1024,256]{1,0:T(8,128)(2,1)}, u32[]{:S(2)}) copy-start(bf16[1024,256]{1,0:T(8,128)(2,1)} %cotangent.1) | copy-start | bytes 1572868
  3.0 13.4 %copy-start.5 = (s32[8,16]{1,0:T(8,128)S(1)}, s32[8,16]{1,0:T(8,128)}, u32[]{:S(2)}) copy-start(s32[8,16]{1,0:T(8,128)} %occupied.1) | copy-start | bytes 1540
  3.0 44.2 %all-to-all-start = ((bf16[64,72,128]{2,1,0:T(8,128)(2,1)}), bf16[64,72,128]{2,1,0:T(8,128)(2,1)S(1)}, u32[]{:S(2)}, u32[]{:S(2)}) async-start(bf16[64,72,128]{2,1,0:T(8,128)(2,1)} %send_clusters.1), calls=%async_computation | async-start | bytes 2359296 | tf_op jit(solution)/shard_map/all_to_all | solution.py:281
  16.4 1.6 copy-start
  18.0 1.6 copy-start.1
  50.4 44.8 %all-to-all-start.1 = ((bf16[64,96,128]{2,1,0:T(8,128)(2,1)}), bf16[64,96,128]{2,1,0:T(8,128)(2,1)S(1)}, u32[]{:S(2)}, u32[]{:S(2)}) async-start(bf16[64,96,128]{2,1,0:T(8,128)(2,1)} %get-tuple-element.11), calls=%async_computation.1 | async-start | bytes 3145728 | tf_op jit(solution)/shard_map/all_to_all | solution.py:281
  56.7 38.5 %copy-start.4 = (bf16[256,256]{1,0:T(8,128)(2,1)S(1)}, bf16[256,256]{1,0:T(8,128)(2,1)}, u32[]{:S(2)}) copy-start(bf16[256,256]{1,0:T(8,128)(2,1)} %w.1) | copy-start | bytes 393220
  56.7 38.5 %copy-start.6 = (f32[256]{0:T(256)S(1)}, f32[256]{0:T(256)}, u32[]{:S(2)}) copy-start(f32[256]{0:T(256)} %param.19) | copy-start | bytes 3076
  99.7 24.3 %all-to-all-start.2 = ((bf16[64,32,128]{2,1,0:T(8,128)(2,1)}), bf16[64,32,128]{2,1,0:T(8,128)(2,1)S(1)}, u32[]{:S(2)}, u32[]{:S(2)}) async-start(bf16[64,32,128]{2,1,0:T(8,128)(2,1)} %get-tuple-element.16), calls=%async_computation.2 | async-start | bytes 1048576 | tf_op jit(solution)/shard_map/all_to_all | solution.py:281
  106.7 1.0 copy-start.3
  125.7 40.3 %copy-start.7 = (bf16[256,256]{1,0:T(8,128)(2,1)S(1)}, bf16[256,256]{1,0:T(8,128)(2,1)}, u32[]{:S(2)}) copy-start(bf16[256,256]{1,0:T(8,128)(2,1)} %param.20) | copy-start | bytes 393220
  125.7 1.6 collective-permute-start
  141.9 20.0 %all-to-all-start.4 = ((bf16[128,4,256]{2,1,0:T(4,128)(2,1)}), bf16[128,4,256]{2,1,0:T(4,128)(2,1)S(1)}, u32[]{:S(2)}, u32[]{:S(2)}) async-start(bf16[128,4,256]{2,1,0:T(4,128)(2,1)} %broadcast_in_dim.2), calls=%async_computation.4 | async-start | bytes 524288 | tf_op jit(solution)/shard_map/all_to_all | solution.py:297
  162.2 4.9 %collective-permute-start.1 = (f32[128,256]{1,0:T(8,128)S(1)}, f32[128,256]{1,0:T(8,128)S(1)}, u32[]{:S(2)}, u32[]{:S(2)}) collective-permute-start(f32[128,256]{1,0:T(8,128)S(1)} %reshape.33), channel_id=1, source_target_pairs={{0,4},{4,0},{1,5},{5,1},{2,6},{6,2},{3,7},{7,3},{8,12},{12,8},{9,1... | collective-permute-start | bytes 393224 | tf_op jit(solution)/shard_map/ppermute | solution.py:285

commit v8 on v6

--- a/solution.py
+++ b/solution.py
@@ -293,7 +293,8 @@
     half = (kept_half + swapped(sent, "dev_2", 1)).astype(BF16)
     tiles = lax.all_to_all(half.reshape(32, 4, F), CHIPS, split_axis=0, concat_axis=0, tiled=True)
     own = jnp.sum(tiles.astype(F32), axis=0)
-    own = (own + swapped(own, "rep", 1)) + (swapped(own, "rep", 2) + swapped(own, "rep", 3))
+    own = own + swapped(own, "rep", 1)
+    own = own + swapped(own, "rep", 3)
     copies = jnp.broadcast_to(own.astype(BF16)[None], (32, 4, F))
     mine = lax.all_to_all(copies, CHIPS, split_axis=0, concat_axis=0, tiled=True).reshape(128, F)
     other = swapped(mine, "dev_2", 1)

time: 168 us -> 169 us (level)
    ppermute x5 -> x4, starting transfers between devices: 8.32 us -> 9.37 us  [swapped(): lax.ppermute(array, axis, [(i, i ^ mask) for i in range(lax.axis_size(axi...]
    ppermute x5 -> x4, waiting for transfers between devices: 4.24 us -> 3.77 us  [swapped(): lax.ppermute(array, axis, [(i, i ^ mask) for i in range(lax.axis_size(axi...]
  transfers between devices with their start and end apart: 9 -> 8, of which waited for: 7 -> 7; matrix products, arithmetic and copies ran while one was open for 1% -> 1% of each run, Pallas kernels for 7% -> 7%
where the time goes in v8:
time: 169 us; the launch traced here: 168 us
  waiting for transfers between devices  83.3 us (49%)
  starting transfers between devices  39.9 us (24%)
  Pallas kernels  23.3 us (14%)
  blocking collectives  13.7 us (8%)
  local copies, waits for them, and re-layouts  4.96 us (3%)
    all_to_all x3, waiting for transfers between devices, exchange(): lax.all_to_all(message, ORDER, split_axis=0, concat_axis=0, tiled=True)  70.7 us
    all_to_all x3, starting transfers between devices, exchange(): lax.all_to_all(message, ORDER, split_axis=0, concat_axis=0, tiled=True)  26.6 us
    pallas_call x7, Pallas kernels, call(): pl.pallas_call(body, out_shape=outs, in_specs=specs[:len(operands)], out_...  23.3 us
    all_to_all x1, blocking collectives, summed_everywhere(): lax.all_to_all(half.reshape(32, 4, F), CHIPS, split_axis=0, concat_axis=0...  13.7 us
    ppermute x4, starting transfers between devices, swapped(): lax.ppermute(array, axis, [(i, i ^ mask) for i in range(lax.axis_size(axi...  9.37 us
    all_to_all x1, waiting for transfers between devices, summed_everywhere(): lax.all_to_all(copies, CHIPS, split_axis=0, concat_axis=0, tiled=True)  8.87 us
    unnamed x16, local copies, waits for them, and re-layouts  4.25 us
    all_to_all x1, starting transfers between devices, summed_everywhere(): lax.all_to_all(copies, CHIPS, split_axis=0, concat_axis=0, tiled=True)  3.86 us
  transfers between devices with their start and end apart: 8, of which 7 were waited for; matrix products, arithmetic and copies ran while one was open for 1% of the time, Pallas kernels for 7%

profile of v8, /device:TPU:1, one launch (start us, length us, event | category | flops | bytes accessed | tf_op | source)
XLA Modules:
  0.0 167.9 jit_solution(11088355520258144214)
XLA Ops:
  0.6 2.3 %send_clusters.1 = bf16[64,72,128]{2,1,0:T(8,128)(2,1)} custom-call(s32[1,64]{1,0:T(1,128)} %owner.1, bf16[1024,256]{1,0:T(8,128)(2,1)} %x.1, bf16[1024,256]{1,0:T(8,128)(2,1)} %h.1, s32[8,128]{1,0:T(8,128)} %bitcast.15), custom_call_target="tpu_custom_call" | custom-call | flops 262144 | bytes 2232576 | tf_op jit(solution)/shard_map/send_clusters/pallas_call | solution.py:38
  3.0 0.0 copy-start.2
  3.0 0.0 copy-start.5
  3.0 13.4 %all-to-all-start = ((bf16[64,72,128]{2,1,0:T(8,128)(2,1)}), bf16[64,72,128]{2,1,0:T(8,128)(2,1)S(1)}, u32[]{:S(2)}, u32[]{:S(2)}) async-start(bf16[64,72,128]{2,1,0:T(8,128)(2,1)} %send_clusters.1), calls=%async_computation | async-start | bytes 2359296 | tf_op jit(solution)/shard_map/all_to_all | solution.py:281
  16.4 0.0 copy-done.2
  16.4 0.0 copy-done.5
  16.4 0.0 copy-start
  16.4 1.6 copy-done
  18.0 0.0 copy-start.1
  18.0 1.6 copy-done.1
  19.6 4.8 %mask_tiles.1.bank = bf16[4096,1024]{1,0:T(8,128)(2,1)} custom-call(s32[8,16]{1,0:T(8,128)S(1)} %copy-done.5, bf16[1024,1024]{1,0:T(8,128)(2,1)S(1)} %copy-done, bf16[1024,1024]{1,0:T(8,128)(2,1)S(1)} %copy-done.1, bf16[1024,256]{1,0:T(8,128)(2,1)S(1)} %copy-done.2), custom_call_target="tpu_custom_call" | custom-call | flops 536870912 | bytes 13107712 | tf_op jit(solution)/shard_map/mask_tiles/pallas_call | solution.py:38
  24.4 22.8 %all-to-all-done.message = bf16[64,72,128]{2,1,0:T(8,128)(2,1)S(1)} async-done(((bf16[64,72,128]{2,1,0:T(8,128)(2,1)}), bf16[64,72,128]{2,1,0:T(8,128)(2,1)S(1)}, u32[]{:S(2)}, u32[]{:S(2)}) %all-to-all-start) | async-done | bytes 1179680 | tf_op jit(solution)/shard_map/all_to_all | solution.py:281
  47.2 3.2 %serve.1 = (bf16[1024,256]{1,0:T(8,128)(2,1)S(1)}, bf16[64,96,128]{2,1,0:T(8,128)(2,1)}) custom-call(s32[1]{0:T(128)} %bitcast.me, bf16[64,72,128]{2,1,0:T(8,128)(2,1)S(1)} %all-to-all-done.message, bf16[4096,1024]{1,0:T(8,128)(2,1)} %mask_tiles.1.bank), custom_call_target="tpu_custom_call" | custom-call | flops 1610612736 | bytes 11665412 | tf_op jit(solution)/shard_map/serve/pallas_call | solution.py:38
  50.4 6.3 %all-to-all-start.1 = ((bf16[64,96,128]{2,1,0:T(8,128)(2,1)}), bf16[64,96,128]{2,1,0:T(8,128)(2,1)S(1)}, u32[]{:S(2)}, u32[]{:S(2)}) async-start(bf16[64,96,128]{2,1,0:T(8,128)(2,1)} %get-tuple-element.11), calls=%async_computation.1 | async-start | bytes 3145728 | tf_op jit(solution)/shard_map/all_to_all | solution.py:281
  56.7 0.0 copy-start.4
  56.7 0.0 copy-start.6
  56.7 3.4 %prepare.1 = (bf16[4096,1024]{1,0:T(8,128)(2,1)}, f32[8,128]{1,0:T(8,128)S(1)}) custom-call(s32[1]{0:T(128)} %bitcast.me, bf16[64,72,128]{2,1,0:T(8,128)(2,1)S(1)} %all-to-all-done.message, bf16[1024,256]{1,0:T(8,128)(2,1)S(1)} %get-tuple-element.12.own_x, bf16[4096,1024]{1,0:T(8,128)(2,1)} %mask_tiles.1.bank), custom_call_target="tpu_custom_call", output_to_operand_aliasing={{0}: (3, {})} | custom-call | flops 536870912 | bytes 18485252 | tf_op jit(solution)/shard_map/prepare/pallas_call | solution.py:38
  60.1 35.1 %all-to-all-done.1.message = bf16[64,96,128]{2,1,0:T(8,128)(2,1)S(1)} async-done(((bf16[64,96,128]{2,1,0:T(8,128)(2,1)}), bf16[64,96,128]{2,1,0:T(8,128)(2,1)S(1)}, u32[]{:S(2)}, u32[]{:S(2)}) %all-to-all-start.1) | async-done | bytes 1572896 | tf_op jit(solution)/shard_map/all_to_all | solution.py:281
  95.2 0.0 copy-done.4
  95.2 0.0 copy-done.6
  95.2 4.5 %first_layer.1 = (bf16[1024,256]{1,0:T(8,128)(2,1)}, bf16[64,32,128]{2,1,0:T(8,128)(2,1)}) custom-call(bf16[64,96,128]{2,1,0:T(8,128)(2,1)S(1)} %all-to-all-done.1.message, bf16[4096,1024]{1,0:T(8,128)(2,1)} %get-tuple-element.13.bank, f32[8,128]{1,0:T(8,128)S(1)} %get-tuple-element.14.numbers, bf16[256,256]{1,0:T(8,128)(2,1)S(1)} %copy-done.4, ...), custom_call_target="tpu_custom_call" | custom-call | flops 1610612736 | bytes 11146240 | tf_op jit(solution)/shard_map/first_layer/pallas_call | solution.py:38
  99.7 7.0 %all-to-all-start.2 = ((bf16[64,32,128]{2,1,0:T(8,128)(2,1)}), bf16[64,32,128]{2,1,0:T(8,128)(2,1)S(1)}, u32[]{:S(2)}, u32[]{:S(2)}) async-start(bf16[64,32,128]{2,1,0:T(8,128)(2,1)} %get-tuple-element.16), calls=%async_computation.2 | async-start | bytes 1048576 | tf_op jit(solution)/shard_map/all_to_all | solution.py:281
  106.6 0.0 copy-start.3
  106.7 1.0 copy-done.3
  107.7 3.5 %second_terms.1.partial = f32[1024,256]{1,0:T(8,128)S(1)} custom-call(bf16[64,96,128]{2,1,0:T(8,128)(2,1)S(1)} %all-to-all-done.1.message, bf16[1024,256]{1,0:T(8,128)(2,1)S(1)} %copy-done.3, bf16[4096,1024]{1,0:T(8,128)(2,1)} %get-tuple-element.13.bank), custom_call_target="tpu_custom_call" | custom-call | flops 1073741824 | bytes 11534336 | tf_op jit(solution)/shard_map/second_terms/pallas_call | solution.py:38
  111.2 0.0 copy-start.7
  111.2 12.8 %all-to-all-done.2.message = bf16[64,32,128]{2,1,0:T(8,128)(2,1)S(1)} async-done(((bf16[64,32,128]{2,1,0:T(8,128)(2,1)}), bf16[64,32,128]{2,1,0:T(8,128)(2,1)S(1)}, u32[]{:S(2)}, u32[]{:S(2)}) %all-to-all-start.2) | async-done | bytes 524320 | tf_op jit(solution)/shard_map/all_to_all | solution.py:281
  124.0 1.7 second_layer.1
  125.7 0.3 collective-permute-start
  126.0 1.3 collective-permute-done
  127.3 13.7 %all_to_all.25 = bf16[32,4,256]{2,1,0:T(4,128)(2,1)S(1)} all-to-all(bf16[32,4,256]{2,1,0:T(4,128)(2,1)S(1)} %reshape.29), channel_id=1, replica_groups=mesh['dev_0'=8,'dev_1'=4,'dev_2'=2,'rep'=4] {'dev_0','dev_1'}, dimensions={0} | all-to-all | bytes 131072 | tf_op jit(solution)/shard_map/all_to_all | solution.py:294
  141.1 0.1 convert_reduce_fusion
  141.1 1.3 collective-permute-start.1
  142.4 1.2 collective-permute-done.1
  143.7 2.5 %collective-permute-start.2 = (f32[4,256]{1,0:T(4,128)S(1)}, f32[4,256]{1,0:T(4,128)S(1)}, u32[]{:S(2)}, u32[]{:S(2)}) collective-permute-start(f32[4,256]{1,0:T(4,128)S(1)} %add.28), channel_id=1, source_target_pairs={{0,3},{1,2},{2,1},{3,0},{4,7},{5,6},{6,5},{7,4},{8,11},{9,10},{10,... | collective-permute-start | bytes 12296 | tf_op jit(solution)/shard_map/ppermute | solution.py:285
  146.1 1.2 collective-permute-done.2
  147.3 0.7 broadcast_in_dim.2
  148.0 3.9 %all-to-all-start.4 = ((bf16[32,4,256]{2,1,0:T(4,128)(2,1)}), bf16[32,4,256]{2,1,0:T(4,128)(2,1)S(1)}, u32[]{:S(2)}, u32[]{:S(2)}) async-start(bf16[32,4,256]{2,1,0:T(4,128)(2,1)} %broadcast_in_dim.2), calls=%async_computation.4 | async-start | bytes 131072 | tf_op jit(solution)/shard_map/all_to_all | solution.py:299
  151.9 8.9 %all-to-all-done.4 = bf16[32,4,256]{2,1,0:T(4,128)(2,1)S(1)} async-done(((bf16[32,4,256]{2,1,0:T(4,128)(2,1)}), bf16[32,4,256]{2,1,0:T(4,128)(2,1)S(1)}, u32[]{:S(2)}, u32[]{:S(2)}) %all-to-all-start.4) | async-done | bytes 65568 | tf_op jit(solution)/shard_map/all_to_all | solution.py:299
  160.7 5.3 %collective-permute-start.3 = (bf16[128,256]{1,0:T(8,128)(2,1)S(1)}, bf16[128,256]{1,0:T(8,128)(2,1)S(1)}, u32[]{:S(2)}, u32[]{:S(2)}) collective-permute-start(bf16[128,256]{1,0:T(8,128)(2,1)S(1)} %reshape.30), channel_id=1, source_target_pairs={{0,4},{4,0},{1,5},{5,1},{2,6},{6,2},{3,7},{7,3},{8,12},{12,8},{9,1... | collective-permute-start | bytes 196616 | tf_op jit(solution)/shard_map/ppermute | solution.py:285
  166.1 0.0 copy-done.7
  166.1 1.1 convolution_convert_fusion
  167.2 0.0 collective-permute-done.3
  167.2 0.7 maximum_convert_fusion
  (7 shorter events, 0.1 us)
Async XLA Ops:
  3.0 13.4 %copy-start.2 = (bf16[1024,256]{1,0:T(8,128)(2,1)S(1)}, bf16[1024,256]{1,0:T(8,128)(2,1)}, u32[]{:S(2)}) copy-start(bf16[1024,256]{1,0:T(8,128)(2,1)} %cotangent.1) | copy-start | bytes 1572868
  3.0 13.4 %copy-start.5 = (s32[8,16]{1,0:T(8,128)S(1)}, s32[8,16]{1,0:T(8,128)}, u32[]{:S(2)}) copy-start(s32[8,16]{1,0:T(8,128)} %occupied.1) | copy-start | bytes 1540
  3.0 44.2 %all-to-all-start = ((bf16[64,72,128]{2,1,0:T(8,128)(2,1)}), bf16[64,72,128]{2,1,0:T(8,128)(2,1)S(1)}, u32[]{:S(2)}, u32[]{:S(2)}) async-start(bf16[64,72,128]{2,1,0:T(8,128)(2,1)} %send_clusters.1), calls=%async_computation | async-start | bytes 2359296 | tf_op jit(solution)/shard_map/all_to_all | solution.py:281
  16.4 1.6 copy-start
  18.0 1.6 copy-start.1
  50.4 44.8 %all-to-all-start.1 = ((bf16[64,96,128]{2,1,0:T(8,128)(2,1)}), bf16[64,96,128]{2,1,0:T(8,128)(2,1)S(1)}, u32[]{:S(2)}, u32[]{:S(2)}) async-start(bf16[64,96,128]{2,1,0:T(8,128)(2,1)} %get-tuple-element.11), calls=%async_computation.1 | async-start | bytes 3145728 | tf_op jit(solution)/shard_map/all_to_all | solution.py:281
  56.7 38.5 %copy-start.4 = (bf16[256,256]{1,0:T(8,128)(2,1)S(1)}, bf16[256,256]{1,0:T(8,128)(2,1)}, u32[]{:S(2)}) copy-start(bf16[256,256]{1,0:T(8,128)(2,1)} %w.1) | copy-start | bytes 393220
  56.7 38.5 %copy-start.6 = (f32[256]{0:T(256)S(1)}, f32[256]{0:T(256)}, u32[]{:S(2)}) copy-start(f32[256]{0:T(256)} %param.19) | copy-start | bytes 3076
  99.7 24.3 %all-to-all-start.2 = ((bf16[64,32,128]{2,1,0:T(8,128)(2,1)}), bf16[64,32,128]{2,1,0:T(8,128)(2,1)S(1)}, u32[]{:S(2)}, u32[]{:S(2)}) async-start(bf16[64,32,128]{2,1,0:T(8,128)(2,1)} %get-tuple-element.16), calls=%async_computation.2 | async-start | bytes 1048576 | tf_op jit(solution)/shard_map/all_to_all | solution.py:281
  106.6 1.0 copy-start.3
  111.2 54.9 %copy-start.7 = (bf16[256,256]{1,0:T(8,128)(2,1)S(1)}, bf16[256,256]{1,0:T(8,128)(2,1)}, u32[]{:S(2)}) copy-start(bf16[256,256]{1,0:T(8,128)(2,1)} %param.20) | copy-start | bytes 393220
  125.7 1.6 collective-permute-start
  141.1 2.5 %collective-permute-start.1 = (f32[4,256]{1,0:T(4,128)S(1)}, f32[4,256]{1,0:T(4,128)S(1)}, u32[]{:S(2)}, u32[]{:S(2)}) collective-permute-start(f32[4,256]{1,0:T(4,128)S(1)} %convert_reduce_fusion), channel_id=1, source_target_pairs={{0,1},{1,0},{2,3},{3,2},{4,5},{5,4},{6,7},{7,6},{8,9},{9,8},{10,11... | collective-permute-start | bytes 12296 | tf_op jit(solution)/shard_map/ppermute | solution.py:285
  143.7 3.7 %collective-permute-start.2 = (f32[4,256]{1,0:T(4,128)S(1)}, f32[4,256]{1,0:T(4,128)S(1)}, u32[]{:S(2)}, u32[]{:S(2)}) collective-permute-start(f32[4,256]{1,0:T(4,128)S(1)} %add.28), channel_id=1, source_target_pairs={{0,3},{1,2},{2,1},{3,0},{4,7},{5,6},{6,5},{7,4},{8,11},{9,10},{10,... | collective-permute-start | bytes 12296 | tf_op jit(solution)/shard_map/ppermute | solution.py:285
  148.0 12.7 %all-to-all-start.4 = ((bf16[32,4,256]{2,1,0:T(4,128)(2,1)}), bf16[32,4,256]{2,1,0:T(4,128)(2,1)S(1)}, u32[]{:S(2)}, u32[]{:S(2)}) async-start(bf16[32,4,256]{2,1,0:T(4,128)(2,1)} %broadcast_in_dim.2), calls=%async_computation.4 | async-start | bytes 131072 | tf_op jit(solution)/shard_map/all_to_all | solution.py:299
  160.7 6.4 %collective-permute-start.3 = (bf16[128,256]{1,0:T(8,128)(2,1)S(1)}, bf16[128,256]{1,0:T(8,128)(2,1)S(1)}, u32[]{:S(2)}, u32[]{:S(2)}) collective-permute-start(bf16[128,256]{1,0:T(8,128)(2,1)S(1)} %reshape.30), channel_id=1, source_target_pairs={{0,4},{4,0},{1,5},{5,1},{2,6},{6,2},{3,7},{7,3},{8,12},{12,8},{9,1... | collective-permute-start | bytes 196616 | tf_op jit(solution)/shard_map/ppermute | solution.py:285

commit v9 on v6

--- a/solution.py
+++ b/solution.py
@@ -263,18 +263,23 @@
         partial[rows, :] = dot(local[rows, :], hidden[...]) + dot(edge[rows, :], far[...])
 
 
-def second_layer(message, partial, bank, numbers, aggregate, gradient, pushed, gather, cotangent, sem):
+def second_layer(
+    message, partial, bank, numbers, w, output_far, gradient,
+    pushed, gather, cotangent, aggregate, output, sem,
+):
     copies = Copies(sem)
     last = copies.start(kept(bank, "cotangent", slice(0, ROWS)), cotangent)
     take(message, 0, pushed)
+    out = []
     for rows, peers in steps():
         collector(numbers, gather, rows)
         total = partial[rows, :] + dot(gather[...], pushed[...])
         aggregate[rows, :] = total.astype(BF16)
+        output[rows, :] = dot(aggregate[rows, :], w[...]).astype(BF16)
+        out.append(copies.start(output.at[rows], output_far.at[rows]))
     last.wait()
-    gradient[...] = lax.dot_general(
-        aggregate[...], cotangent[...], (((0,), (0,)), ((), ())), preferred_element_type=F32
-    )
+    gradient[...] = dot_flipped(aggregate[...], cotangent[...])
+    wait(*out)
 
 
 def exchange(message):
@@ -406,17 +411,16 @@
         name="second_terms",
     )
     pushed = exchange(push)
-    aggregate, term = call(
+    output, term = call(
         second_layer,
-        "vvhvvv",
+        "vvhvvhv",
         (shaped(ROWS, F), shaped(F, F, dtype=F32)),
-        (pushed, partial_two, bank, numbers),
-        own=(nodes, half, nodes),
-        copies=1,
+        (pushed, partial_two, bank, numbers, w_second),
+        own=(nodes, half, nodes, nodes, nodes),
+        copies=1 + count,
         flops=2 * wide,
         name="second_layer",
     )
-    output = jnp.dot(aggregate, w_second, preferred_element_type=F32).astype(BF16)
     return (hidden, output, summed_everywhere(term))
 
 

time: 168 us -> 168 us (level)
  blocking collectives: 13.7 us -> 25.6 us
  waiting for transfers between devices: 83.8 us -> 75.8 us
  starting transfers between devices: 38.8 us -> 35 us
    all_to_all x0 -> x1, blocking collectives: none -> 11.8 us  [summed_everywhere(): lax.all_to_all(copies, CHIPS, split_axis=0, concat_axis=0, tiled=True)]
    all_to_all x1 -> x0, waiting for transfers between devices: 8.87 us -> none  [summed_everywhere(): lax.all_to_all(copies, CHIPS, split_axis=0, concat_axis=0, tiled=True)]
    all_to_all x1 -> x0, starting transfers between devices: 3.86 us -> none  [summed_everywhere(): lax.all_to_all(copies, CHIPS, split_axis=0, concat_axis=0, tiled=True)]
  transfers between devices with their start and end apart: 9 -> 8, of which waited for: 7 -> 7; matrix products, arithmetic and copies ran while one was open for 1% -> 0% of each run, Pallas kernels for 7% -> 7%
where the time goes in v9:
time: 168 us; the launch traced here: 167 us
  waiting for transfers between devices  75.8 us (45%)
  starting transfers between devices  35 us (21%)
  blocking collectives  25.6 us (15%)
  Pallas kernels  24.6 us (15%)
  local copies, waits for them, and re-layouts  4.33 us (3%)
    all_to_all x3, waiting for transfers between devices, exchange(): lax.all_to_all(message, ORDER, split_axis=0, concat_axis=0, tiled=True)  70.7 us
    all_to_all x3, starting transfers between devices, exchange(): lax.all_to_all(message, ORDER, split_axis=0, concat_axis=0, tiled=True)  26.6 us
    pallas_call x7, Pallas kernels, call(): pl.pallas_call(body, out_shape=outs, in_specs=specs[:len(operands)], out_...  24.6 us
    all_to_all x1, blocking collectives, summed_everywhere(): lax.all_to_all(half.reshape(32, 4, F), CHIPS, split_axis=0, concat_axis=0...  13.7 us
    all_to_all x1, blocking collectives, summed_everywhere(): lax.all_to_all(copies, CHIPS, split_axis=0, concat_axis=0, tiled=True)  11.8 us
    ppermute x5, starting transfers between devices, swapped(): lax.ppermute(array, axis, [(i, i ^ mask) for i in range(lax.axis_size(axi...  8.4 us
    ppermute x5, waiting for transfers between devices, swapped(): lax.ppermute(array, axis, [(i, i ^ mask) for i in range(lax.axis_size(axi...  5.14 us
    unnamed x16, local copies, waits for them, and re-layouts  4.24 us
  transfers between devices with their start and end apart: 8, of which 7 were waited for; matrix products, arithmetic and copies ran while one was open for 0% of the time, Pallas kernels for 7%

profile of v9, /device:TPU:1, one launch (start us, length us, event | category | flops | bytes accessed | tf_op | source)
XLA Modules:
  0.0 167.0 jit_solution(4508909184073801536)
XLA Ops:
  0.6 2.3 %send_clusters.1 = bf16[64,72,128]{2,1,0:T(8,128)(2,1)} custom-call(s32[1,64]{1,0:T(1,128)} %owner.1, bf16[1024,256]{1,0:T(8,128)(2,1)} %x.1, bf16[1024,256]{1,0:T(8,128)(2,1)} %h.1, s32[8,128]{1,0:T(8,128)} %bitcast.13), custom_call_target="tpu_custom_call" | custom-call | flops 262144 | bytes 2232576 | tf_op jit(solution)/shard_map/send_clusters/pallas_call | solution.py:38
  3.0 0.0 copy-start.2
  3.0 0.0 copy-start.6
  3.0 13.4 %all-to-all-start = ((bf16[64,72,128]{2,1,0:T(8,128)(2,1)}), bf16[64,72,128]{2,1,0:T(8,128)(2,1)S(1)}, u32[]{:S(2)}, u32[]{:S(2)}) async-start(bf16[64,72,128]{2,1,0:T(8,128)(2,1)} %send_clusters.1), calls=%async_computation | async-start | bytes 2359296 | tf_op jit(solution)/shard_map/all_to_all | solution.py:286
  16.4 0.0 copy-done.2
  16.4 0.0 copy-done.6
  16.4 0.0 copy-start
  16.4 1.6 copy-done
  18.0 0.0 copy-start.1
  18.0 1.6 copy-done.1
  19.6 4.8 %mask_tiles.1.bank = bf16[4096,1024]{1,0:T(8,128)(2,1)} custom-call(s32[8,16]{1,0:T(8,128)S(1)} %copy-done.6, bf16[1024,1024]{1,0:T(8,128)(2,1)S(1)} %copy-done, bf16[1024,1024]{1,0:T(8,128)(2,1)S(1)} %copy-done.1, bf16[1024,256]{1,0:T(8,128)(2,1)S(1)} %copy-done.2), custom_call_target="tpu_custom_call" | custom-call | flops 536870912 | bytes 13107712 | tf_op jit(solution)/shard_map/mask_tiles/pallas_call | solution.py:38
  24.4 22.8 %all-to-all-done.message = bf16[64,72,128]{2,1,0:T(8,128)(2,1)S(1)} async-done(((bf16[64,72,128]{2,1,0:T(8,128)(2,1)}), bf16[64,72,128]{2,1,0:T(8,128)(2,1)S(1)}, u32[]{:S(2)}, u32[]{:S(2)}) %all-to-all-start) | async-done | bytes 1179680 | tf_op jit(solution)/shard_map/all_to_all | solution.py:286
  47.2 3.2 %serve.1 = (bf16[1024,256]{1,0:T(8,128)(2,1)S(1)}, bf16[64,96,128]{2,1,0:T(8,128)(2,1)}) custom-call(s32[1]{0:T(128)} %bitcast.me, bf16[64,72,128]{2,1,0:T(8,128)(2,1)S(1)} %all-to-all-done.message, bf16[4096,1024]{1,0:T(8,128)(2,1)} %mask_tiles.1.bank), custom_call_target="tpu_custom_call" | custom-call | flops 1610612736 | bytes 11665412 | tf_op jit(solution)/shard_map/serve/pallas_call | solution.py:38
  50.4 6.3 %all-to-all-start.1 = ((bf16[64,96,128]{2,1,0:T(8,128)(2,1)}), bf16[64,96,128]{2,1,0:T(8,128)(2,1)S(1)}, u32[]{:S(2)}, u32[]{:S(2)}) async-start(bf16[64,96,128]{2,1,0:T(8,128)(2,1)} %get-tuple-element.11), calls=%async_computation.1 | async-start | bytes 3145728 | tf_op jit(solution)/shard_map/all_to_all | solution.py:286
  56.7 0.0 copy-start.4
  56.7 0.0 copy-start.7
  56.7 3.4 %prepare.1 = (bf16[4096,1024]{1,0:T(8,128)(2,1)}, f32[8,128]{1,0:T(8,128)S(1)}) custom-call(s32[1]{0:T(128)} %bitcast.me, bf16[64,72,128]{2,1,0:T(8,128)(2,1)S(1)} %all-to-all-done.message, bf16[1024,256]{1,0:T(8,128)(2,1)S(1)} %get-tuple-element.12.own_x, bf16[4096,1024]{1,0:T(8,128)(2,1)} %mask_tiles.1.bank), custom_call_target="tpu_custom_call", output_to_operand_aliasing={{0}: (3, {})} | custom-call | flops 536870912 | bytes 18485252 | tf_op jit(solution)/shard_map/prepare/pallas_call | solution.py:38
  60.1 35.1 %all-to-all-done.1.message = bf16[64,96,128]{2,1,0:T(8,128)(2,1)S(1)} async-done(((bf16[64,96,128]{2,1,0:T(8,128)(2,1)}), bf16[64,96,128]{2,1,0:T(8,128)(2,1)S(1)}, u32[]{:S(2)}, u32[]{:S(2)}) %all-to-all-start.1) | async-done | bytes 1572896 | tf_op jit(solution)/shard_map/all_to_all | solution.py:286
  95.2 0.0 copy-done.4
  95.2 0.0 copy-done.7
  95.2 4.5 %first_layer.1 = (bf16[1024,256]{1,0:T(8,128)(2,1)}, bf16[64,32,128]{2,1,0:T(8,128)(2,1)}) custom-call(bf16[64,96,128]{2,1,0:T(8,128)(2,1)S(1)} %all-to-all-done.1.message, bf16[4096,1024]{1,0:T(8,128)(2,1)} %get-tuple-element.13.bank, f32[8,128]{1,0:T(8,128)S(1)} %get-tuple-element.14.numbers, bf16[256,256]{1,0:T(8,128)(2,1)S(1)} %copy-done.4, ...), custom_call_target="tpu_custom_call" | custom-call | flops 1610612736 | bytes 11146240 | tf_op jit(solution)/shard_map/first_layer/pallas_call | solution.py:38
  99.7 7.0 %all-to-all-start.2 = ((bf16[64,32,128]{2,1,0:T(8,128)(2,1)}), bf16[64,32,128]{2,1,0:T(8,128)(2,1)S(1)}, u32[]{:S(2)}, u32[]{:S(2)}) async-start(bf16[64,32,128]{2,1,0:T(8,128)(2,1)} %get-tuple-element.16), calls=%async_computation.2 | async-start | bytes 1048576 | tf_op jit(solution)/shard_map/all_to_all | solution.py:286
  106.7 0.0 copy-start.3
  106.7 1.0 copy-done.3
  107.7 0.0 copy-start.5
  107.7 3.5 %second_terms.1.partial = f32[1024,256]{1,0:T(8,128)S(1)} custom-call(bf16[64,96,128]{2,1,0:T(8,128)(2,1)S(1)} %all-to-all-done.1.message, bf16[1024,256]{1,0:T(8,128)(2,1)S(1)} %copy-done.3, bf16[4096,1024]{1,0:T(8,128)(2,1)} %get-tuple-element.13.bank), custom_call_target="tpu_custom_call" | custom-call | flops 1073741824 | bytes 11534336 | tf_op jit(solution)/shard_map/second_terms/pallas_call | solution.py:38
  111.3 12.8 %all-to-all-done.2.message = bf16[64,32,128]{2,1,0:T(8,128)(2,1)S(1)} async-done(((bf16[64,32,128]{2,1,0:T(8,128)(2,1)}), bf16[64,32,128]{2,1,0:T(8,128)(2,1)S(1)}, u32[]{:S(2)}, u32[]{:S(2)}) %all-to-all-start.2) | async-done | bytes 524320 | tf_op jit(solution)/shard_map/all_to_all | solution.py:286
  124.0 0.0 copy-done.5
  124.0 2.9 %second_layer.1 = (bf16[1024,256]{1,0:T(8,128)(2,1)}, f32[256,256]{1,0:T(8,128)S(1)}) custom-call(bf16[64,32,128]{2,1,0:T(8,128)(2,1)S(1)} %all-to-all-done.2.message, f32[1024,256]{1,0:T(8,128)S(1)} %second_terms.1.partial, bf16[4096,1024]{1,0:T(8,128)(2,1)} %get-tuple-element.13.bank, f32[8,128]{1,0:T(8,128)S(1)} %get-tuple-element.14.numbers, ...), custom_call_target="tpu_custom_call" | custom-call | flops 1073741824 | bytes 10883072 | tf_op jit(solution)/shard_map/second_layer/pallas_call | solution.py:38
  127.0 0.3 collective-permute-start
  127.2 1.3 collective-permute-done
  128.6 13.7 %all_to_all.25 = bf16[32,4,256]{2,1,0:T(4,128)(2,1)S(1)} all-to-all(bf16[32,4,256]{2,1,0:T(4,128)(2,1)S(1)} %reshape.29), channel_id=1, replica_groups=mesh['dev_0'=8,'dev_1'=4,'dev_2'=2,'rep'=4] {'dev_0','dev_1'}, dimensions={0} | all-to-all | bytes 131072 | tf_op jit(solution)/shard_map/all_to_all | solution.py:299
  142.4 0.1 convert_reduce_fusion
  142.4 2.8 %collective-permute-start.2 = (f32[4,256]{1,0:T(4,128)S(1)}, f32[4,256]{1,0:T(4,128)S(1)}, u32[]{:S(2)}, u32[]{:S(2)}) collective-permute-start(f32[4,256]{1,0:T(4,128)S(1)} %convert_reduce_fusion), channel_id=1, source_target_pairs={{0,2},{1,3},{2,0},{3,1},{4,6},{5,7},{6,4},{7,5},{8,10},{9,11},{10,... | collective-permute-start | bytes 12296 | tf_op jit(solution)/shard_map/ppermute | solution.py:290
  145.2 0.9 collective-permute-start.3
  146.1 0.0 collective-permute-start.1
  146.1 0.4 collective-permute-done.2
  146.5 2.5 %collective-permute-done.3 = f32[4,256]{1,0:T(4,128)S(1)} collective-permute-done((f32[4,256]{1,0:T(4,128)S(1)}, f32[4,256]{1,0:T(4,128)S(1)}, u32[]{:S(2)}, u32[]{:S(2)}) %collective-permute-start.3) | collective-permute-done | bytes 4128 | tf_op jit(solution)/shard_map/ppermute | solution.py:290
  149.0 0.0 collective-permute-done.1
  149.0 11.8 %all_to_all.26 = bf16[32,4,256]{2,1,0:T(4,128)(2,1)S(1)} all-to-all(bf16[32,4,256]{2,1,0:T(4,128)(2,1)S(1)} %broadcast_in_dim.2), channel_id=1, replica_groups=mesh['dev_0'=8,'dev_1'=4,'dev_2'=2,'rep'=4] {'dev_0','dev_1'}, dimensions={0} | all-to-all | bytes 131072 | tf_op jit(solution)/shard_map/all_to_all | solution.py:303
  160.9 4.4 %collective-permute-start.4 = (bf16[128,256]{1,0:T(8,128)(2,1)S(1)}, bf16[128,256]{1,0:T(8,128)(2,1)S(1)}, u32[]{:S(2)}, u32[]{:S(2)}) collective-permute-start(bf16[128,256]{1,0:T(8,128)(2,1)S(1)} %reshape.30), channel_id=1, source_target_pairs={{0,4},{4,0},{1,5},{5,1},{2,6},{6,2},{3,7},{7,3},{8,12},{12,8},{9,1... | collective-permute-start | bytes 196616 | tf_op jit(solution)/shard_map/ppermute | solution.py:290
  165.4 0.9 collective-permute-done.4
  166.3 0.7 maximum_convert_fusion
  (7 shorter events, 0.1 us)
Async XLA Ops:
  3.0 13.4 %copy-start.2 = (bf16[1024,256]{1,0:T(8,128)(2,1)S(1)}, bf16[1024,256]{1,0:T(8,128)(2,1)}, u32[]{:S(2)}) copy-start(bf16[1024,256]{1,0:T(8,128)(2,1)} %cotangent.1) | copy-start | bytes 1572868
  3.0 13.4 %copy-start.6 = (s32[8,16]{1,0:T(8,128)S(1)}, s32[8,16]{1,0:T(8,128)}, u32[]{:S(2)}) copy-start(s32[8,16]{1,0:T(8,128)} %occupied.1) | copy-start | bytes 1540
  3.0 44.2 %all-to-all-start = ((bf16[64,72,128]{2,1,0:T(8,128)(2,1)}), bf16[64,72,128]{2,1,0:T(8,128)(2,1)S(1)}, u32[]{:S(2)}, u32[]{:S(2)}) async-start(bf16[64,72,128]{2,1,0:T(8,128)(2,1)} %send_clusters.1), calls=%async_computation | async-start | bytes 2359296 | tf_op jit(solution)/shard_map/all_to_all | solution.py:286
  16.4 1.6 copy-start
  18.0 1.6 copy-start.1
  50.4 44.8 %all-to-all-start.1 = ((bf16[64,96,128]{2,1,0:T(8,128)(2,1)}), bf16[64,96,128]{2,1,0:T(8,128)(2,1)S(1)}, u32[]{:S(2)}, u32[]{:S(2)}) async-start(bf16[64,96,128]{2,1,0:T(8,128)(2,1)} %get-tuple-element.11), calls=%async_computation.1 | async-start | bytes 3145728 | tf_op jit(solution)/shard_map/all_to_all | solution.py:286
  56.7 38.5 %copy-start.4 = (bf16[256,256]{1,0:T(8,128)(2,1)S(1)}, bf16[256,256]{1,0:T(8,128)(2,1)}, u32[]{:S(2)}) copy-start(bf16[256,256]{1,0:T(8,128)(2,1)} %w.2) | copy-start | bytes 393220
  56.7 38.5 %copy-start.7 = (f32[256]{0:T(256)S(1)}, f32[256]{0:T(256)}, u32[]{:S(2)}) copy-start(f32[256]{0:T(256)} %param.19) | copy-start | bytes 3076
  99.7 24.3 %all-to-all-start.2 = ((bf16[64,32,128]{2,1,0:T(8,128)(2,1)}), bf16[64,32,128]{2,1,0:T(8,128)(2,1)S(1)}, u32[]{:S(2)}, u32[]{:S(2)}) async-start(bf16[64,32,128]{2,1,0:T(8,128)(2,1)} %get-tuple-element.16), calls=%async_computation.2 | async-start | bytes 1048576 | tf_op jit(solution)/shard_map/all_to_all | solution.py:286
  106.7 1.0 copy-start.3
  107.7 16.3 %copy-start.5 = (bf16[256,256]{1,0:T(8,128)(2,1)S(1)}, bf16[256,256]{1,0:T(8,128)(2,1)}, u32[]{:S(2)}) copy-start(bf16[256,256]{1,0:T(8,128)(2,1)} %w.3) | copy-start | bytes 393220
  127.0 1.6 collective-permute-start
  142.4 4.0 %collective-permute-start.2 = (f32[4,256]{1,0:T(4,128)S(1)}, f32[4,256]{1,0:T(4,128)S(1)}, u32[]{:S(2)}, u32[]{:S(2)}) collective-permute-start(f32[4,256]{1,0:T(4,128)S(1)} %convert_reduce_fusion), channel_id=1, source_target_pairs={{0,2},{1,3},{2,0},{3,1},{4,6},{5,7},{6,4},{7,5},{8,10},{9,11},{10,... | collective-permute-start | bytes 12296 | tf_op jit(solution)/shard_map/ppermute | solution.py:290
  145.2 3.8 %collective-permute-start.3 = (f32[4,256]{1,0:T(4,128)S(1)}, f32[4,256]{1,0:T(4,128)S(1)}, u32[]{:S(2)}, u32[]{:S(2)}) collective-permute-start(f32[4,256]{1,0:T(4,128)S(1)} %convert_reduce_fusion), channel_id=1, source_target_pairs={{0,3},{1,2},{2,1},{3,0},{4,7},{5,6},{6,5},{7,4},{8,11},{9,10},{10,... | collective-permute-start | bytes 12296 | tf_op jit(solution)/shard_map/ppermute | solution.py:290
  146.1 2.9 %collective-permute-start.1 = (f32[4,256]{1,0:T(4,128)S(1)}, f32[4,256]{1,0:T(4,128)S(1)}, u32[]{:S(2)}, u32[]{:S(2)}) collective-permute-start(f32[4,256]{1,0:T(4,128)S(1)} %convert_reduce_fusion), channel_id=1, source_target_pairs={{0,1},{1,0},{2,3},{3,2},{4,5},{5,4},{6,7},{7,6},{8,9},{9,8},{10,11... | collective-permute-start | bytes 12296 | tf_op jit(solution)/shard_map/ppermute | solution.py:290
  160.9 5.3 %collective-permute-start.4 = (bf16[128,256]{1,0:T(8,128)(2,1)S(1)}, bf16[128,256]{1,0:T(8,128)(2,1)S(1)}, u32[]{:S(2)}, u32[]{:S(2)}) collective-permute-start(bf16[128,256]{1,0:T(8,128)(2,1)S(1)} %reshape.30), channel_id=1, source_target_pairs={{0,4},{4,0},{1,5},{5,1},{2,6},{6,2},{3,7},{7,3},{8,12},{12,8},{9,1... | collective-permute-start | bytes 196616 | tf_op jit(solution)/shard_map/ppermute | solution.py:290

commit v10 on v9

--- a/solution.py
+++ b/solution.py
@@ -295,7 +295,7 @@
     halves = term.reshape(2, ROWS // 8, F)
     kept_half = lax.dynamic_index_in_dim(halves, core, 0, keepdims=False)
     sent = lax.dynamic_index_in_dim(halves, 1 - core, 0, keepdims=False)
-    half = (kept_half + swapped(sent, "dev_2", 1)).astype(BF16)
+    half = (kept_half + swapped(sent.astype(BF16), "dev_2", 1)).astype(BF16)
     tiles = lax.all_to_all(half.reshape(32, 4, F), CHIPS, split_axis=0, concat_axis=0, tiled=True)
     own = jnp.sum(tiles.astype(F32), axis=0)
     own = (own + swapped(own, "rep", 1)) + (swapped(own, "rep", 2) + swapped(own, "rep", 3))

time: 168 us -> 168 us (level)
  no operation moved by 1% of the time
where the time goes in v10:
time: 168 us; the launch traced here: 167 us
  waiting for transfers between devices  75.7 us (45%)
  starting transfers between devices  35 us (21%)
  blocking collectives  25.6 us (15%)
  Pallas kernels  24.6 us (15%)
  local copies, waits for them, and re-layouts  4.33 us (3%)
    all_to_all x3, waiting for transfers between devices, exchange(): lax.all_to_all(message, ORDER, split_axis=0, concat_axis=0, tiled=True)  70.7 us
    all_to_all x3, starting transfers between devices, exchange(): lax.all_to_all(message, ORDER, split_axis=0, concat_axis=0, tiled=True)  26.6 us
    pallas_call x7, Pallas kernels, call(): pl.pallas_call(body, out_shape=outs, in_specs=specs[:len(operands)], out_...  24.6 us
    all_to_all x1, blocking collectives, summed_everywhere(): lax.all_to_all(half.reshape(32, 4, F), CHIPS, split_axis=0, concat_axis=0...  13.8 us
    all_to_all x1, blocking collectives, summed_everywhere(): lax.all_to_all(copies, CHIPS, split_axis=0, concat_axis=0, tiled=True)  11.9 us
    ppermute x5, starting transfers between devices, swapped(): lax.ppermute(array, axis, [(i, i ^ mask) for i in range(lax.axis_size(axi...  8.39 us
    ppermute x5, waiting for transfers between devices, swapped(): lax.ppermute(array, axis, [(i, i ^ mask) for i in range(lax.axis_size(axi...  5.03 us
    unnamed x16, local copies, waits for them, and re-layouts  4.24 us
  transfers between devices with their start and end apart: 8, of which 7 were waited for; matrix products, arithmetic and copies ran while one was open for 0% of the time, Pallas kernels for 7%

profile of v10, /device:TPU:1, one launch (start us, length us, event | category | flops | bytes accessed | tf_op | source)
XLA Modules:
  0.0 166.9 jit_solution(8099455304733025194)
XLA Ops:
  0.6 2.3 %send_clusters.1 = bf16[64,72,128]{2,1,0:T(8,128)(2,1)} custom-call(s32[1,64]{1,0:T(1,128)} %owner.1, bf16[1024,256]{1,0:T(8,128)(2,1)} %x.1, bf16[1024,256]{1,0:T(8,128)(2,1)} %h.1, s32[8,128]{1,0:T(8,128)} %bitcast.13), custom_call_target="tpu_custom_call" | custom-call | flops 262144 | bytes 2232576 | tf_op jit(solution)/shard_map/send_clusters/pallas_call | solution.py:38
  3.0 0.0 copy-start.2
  3.0 0.0 copy-start.6
  3.0 13.4 %all-to-all-start = ((bf16[64,72,128]{2,1,0:T(8,128)(2,1)}), bf16[64,72,128]{2,1,0:T(8,128)(2,1)S(1)}, u32[]{:S(2)}, u32[]{:S(2)}) async-start(bf16[64,72,128]{2,1,0:T(8,128)(2,1)} %send_clusters.1), calls=%async_computation | async-start | bytes 2359296 | tf_op jit(solution)/shard_map/all_to_all | solution.py:286
  16.4 0.0 copy-done.2
  16.4 0.0 copy-done.6
  16.4 0.0 copy-start
  16.4 1.6 copy-done
  18.0 0.0 copy-start.1
  18.0 1.6 copy-done.1
  19.6 4.8 %mask_tiles.1.bank = bf16[4096,1024]{1,0:T(8,128)(2,1)} custom-call(s32[8,16]{1,0:T(8,128)S(1)} %copy-done.6, bf16[1024,1024]{1,0:T(8,128)(2,1)S(1)} %copy-done, bf16[1024,1024]{1,0:T(8,128)(2,1)S(1)} %copy-done.1, bf16[1024,256]{1,0:T(8,128)(2,1)S(1)} %copy-done.2), custom_call_target="tpu_custom_call" | custom-call | flops 536870912 | bytes 13107712 | tf_op jit(solution)/shard_map/mask_tiles/pallas_call | solution.py:38
  24.4 22.8 %all-to-all-done.message = bf16[64,72,128]{2,1,0:T(8,128)(2,1)S(1)} async-done(((bf16[64,72,128]{2,1,0:T(8,128)(2,1)}), bf16[64,72,128]{2,1,0:T(8,128)(2,1)S(1)}, u32[]{:S(2)}, u32[]{:S(2)}) %all-to-all-start) | async-done | bytes 1179680 | tf_op jit(solution)/shard_map/all_to_all | solution.py:286
  47.2 3.2 %serve.1 = (bf16[1024,256]{1,0:T(8,128)(2,1)S(1)}, bf16[64,96,128]{2,1,0:T(8,128)(2,1)}) custom-call(s32[1]{0:T(128)} %bitcast.me, bf16[64,72,128]{2,1,0:T(8,128)(2,1)S(1)} %all-to-all-done.message, bf16[4096,1024]{1,0:T(8,128)(2,1)} %mask_tiles.1.bank), custom_call_target="tpu_custom_call" | custom-call | flops 1610612736 | bytes 11665412 | tf_op jit(solution)/shard_map/serve/pallas_call | solution.py:38
  50.4 6.3 %all-to-all-start.1 = ((bf16[64,96,128]{2,1,0:T(8,128)(2,1)}), bf16[64,96,128]{2,1,0:T(8,128)(2,1)S(1)}, u32[]{:S(2)}, u32[]{:S(2)}) async-start(bf16[64,96,128]{2,1,0:T(8,128)(2,1)} %get-tuple-element.11), calls=%async_computation.1 | async-start | bytes 3145728 | tf_op jit(solution)/shard_map/all_to_all | solution.py:286
  56.7 0.0 copy-start.4
  56.7 0.0 copy-start.7
  56.7 3.4 %prepare.1 = (bf16[4096,1024]{1,0:T(8,128)(2,1)}, f32[8,128]{1,0:T(8,128)S(1)}) custom-call(s32[1]{0:T(128)} %bitcast.me, bf16[64,72,128]{2,1,0:T(8,128)(2,1)S(1)} %all-to-all-done.message, bf16[1024,256]{1,0:T(8,128)(2,1)S(1)} %get-tuple-element.12.own_x, bf16[4096,1024]{1,0:T(8,128)(2,1)} %mask_tiles.1.bank), custom_call_target="tpu_custom_call", output_to_operand_aliasing={{0}: (3, {})} | custom-call | flops 536870912 | bytes 18485252 | tf_op jit(solution)/shard_map/prepare/pallas_call | solution.py:38
  60.1 35.1 %all-to-all-done.1.message = bf16[64,96,128]{2,1,0:T(8,128)(2,1)S(1)} async-done(((bf16[64,96,128]{2,1,0:T(8,128)(2,1)}), bf16[64,96,128]{2,1,0:T(8,128)(2,1)S(1)}, u32[]{:S(2)}, u32[]{:S(2)}) %all-to-all-start.1) | async-done | bytes 1572896 | tf_op jit(solution)/shard_map/all_to_all | solution.py:286
  95.2 0.0 copy-done.4
  95.2 0.0 copy-done.7
  95.2 4.5 %first_layer.1 = (bf16[1024,256]{1,0:T(8,128)(2,1)}, bf16[64,32,128]{2,1,0:T(8,128)(2,1)}) custom-call(bf16[64,96,128]{2,1,0:T(8,128)(2,1)S(1)} %all-to-all-done.1.message, bf16[4096,1024]{1,0:T(8,128)(2,1)} %get-tuple-element.13.bank, f32[8,128]{1,0:T(8,128)S(1)} %get-tuple-element.14.numbers, bf16[256,256]{1,0:T(8,128)(2,1)S(1)} %copy-done.4, ...), custom_call_target="tpu_custom_call" | custom-call | flops 1610612736 | bytes 11146240 | tf_op jit(solution)/shard_map/first_layer/pallas_call | solution.py:38
  99.7 7.0 %all-to-all-start.2 = ((bf16[64,32,128]{2,1,0:T(8,128)(2,1)}), bf16[64,32,128]{2,1,0:T(8,128)(2,1)S(1)}, u32[]{:S(2)}, u32[]{:S(2)}) async-start(bf16[64,32,128]{2,1,0:T(8,128)(2,1)} %get-tuple-element.16), calls=%async_computation.2 | async-start | bytes 1048576 | tf_op jit(solution)/shard_map/all_to_all | solution.py:286
  106.7 0.0 copy-start.3
  106.7 1.0 copy-done.3
  107.7 0.0 copy-start.5
  107.7 3.5 %second_terms.1.partial = f32[1024,256]{1,0:T(8,128)S(1)} custom-call(bf16[64,96,128]{2,1,0:T(8,128)(2,1)S(1)} %all-to-all-done.1.message, bf16[1024,256]{1,0:T(8,128)(2,1)S(1)} %copy-done.3, bf16[4096,1024]{1,0:T(8,128)(2,1)} %get-tuple-element.13.bank), custom_call_target="tpu_custom_call" | custom-call | flops 1073741824 | bytes 11534336 | tf_op jit(solution)/shard_map/second_terms/pallas_call | solution.py:38
  111.3 12.8 %all-to-all-done.2.message = bf16[64,32,128]{2,1,0:T(8,128)(2,1)S(1)} async-done(((bf16[64,32,128]{2,1,0:T(8,128)(2,1)}), bf16[64,32,128]{2,1,0:T(8,128)(2,1)S(1)}, u32[]{:S(2)}, u32[]{:S(2)}) %all-to-all-start.2) | async-done | bytes 524320 | tf_op jit(solution)/shard_map/all_to_all | solution.py:286
  124.0 0.0 copy-done.5
  124.0 2.9 %second_layer.1 = (bf16[1024,256]{1,0:T(8,128)(2,1)}, f32[256,256]{1,0:T(8,128)S(1)}) custom-call(bf16[64,32,128]{2,1,0:T(8,128)(2,1)S(1)} %all-to-all-done.2.message, f32[1024,256]{1,0:T(8,128)S(1)} %second_terms.1.partial, bf16[4096,1024]{1,0:T(8,128)(2,1)} %get-tuple-element.13.bank, f32[8,128]{1,0:T(8,128)S(1)} %get-tuple-element.14.numbers, ...), custom_call_target="tpu_custom_call" | custom-call | flops 1073741824 | bytes 10883072 | tf_op jit(solution)/shard_map/second_layer/pallas_call | solution.py:38
  127.0 0.3 collective-permute-start
  127.2 1.2 collective-permute-done
  128.5 13.8 %all_to_all.25 = bf16[32,4,256]{2,1,0:T(4,128)(2,1)S(1)} all-to-all(bf16[32,4,256]{2,1,0:T(4,128)(2,1)S(1)} %reshape.30), channel_id=1, replica_groups=mesh['dev_0'=8,'dev_1'=4,'dev_2'=2,'rep'=4] {'dev_0','dev_1'}, dimensions={0} | all-to-all | bytes 131072 | tf_op jit(solution)/shard_map/all_to_all | solution.py:299
  142.3 0.1 convert_reduce_fusion
  142.3 2.8 %collective-permute-start.2 = (f32[4,256]{1,0:T(4,128)S(1)}, f32[4,256]{1,0:T(4,128)S(1)}, u32[]{:S(2)}, u32[]{:S(2)}) collective-permute-start(f32[4,256]{1,0:T(4,128)S(1)} %convert_reduce_fusion), channel_id=1, source_target_pairs={{0,2},{1,3},{2,0},{3,1},{4,6},{5,7},{6,4},{7,5},{8,10},{9,11},{10,... | collective-permute-start | bytes 12296 | tf_op jit(solution)/shard_map/ppermute | solution.py:290
  145.2 0.9 collective-permute-start.3
  146.0 0.0 collective-permute-start.1
  146.0 0.4 collective-permute-done.2
  146.4 2.5 %collective-permute-done.3 = f32[4,256]{1,0:T(4,128)S(1)} collective-permute-done((f32[4,256]{1,0:T(4,128)S(1)}, f32[4,256]{1,0:T(4,128)S(1)}, u32[]{:S(2)}, u32[]{:S(2)}) %collective-permute-start.3) | collective-permute-done | bytes 4128 | tf_op jit(solution)/shard_map/ppermute | solution.py:290
  148.9 0.0 collective-permute-done.1
  148.9 11.9 %all_to_all.26 = bf16[32,4,256]{2,1,0:T(4,128)(2,1)S(1)} all-to-all(bf16[32,4,256]{2,1,0:T(4,128)(2,1)S(1)} %broadcast_in_dim.2), channel_id=1, replica_groups=mesh['dev_0'=8,'dev_1'=4,'dev_2'=2,'rep'=4] {'dev_0','dev_1'}, dimensions={0} | all-to-all | bytes 131072 | tf_op jit(solution)/shard_map/all_to_all | solution.py:303
  160.8 4.4 %collective-permute-start.4 = (bf16[128,256]{1,0:T(8,128)(2,1)S(1)}, bf16[128,256]{1,0:T(8,128)(2,1)S(1)}, u32[]{:S(2)}, u32[]{:S(2)}) collective-permute-start(bf16[128,256]{1,0:T(8,128)(2,1)S(1)} %reshape.31), channel_id=1, source_target_pairs={{0,4},{4,0},{1,5},{5,1},{2,6},{6,2},{3,7},{7,3},{8,12},{12,8},{9,1... | collective-permute-start | bytes 196616 | tf_op jit(solution)/shard_map/ppermute | solution.py:290
  165.3 0.9 collective-permute-done.4
  166.2 0.7 maximum_convert_fusion
  (7 shorter events, 0.1 us)
Async XLA Ops:
  3.0 13.4 %copy-start.2 = (bf16[1024,256]{1,0:T(8,128)(2,1)S(1)}, bf16[1024,256]{1,0:T(8,128)(2,1)}, u32[]{:S(2)}) copy-start(bf16[1024,256]{1,0:T(8,128)(2,1)} %cotangent.1) | copy-start | bytes 1572868
  3.0 13.4 %copy-start.6 = (s32[8,16]{1,0:T(8,128)S(1)}, s32[8,16]{1,0:T(8,128)}, u32[]{:S(2)}) copy-start(s32[8,16]{1,0:T(8,128)} %occupied.1) | copy-start | bytes 1540
  3.0 44.2 %all-to-all-start = ((bf16[64,72,128]{2,1,0:T(8,128)(2,1)}), bf16[64,72,128]{2,1,0:T(8,128)(2,1)S(1)}, u32[]{:S(2)}, u32[]{:S(2)}) async-start(bf16[64,72,128]{2,1,0:T(8,128)(2,1)} %send_clusters.1), calls=%async_computation | async-start | bytes 2359296 | tf_op jit(solution)/shard_map/all_to_all | solution.py:286
  16.4 1.6 copy-start
  18.0 1.6 copy-start.1
  50.4 44.8 %all-to-all-start.1 = ((bf16[64,96,128]{2,1,0:T(8,128)(2,1)}), bf16[64,96,128]{2,1,0:T(8,128)(2,1)S(1)}, u32[]{:S(2)}, u32[]{:S(2)}) async-start(bf16[64,96,128]{2,1,0:T(8,128)(2,1)} %get-tuple-element.11), calls=%async_computation.1 | async-start | bytes 3145728 | tf_op jit(solution)/shard_map/all_to_all | solution.py:286
  56.7 38.5 %copy-start.4 = (bf16[256,256]{1,0:T(8,128)(2,1)S(1)}, bf16[256,256]{1,0:T(8,128)(2,1)}, u32[]{:S(2)}) copy-start(bf16[256,256]{1,0:T(8,128)(2,1)} %w.2) | copy-start | bytes 393220
  56.7 38.5 %copy-start.7 = (f32[256]{0:T(256)S(1)}, f32[256]{0:T(256)}, u32[]{:S(2)}) copy-start(f32[256]{0:T(256)} %param.19) | copy-start | bytes 3076
  99.7 24.3 %all-to-all-start.2 = ((bf16[64,32,128]{2,1,0:T(8,128)(2,1)}), bf16[64,32,128]{2,1,0:T(8,128)(2,1)S(1)}, u32[]{:S(2)}, u32[]{:S(2)}) async-start(bf16[64,32,128]{2,1,0:T(8,128)(2,1)} %get-tuple-element.16), calls=%async_computation.2 | async-start | bytes 1048576 | tf_op jit(solution)/shard_map/all_to_all | solution.py:286
  106.7 1.0 copy-start.3
  107.7 16.3 %copy-start.5 = (bf16[256,256]{1,0:T(8,128)(2,1)S(1)}, bf16[256,256]{1,0:T(8,128)(2,1)}, u32[]{:S(2)}) copy-start(bf16[256,256]{1,0:T(8,128)(2,1)} %w.3) | copy-start | bytes 393220
  127.0 1.5 collective-permute-start
  142.3 4.0 %collective-permute-start.2 = (f32[4,256]{1,0:T(4,128)S(1)}, f32[4,256]{1,0:T(4,128)S(1)}, u32[]{:S(2)}, u32[]{:S(2)}) collective-permute-start(f32[4,256]{1,0:T(4,128)S(1)} %convert_reduce_fusion), channel_id=1, source_target_pairs={{0,2},{1,3},{2,0},{3,1},{4,6},{5,7},{6,4},{7,5},{8,10},{9,11},{10,... | collective-permute-start | bytes 12296 | tf_op jit(solution)/shard_map/ppermute | solution.py:290
  145.2 3.8 %collective-permute-start.3 = (f32[4,256]{1,0:T(4,128)S(1)}, f32[4,256]{1,0:T(4,128)S(1)}, u32[]{:S(2)}, u32[]{:S(2)}) collective-permute-start(f32[4,256]{1,0:T(4,128)S(1)} %convert_reduce_fusion), channel_id=1, source_target_pairs={{0,3},{1,2},{2,1},{3,0},{4,7},{5,6},{6,5},{7,4},{8,11},{9,10},{10,... | collective-permute-start | bytes 12296 | tf_op jit(solution)/shard_map/ppermute | solution.py:290
  146.0 2.9 %collective-permute-start.1 = (f32[4,256]{1,0:T(4,128)S(1)}, f32[4,256]{1,0:T(4,128)S(1)}, u32[]{:S(2)}, u32[]{:S(2)}) collective-permute-start(f32[4,256]{1,0:T(4,128)S(1)} %convert_reduce_fusion), channel_id=1, source_target_pairs={{0,1},{1,0},{2,3},{3,2},{4,5},{5,4},{6,7},{7,6},{8,9},{9,8},{10,11... | collective-permute-start | bytes 12296 | tf_op jit(solution)/shard_map/ppermute | solution.py:290
  160.8 5.3 %collective-permute-start.4 = (bf16[128,256]{1,0:T(8,128)(2,1)S(1)}, bf16[128,256]{1,0:T(8,128)(2,1)S(1)}, u32[]{:S(2)}, u32[]{:S(2)}) collective-permute-start(bf16[128,256]{1,0:T(8,128)(2,1)S(1)} %reshape.31), channel_id=1, source_target_pairs={{0,4},{4,0},{1,5},{5,1},{2,6},{6,2},{3,7},{7,3},{8,12},{12,8},{9,1... | collective-permute-start | bytes 196616 | tf_op jit(solution)/shard_map/ppermute | solution.py:290
